TPU v7x, 32 devices: a whole 2x2x4 slice. The times are simulated.
32 devices in a mesh: pair: 16 (over z, y, x), sector: 2 (over core).
Axes of the slice: x: 2, y: 2, z: 4, core: 2. Of those that a mesh axis runs over, the one named last changes fastest.
Arguments:
- wavefunction: float32 [2, 512, 512], P('sector', 'pair'), may hold values from -6 to 6
- preconditioner: float32 [2, 512, 512], P('sector', 'pair'), may hold values from 0.5 to 4
- left_ops: float32 [48, 2, 512, 512], P('pair', 'sector'), may hold values from -0.25 to 0.25
- right_ops: float32 [48, 2, 512, 512], P('pair', 'sector'), may hold values from -0.02734375 to 0.02734375
- charges: int32 [48], P('pair'), may hold values from 0 to 2
- coupling: int32 [2, 3], P('sector'), may hold values 0 or 1
Outputs:
- new_state: float32 [2, 512, 512], P('sector', 'pair')
- new_image: float32 [2, 512, 512], P('sector', 'pair')
- energies: float32 [2], replicated
All inputs are finite; a program needn't handle non-finite values. No bound on the sum of `coupling` on one device may be relied on, other than what follows from the above.
Results may differ from a plain program's by a relative error of at most 0.0003.
Values sent between devices are 32-bit elements; how exact they have to be, the bound alone decides.
No kernel may reach another device: no remote copies, remote signals or barrier semaphores. Data moves between devices by JAX's collectives and lax.ppermute only.
A program may use at most 64 MiB of HBM per device.

v0:
```python
import math

import jax
import jax.numpy as jnp
from jax import lax
from jax.sharding import PartitionSpec as P

highest = lax.Precision.HIGHEST


def shifted(block, axis, distance):
    devices = range(lax.axis_size(axis))
    route = [((i - distance) % len(devices), i) for i in devices]
    return lax.ppermute(block, axis, route)


def product(first, second):
    return jnp.dot(first, second, precision=highest, preferred_element_type=jnp.float32)


def sigma_apply(vector, left_ops, right_ops, charges, coupling):
    lower_rows = shifted(vector, "sector", 1)
    upper_rows = shifted(vector, "sector", -1)
    gathered = (
        lax.all_gather(lower_rows, "pair", axis=1, tiled=True),
        lax.all_gather(vector, "pair", axis=1, tiled=True),
        lax.all_gather(upper_rows, "pair", axis=1, tiled=True),
    )
    stacked = jnp.concatenate(gathered, axis=0)
    own_block = stacked[1]
    targets = jnp.zeros_like(stacked)
    for which_pair in range(left_ops.shape[0]):
        left_block = left_ops[which_pair, 0]
        right_block = right_ops[which_pair, 0]
        charge_slot = charges[which_pair]
        allowed = lax.dynamic_index_in_dim(coupling[0], charge_slot, 0, keepdims=False).astype(
            jnp.float32
        )
        source_block = lax.dynamic_index_in_dim(stacked, charge_slot, 0, keepdims=False)
        forward = product(product(left_block, own_block), right_block.T)
        backward = product(product(left_block.T, source_block), right_block)
        current = lax.dynamic_index_in_dim(targets, charge_slot, 0, keepdims=False)
        targets = lax.dynamic_update_index_in_dim(
            targets, current + allowed * forward, charge_slot, 0
        )
        targets = targets.at[1].add(allowed * backward)
    from_below = shifted(targets[2], "sector", 1)
    from_above = shifted(targets[0], "sector", -1)
    combined = targets[1] + from_below + from_above
    return lax.psum_scatter(combined[None], "pair", scatter_dimension=1, tiled=True)


def per_device(wavefunction, preconditioner, left_ops, right_ops, charges, coupling):
    first_image = sigma_apply(wavefunction, left_ops, right_ops, charges, coupling)
    norm_sq, correlation = lax.psum(
        (jnp.sum(wavefunction * wavefunction), jnp.sum(wavefunction * first_image)),
        ("pair", "sector"),
    )
    theta = correlation / norm_sq
    inverse = lax.rsqrt(norm_sq)
    vector = wavefunction * inverse
    image = first_image * inverse
    residual = image - theta * vector
    correction = residual / preconditioner
    along, squared = lax.psum(
        (jnp.sum(vector * correction), jnp.sum(correction * correction)), ("pair", "sector")
    )
    orthogonal = correction - along * vector
    length_sq = squared - along * along
    basis = orthogonal * lax.rsqrt(length_sq + 1e-30)
    second_image = sigma_apply(basis, left_ops, right_ops, charges, coupling)
    corner, cross = lax.psum(
        (jnp.sum(basis * second_image), jnp.sum(vector * second_image)), ("pair", "sector")
    )
    half = (theta - corner) / 2.0
    lowest = (theta + corner) / 2.0 - jnp.sqrt(half * half + cross * cross)
    first_weight = corner - lowest
    second_weight = -cross
    size_norm = jnp.sqrt(first_weight * first_weight + second_weight * second_weight + 1e-30)
    entries = (
        lax.axis_size("sector")
        * lax.axis_size("pair")
        * wavefunction.shape[1]
        * wavefunction.shape[2]
    )
    scale = jnp.float32(math.sqrt(entries))
    factor_one = scale * first_weight / size_norm
    factor_two = scale * second_weight / size_norm
    new_state = factor_one * vector + factor_two * basis
    new_image = factor_one * image + factor_two * second_image
    energies = jnp.stack([theta, lowest])
    return (new_state, new_image, energies)


def solution(mesh):
    in_specs = (
        P("sector", "pair", None),
        P("sector", "pair", None),
        P("pair", "sector", None, None),
        P("pair", "sector", None, None),
        P("pair"),
        P("sector", None),
    )
    out_specs = (P("sector", "pair", None), P("sector", "pair", None), P())
    return jax.shard_map(
        per_device, mesh=mesh, in_specs=in_specs, out_specs=out_specs, check_vma=False
    )
```

profile of v0, /device:TPU:0, one launch (start us, length us, event | category | flops | bytes accessed | tf_op | source)
XLA Modules:
  0.0 603.9 jit_solution(9496863320256029471)
XLA Ops:
  21.1 47.5 %all-gather.5.cloned.1.call-done = f32[1,512,512]{2,1,0:T(8,128)} async-done(((f32[1,32,512]{2,1,0:T(8,128)}), f32[1,512,512]{2,1,0:T(8,128)}) %all-gather.5.cloned.1.call-update) | async-done | bytes 1048592 | tf_op jit(solution)/shard_map/all_gather | solution.py:26
  68.6 3.4 fusion.82
  74.0 4.4 fusion.21
  84.1 41.8 %all-gather.7.cloned.1.call-done = f32[1,512,512]{2,1,0:T(8,128)} async-done(((f32[1,32,512]{2,1,0:T(8,128)}), f32[1,512,512]{2,1,0:T(8,128)}) %all-gather.7.cloned.1.call-update) | async-done | bytes 1048592 | tf_op jit(solution)/shard_map/all_gather | solution.py:25
  132.5 4.5 fusion.23
  141.2 4.2 fusion.25
  146.7 2.9 fusion.14
  155.5 4.3 fusion.39
  159.8 77.7 %reduce-scatter.3.cloned.1.call-done = f32[1,32,512]{2,1,0:T(8,128)} async-done(((f32[1,512,512]{2,1,0:T(8,128)}), f32[1,32,512]{2,1,0:T(8,128)}) %reduce-scatter.3.cloned.1.call-update) | async-done | bytes 65552 | tf_op jit(solution)/shard_map/reduce_scatter | solution.py:50
  239.0 37.1 %all-reduce.2 = (f32[]{:T(128)}, f32[]{:T(128)}) all-reduce(f32[]{:T(128)} %get-tuple-element.80, f32[]{:T(128)} %get-tuple-element.79), channel_id=1, replica_groups=mesh['pair'=16,'sector'=2] {'pair','sector'}, use_global_device_ids=true, to_apply=%region_4.5 | all-reduce | flops 2 | bytes 16 | tf_op jit(solution)/shard_map/psum | solution.py:55
  279.6 41.4 %all-reduce.1 = (f32[]{:T(128)}, f32[]{:T(128)}) all-reduce(f32[]{:T(128)} %get-tuple-element.78, f32[]{:T(128)} %get-tuple-element.77), channel_id=1, replica_groups=mesh['pair'=16,'sector'=2] {'pair','sector'}, use_global_device_ids=true, to_apply=%region_8.9 | all-reduce | flops 2 | bytes 16 | tf_op jit(solution)/shard_map/psum | solution.py:65
  326.7 53.3 %all-gather.9.cloned.1.call-done = f32[1,512,512]{2,1,0:T(8,128)} async-done(((f32[1,32,512]{2,1,0:T(8,128)}), f32[1,512,512]{2,1,0:T(8,128)}) %all-gather.9.cloned.1.call-update) | async-done | bytes 1048592 | tf_op jit(solution)/shard_map/all_gather | solution.py:26
  380.0 4.7 fusion.50
  386.7 5.7 fusion.10
  392.4 4.5 fusion.48
  396.9 4.7 fusion.46
  401.6 35.6 %all-gather.11.cloned.1.call-done = f32[1,512,512]{2,1,0:T(8,128)} async-done(((f32[1,32,512]{2,1,0:T(8,128)}), f32[1,512,512]{2,1,0:T(8,128)}) %all-gather.11.cloned.1.call-update) | async-done | bytes 1048592 | tf_op jit(solution)/shard_map/all_gather | solution.py:25
  443.8 4.2 fusion.29
  449.3 4.5 fusion.7
  453.7 4.4 fusion.31
  459.5 4.5 fusion.3
  469.9 4.3 fusion.36
  474.2 77.7 %reduce-scatter.5.cloned.1.call-done = f32[1,32,512]{2,1,0:T(8,128)} async-done(((f32[1,512,512]{2,1,0:T(8,128)}), f32[1,32,512]{2,1,0:T(8,128)}) %reduce-scatter.5.cloned.1.call-update) | async-done | bytes 65552 | tf_op jit(solution)/shard_map/reduce_scatter | solution.py:50
  553.4 37.1 %all-reduce = (f32[]{:T(128)}, f32[]{:T(128)}) all-reduce(f32[]{:T(128)} %get-tuple-element.76, f32[]{:T(128)} %get-tuple-element.75), channel_id=1, replica_groups=mesh['pair'=16,'sector'=2] {'pair','sector'}, use_global_device_ids=true, to_apply=%region_13.14 | all-reduce | flops 2 | bytes 16 | tf_op jit(solution)/shard_map/psum | solution.py:72
  (89 shorter events, 59.1 us)
Async XLA Ops:
  7.2 61.4 %all-gather.5.cloned.1.call-start = ((), (), s32[]{:S(2)}) async-start(), calls=%async_computation.2 | async-start | bytes 1114112 | tf_op jit(solution)/shard_map/all_gather | solution.py:26
  7.9 118.0 %all-gather.7.cloned.1.call-start = ((), (), s32[]{:S(2)}) async-start(), calls=%async_computation.3 | async-start | bytes 1114112 | tf_op jit(solution)/shard_map/all_gather | solution.py:25
  7.9 1.7 collective-permute-start
  10.3 227.2 %reduce-scatter.3.cloned.1.call-start = ((), (), s32[]{:S(2)}) async-start(), calls=%async_computation.4 | async-start | bytes 1114112 | tf_op jit(solution)/shard_map/reduce_scatter | solution.py:50
  72.0 6.5 %copy-start = (f32[3,1,512,512]{3,2,1,0:T(8,128)S(1)}, f32[3,1,512,512]{3,2,1,0:T(8,128)}, u32[]{:S(2)}) copy-start(f32[3,1,512,512]{3,2,1,0:T(8,128)} %param.20) | copy-start | bytes 9437188
  72.0 6.5 %copy-start.3 = (f32[1,512,512]{2,1,0:T(8,128)S(1)}, f32[1,512,512]{2,1,0:T(8,128)}, u32[]{:S(2)}) copy-start(f32[1,512,512]{2,1,0:T(8,128)} %all-gather.5.cloned.1.call-done) | copy-start | bytes 3145732
  128.7 3.9 copy-start.1
  132.5 5.8 copy-start.8
  141.2 5.5 copy-start.6
  151.3 2.7 collective-permute-start.1
  151.4 4.1 collective-permute-start.2
  153.8 83.7 %copy-start.11 = (f32[1,32,512]{2,1,0:T(8,128)S(1)}, f32[1,32,512]{2,1,0:T(8,128)}, u32[]{:S(2)}) copy-start(f32[1,32,512]{2,1,0:T(8,128)} %param.18) | copy-start | bytes 196612
  153.8 124.3 %copy-start.16 = (f32[1,32,512]{2,1,0:T(8,128)S(1)}, f32[1,32,512]{2,1,0:T(8,128)}, u32[]{:S(2)}) copy-start(f32[1,32,512]{2,1,0:T(8,128)} %param.19) | copy-start | bytes 196612
  159.8 220.2 %all-gather.9.cloned.1.call-start = ((), (), s32[]{:S(2)}) async-start(), calls=%async_computation.5 | async-start | bytes 1114112 | tf_op jit(solution)/shard_map/all_gather | solution.py:26
  324.3 112.9 %all-gather.11.cloned.1.call-start = ((), (), s32[]{:S(2)}) async-start(), calls=%async_computation.6 | async-start | bytes 1114112 | tf_op jit(solution)/shard_map/all_gather | solution.py:25
  324.3 1.5 collective-permute-start.3
  326.5 225.5 %reduce-scatter.5.cloned.1.call-start = ((), (), s32[]{:S(2)}) async-start(), calls=%async_computation.7 | async-start | bytes 1114112 | tf_op jit(solution)/shard_map/reduce_scatter | solution.py:50
  384.7 7.7 %copy-start.4 = (f32[1,512,512]{2,1,0:T(8,128)S(1)}, f32[1,512,512]{2,1,0:T(8,128)}, u32[]{:S(2)}) copy-start(f32[1,512,512]{2,1,0:T(8,128)} %all-gather.9.cloned.1.call-done) | copy-start | bytes 3145732
  443.8 5.5 copy-start.7
  453.7 5.7 copy-start.5
  465.7 2.7 collective-permute-start.4
  465.8 4.1 collective-permute-start.5
  468.2 83.8 %copy-start.12 = (f32[1,32,512]{2,1,0:T(8,128)S(1)}, f32[1,32,512]{2,1,0:T(8,128)}, u32[]{:S(2)}) copy-start(f32[1,32,512]{2,1,0:T(8,128)} %subtract_multiply_fusion) | copy-start | bytes 196612
  468.2 126.9 %copy-start.13 = (f32[1,32,512]{2,1,0:T(8,128)S(1)}, f32[1,32,512]{2,1,0:T(8,128)}, u32[]{:S(2)}) copy-start(f32[1,32,512]{2,1,0:T(8,128)} %reduce-scatter.3.cloned.1.call-done) | copy-start | bytes 196612
  (5 other events, 10.5 us)
Sparse Core Ops, SparseCore 0:
  10.7 57.8 all-gather.4
  71.9 53.9 all-gather.6
  159.9 77.5 reduce-scatter.2
  324.4 55.5 all-gather.8
  383.2 53.9 all-gather.10
  474.3 77.5 reduce-scatter.4
where the time goes:
time: 615 us; the launch traced here: 604 us
  waiting for transfers between devices  340 us (55%)
  blocking collectives  116 us (19%)
  matrix products  85 us (14%)
  between operations  30.9 us (5%)
  local copies, waits for them, and re-layouts  22.4 us (4%)
  other arithmetic  7.79 us (1%)
    reduce_scatter x2, waiting for transfers between devices, sigma_apply(): lax.psum_scatter(combined[None], 'pair', scatter_dimension=1, tiled=True)  155 us
    all_gather x2, waiting for transfers between devices, sigma_apply(): lax.all_gather(vector, 'pair', axis=1, tiled=True)  101 us
    dot_general x24, matrix products, product(): jnp.dot(first, second, precision=highest, preferred_element_type=jnp.floa...  85 us
    all_gather x2, waiting for transfers between devices, sigma_apply(): lax.all_gather(lower_rows, 'pair', axis=1, tiled=True)  77.3 us
    psum x1, blocking collectives, per_device(): lax.psum((jnp.sum(vector * correction), jnp.sum(correction * correction))...  41.4 us
    psum x1, blocking collectives, per_device(): lax.psum((jnp.sum(wavefunction * wavefunction), jnp.sum(wavefunction * fi...  37.1 us
    psum x1, blocking collectives, per_device(): lax.psum((jnp.sum(basis * second_image), jnp.sum(vector * second_image)),...  37.1 us
  transfers between devices with their start and end apart: 12, of which 12 were waited for; matrix products, arithmetic and copies ran while one was open for 7% of the time, Pallas kernels for 0%

commit v1 on v0

v1 whole, which is shorter than its diff:
```python
import functools
import math

import jax
import jax.numpy as jnp
from jax import lax
from jax.experimental import pallas as pl
from jax.experimental.pallas import tpu as pltpu
from jax.sharding import PartitionSpec as P

F32, BF16 = jnp.float32, jnp.bfloat16
PLANE = 4
LIMIT = 40 * 1024 * 1024


def swap(block, mask):
    return lax.ppermute(block, "pair", [(i, i ^ mask) for i in range(lax.axis_size("pair"))])


def shifted(block, distance):
    size = lax.axis_size("sector")
    return lax.ppermute(block, "sector", [((i - distance) % size, i) for i in range(size)])


def neighbours(block):
    if lax.axis_size("sector") == 2:
        return [shifted(block, 1)]
    return [shifted(block, 1), shifted(block, -1)]


def to_neighbours(blocks):
    if lax.axis_size("sector") == 2:
        return [shifted(blocks[0], 1)]
    return [shifted(blocks[0], -1), shifted(blocks[1], 1)]


def gather_rows(block):
    count, half = lax.axis_size("pair"), block.shape[1] // 2
    column = jnp.concatenate([block] + [swap(block, k) for k in range(PLANE, count, PLANE)], axis=0)
    a, b = column[:, :half], column[:, half:]
    a = jnp.concatenate([a, swap(a, 1)], axis=0)
    b = jnp.concatenate([b, swap(b, 2)], axis=0)
    return [a, b, swap(a, 2), swap(b, 1)]


def piece_slots(count):
    deep = range(0, count, PLANE)
    a = [k + x for x in (0, 1) for k in deep]
    b = [k + y for y in (0, 2) for k in deep]
    return [a, b, [k + 2 for k in a], [k + 1 for k in b]]


def term_slots(count):
    deep = range(0, count, PLANE)
    a = [k + y for y in (0, 2) for k in deep]
    b = [k + x for x in (0, 1) for k in deep]
    return [a, b, [k + 1 for k in a], [k + 2 for k in b]]


def scatter_rows(terms, scalars):
    count = lax.axis_size("pair")
    keep_a, keep_b, send_a, send_b = terms
    a = keep_a + swap(send_a, 1)
    b = keep_b + swap(send_b, 2)
    scalars = scalars + swap(scalars, 1)
    split = a.shape[0] // 2
    a = a[:split] + swap(a[split:], 2)
    b = b[:split] + swap(b[split:], 1)
    scalars = scalars + swap(scalars, 2)
    rows = split // (count // PLANE)
    both = jnp.concatenate([a, b], axis=1)
    total, sums = both[:rows], scalars
    for step in range(1, count // PLANE):
        total = total + swap(both[step * rows : (step + 1) * rows], step * PLANE)
        sums = sums + swap(scalars, step * PLANE)
    return total, sums


def split(value):
    high = value.astype(BF16)
    return high, (value - high.astype(F32)).astype(BF16)


def dot(first, second):
    return jnp.dot(first, second, preferred_element_type=F32)


def dot3(first, second):
    return dot(first[0], second[0]) + dot(first[0], second[1]) + dot(first[1], second[0])


def prepare_kernel(left_ref, right_ref, left_out, left_t_out, right_out, right_t_out):
    for source, plain, turned in ((left_ref, left_out, left_t_out), (right_ref, right_out, right_t_out)):
        value = source[...]
        plain[0], plain[1] = split(value)
        turned[0], turned[1] = split(value.T)


def prepare(left_ops, right_ops):
    pairs, _, m, _ = left_ops.shape
    source = pl.BlockSpec((None, None, m, m), lambda p: (p, 0, 0, 0))
    target = pl.BlockSpec((None, 2, m, m), lambda p: (p, 0, 0, 0))
    return pl.pallas_call(
        prepare_kernel,
        grid=(pairs,),
        in_specs=[source, source],
        out_specs=[target] * 4,
        out_shape=[jax.ShapeDtypeStruct((pairs, 2, m, m), BF16)] * 4,
        compiler_params=pltpu.CompilerParams(vmem_limit_bytes=LIMIT),
        cost_estimate=pl.CostEstimate(flops=pairs * m * m * 1000, bytes_accessed=24 * pairs * m * m, transcendentals=0),
    )(left_ops, right_ops)


def unpack(me, pieces, count, high, low):
    half = pieces[0].shape[1]
    for which, (piece, slots) in enumerate(zip(pieces, piece_slots(count))):
        rows = piece.shape[0] // len(slots)
        columns = pl.ds((which % 2) * half, half)
        for at, slot in enumerate(slots):
            where = pl.multiple_of((me ^ slot) * rows, rows)
            high[pl.ds(where, rows), columns], low[pl.ds(where, rows), columns] = split(
                piece[at * rows : (at + 1) * rows, :]
            )


def pack(me, total, count, pieces, extra=None):
    half = pieces[0].shape[1]
    for which, (piece, slots) in enumerate(zip(pieces, term_slots(count))):
        rows = piece.shape[0] // len(slots)
        columns = pl.ds((which % 2) * half, half)
        for at, slot in enumerate(slots):
            where = pl.multiple_of((me ^ slot) * rows, rows)
            span = slice(at * rows, (at + 1) * rows)
            value = total[pl.ds(where, rows), columns]
            piece[span, :] = value if extra is None else value + extra[which][span, :]


def block_of(charge, sectors):
    return jnp.where(charge == 1, 0, 1 if sectors == 2 else jnp.where(charge == 0, 1, 2))


def forward_kernel(count, sectors, me_ref, charges_ref, coupling_ref, *refs):
    pieces, (left, right_t), refs = refs[:4], refs[4:6], refs[6:]
    blocks = min(sectors, 3)
    outs, (high, low, total) = refs[: 4 * blocks], refs[4 * blocks :]
    pair, me = pl.program_id(0), me_ref[0]

    @pl.when(pair == 0)
    def _():
        unpack(me, pieces, count, high, low)
        total[...] = jnp.zeros_like(total)

    charge = charges_ref[pair]
    allowed = coupling_ref[0, charge].astype(F32)
    inner = dot3((left[0], left[1]), (high[...], low[...])) * allowed
    term = dot3(split(inner), (right_t[0], right_t[1]))
    block = block_of(charge, sectors)
    total[block] = total[block] + term

    @pl.when(pair == pl.num_programs(0) - 1)
    def _():
        for block in range(blocks):
            pack(me, total.at[block], count, outs[4 * block : 4 * block + 4])


def backward_kernel(count, sectors, me_ref, charges_ref, coupling_ref, *refs):
    blocks = min(sectors, 3)
    pieces, refs = refs[: 4 * blocks], refs[4 * blocks :]
    right, left_t, first, refs = refs[0], refs[1], refs[2:6], refs[6:]
    outs, sums, (high, low, total) = refs[:4], refs[4], refs[5:]
    pair, me = pl.program_id(0), me_ref[0]

    @pl.when(pair == 0)
    def _():
        for block in range(blocks):
            unpack(me, pieces[4 * block : 4 * block + 4], count, high.at[block], low.at[block])
        total[...] = jnp.zeros_like(total)

    charge = charges_ref[pair]
    allowed = coupling_ref[0, charge].astype(F32)
    block = block_of(charge, sectors)
    inner = dot3((high[block], low[block]), (right[0], right[1])) * allowed
    total[...] = total[...] + dot3((left_t[0], left_t[1]), split(inner))

    @pl.when(pair == pl.num_programs(0) - 1)
    def _():
        own = high[0].astype(F32) + low[0].astype(F32)
        sums[...] = jnp.full(sums.shape, 2.0 * jnp.sum(own * total[...]), F32)
        pack(me, total, count, outs, first)


def call(kernel, pairs, m, scalars, pieces, ops, extra, outs, scratch):
    whole = pl.BlockSpec(memory_space=pltpu.VMEM)
    op = pl.BlockSpec((None, 2, m, m), lambda p, *_: (p, 0, 0, 0))
    return pl.pallas_call(
        kernel,
        grid_spec=pltpu.PrefetchScalarGridSpec(
            num_scalar_prefetch=3,
            grid=(pairs,),
            in_specs=[whole] * len(pieces) + [op] * len(ops) + [whole] * len(extra),
            out_specs=[whole] * len(outs),
            scratch_shapes=scratch,
        ),
        out_shape=outs,
        compiler_params=pltpu.CompilerParams(vmem_limit_bytes=LIMIT),
        cost_estimate=pl.CostEstimate(flops=12 * pairs * m**3, bytes_accessed=8 * pairs * m * m, transcendentals=0),
    )(*scalars, *pieces, *ops, *extra)


def sigma_apply(block, ops, scalars, extra_sums):
    left, left_t, right, right_t = ops
    pairs, m = left.shape[0], left.shape[2]
    count, sectors = lax.axis_size("pair"), lax.axis_size("sector")
    blocks = min(sectors, 3)
    own = gather_rows(block)
    others = [neighbours(piece) for piece in own]
    others = [[others[q][b] for q in range(4)] for b in range(blocks - 1)]
    shape = jax.ShapeDtypeStruct((m // 2, m // 2), F32)
    tile = jax.ShapeDtypeStruct((8, 128), F32)
    made = call(
        functools.partial(forward_kernel, count, sectors), pairs, m, scalars, own, [left, right_t], [],
        [shape] * (4 * blocks),
        [pltpu.VMEM((m, m), BF16), pltpu.VMEM((m, m), BF16), pltpu.VMEM((blocks, m, m), F32)],
    )
    aimed = [made[4 * b : 4 * b + 4] for b in range(blocks)]
    arrived = [to_neighbours([aimed[b][q] for b in range(1, blocks)]) for q in range(4)]
    *mine, product = call(
        functools.partial(backward_kernel, count, sectors), pairs, m, scalars, own + sum(others, []), [right, left_t],
        aimed[0], [shape] * 4 + [tile],
        [pltpu.VMEM((blocks, m, m), BF16), pltpu.VMEM((blocks, m, m), BF16), pltpu.VMEM((m, m), F32)],
    )
    terms = [sum(arrived[q], mine[q]) for q in range(4)]
    row = lax.broadcasted_iota(jnp.int32, tile.shape, 0)
    sums = jnp.where(row == 0, product, extra_sums)
    if sectors == 2:
        sums = sums + shifted(sums, 1)
    else:
        sums = lax.psum(sums, "sector")
    rows, sums = scatter_rows(terms, sums)
    return rows, sums[:, 0]


def tile_of(values):
    row = lax.broadcasted_iota(jnp.int32, (8, 128), 0)
    tile = jnp.zeros((8, 128), F32)
    for at, value in enumerate(values):
        tile = jnp.where(row == at + 1, value, tile)
    return tile


def per_device(wavefunction, preconditioner, left_ops, right_ops, charges, coupling):
    vector, divisor = wavefunction[0], preconditioner[0]
    ops = prepare(left_ops, right_ops)
    scalars = (lax.axis_index("pair").astype(jnp.int32)[None], charges, coupling)
    image, sums = sigma_apply(vector, ops, scalars, tile_of([jnp.sum(vector * vector)]))
    correlation, norm_sq = sums[0], sums[1]
    theta = correlation / norm_sq
    inverse = lax.rsqrt(norm_sq)
    correction = (image - theta * vector) / divisor
    second, sums = sigma_apply(
        correction, ops, scalars,
        tile_of([jnp.sum(vector * correction), jnp.sum(correction * correction), jnp.sum(image * correction)]),
    )
    along = sums[1] / norm_sq
    length_sq = (sums[2] - along * sums[1]) / norm_sq
    factor = inverse * lax.rsqrt(length_sq + 1e-30)
    corner = factor * factor * (sums[0] - 2.0 * along * sums[3] + along * along * correlation)
    cross = inverse * factor * (sums[3] - along * correlation)
    half = (theta - corner) / 2.0
    lowest = (theta + corner) / 2.0 - jnp.sqrt(half * half + cross * cross)
    first_weight = corner - lowest
    second_weight = -cross
    size_norm = jnp.sqrt(first_weight * first_weight + second_weight * second_weight + 1e-30)
    entries = lax.axis_size("sector") * lax.axis_size("pair") * vector.shape[0] * vector.shape[1]
    scale = jnp.float32(math.sqrt(entries))
    factor_two = scale * second_weight / size_norm * factor
    factor_one = scale * first_weight / size_norm * inverse - factor_two * along
    new_state = factor_one * vector + factor_two * correction
    new_image = factor_one * image + factor_two * second
    return (new_state[None], new_image[None], jnp.stack([theta, lowest]))


def solution(mesh):
    in_specs = (
        P("sector", "pair", None),
        P("sector", "pair", None),
        P("pair", "sector", None, None),
        P("pair", "sector", None, None),
        P("pair"),
        P("sector", None),
    )
    out_specs = (P("sector", "pair", None), P("sector", "pair", None), P())
    return jax.shard_map(
        per_device, mesh=mesh, in_specs=in_specs, out_specs=out_specs, check_vma=False
    )
```

time: 615 us -> 177 us (0.29); the launches traced: 604 us -> 176 us
  waiting for transfers between devices: 340 us -> 52.4 us
  blocking collectives: 116 us -> 0 us
  matrix products: 85 us -> 0 us
  starting transfers between devices: 2.17 us -> 56.5 us
  Pallas kernels: 0 us -> 32 us
  between operations: 30.9 us -> 9.75 us
  local copies, waits for them, and re-layouts: 22.4 us -> 14.5 us
    all_gather x4 -> x0, waiting for transfers between devices: 178 us -> none  [the longest x2 101 us: sigma_apply(): lax.all_gather(vector, 'pair', axis=1, tiled=True)]
    reduce_scatter x2 -> x0, waiting for transfers between devices: 155 us -> none  [sigma_apply(): lax.psum_scatter(combined[None], 'pair', scatter_dimension=1, tiled=True)]
    psum x3 -> x0, blocking collectives: 116 us -> none  [the longest x1 41.4 us: per_device(): lax.psum((jnp.sum(vector * correction), jnp.sum(correction * correction))...]
    dot_general x24 -> x0, matrix products: 85 us -> none  [product(): jnp.dot(first, second, precision=highest, preferred_element_type=jnp.floa...]
    ppermute x6 -> x56, starting transfers between devices: 1.76 us -> 56.5 us  [the longest x38 52.1 us: swap(): lax.ppermute(block, 'pair', [(i, i ^ mask) for i in range(lax.axis_size('...]
    ppermute x6 -> x56, waiting for transfers between devices: 5.96 us -> 52.4 us  [the longest x38 51.5 us: swap(): lax.ppermute(block, 'pair', [(i, i ^ mask) for i in range(lax.axis_size('...]
    pallas_call x0 -> x5, Pallas kernels: none -> 32 us  [the longest x4 27.6 us: call(): pl.pallas_call(kernel, grid_spec=pltpu.PrefetchScalarGridSpec(num_scalar_...]
    dynamic_slice x5 -> x0, local copies, waits for them, and re-layouts: 6.61 us -> none  [the longest x4 5.17 us: sigma_apply(): current = lax.dynamic_index_in_dim(targets, charge_slot, 0, keepdims=False)]
  transfers between devices with their start and end apart: 12 -> 56, of which waited for: 12 -> 23; matrix products, arithmetic and copies ran while one was open for 7% -> 4% of each run, Pallas kernels for 0% -> 18%
where the time goes in v1:
time: 177 us; the launch traced here: 176 us
  starting transfers between devices  56.5 us (32%)
  waiting for transfers between devices  52.4 us (30%)
  Pallas kernels  32 us (18%)
  local copies, waits for them, and re-layouts  14.5 us (8%)
  other arithmetic  11 us (6%)
  between operations  9.75 us (6%)
    ppermute x38, starting transfers between devices, swap(): lax.ppermute(block, 'pair', [(i, i ^ mask) for i in range(lax.axis_size('...  52.1 us
    ppermute x38, waiting for transfers between devices, swap(): lax.ppermute(block, 'pair', [(i, i ^ mask) for i in range(lax.axis_size('...  51.5 us
    pallas_call x4, Pallas kernels, call(): pl.pallas_call(kernel, grid_spec=pltpu.PrefetchScalarGridSpec(num_scalar_...  27.6 us
    unnamed x36, local copies, waits for them, and re-layouts  13.2 us
    ppermute x18, starting transfers between devices, shifted(): lax.ppermute(block, 'sector', [((i - distance) % size, i) for i in range(...  4.46 us
    pallas_call x1, Pallas kernels, prepare(): pl.pallas_call(prepare_kernel, grid=(pairs,), in_specs=[source, source],...  4.37 us
  transfers between devices with their start and end apart: 56, of which 23 were waited for; matrix products, arithmetic and copies ran while one was open for 4% of the time, Pallas kernels for 18%

profile of v1, /device:TPU:0, one launch (start us, length us, event | category | flops | bytes accessed | tf_op | source)
XLA Modules:
  0.0 176.0 jit_solution(8083843048563323130)
XLA Ops:
  0.6 3.1 %collective-permute-start = (f32[32,512]{1,0:T(8,128)}, f32[32,512]{1,0:T(8,128)S(1)}, u32[]{:S(2)}, u32[]{:S(2)}) collective-permute-start(f32[32,512]{1,0:T(8,128)} %bitcast.22), channel_id=1, source_target_pairs={{0,8},{2,10},{4,12},{6,14},{8,0},{10,2},{12,4},{14,6},{16,24},{18,... | collective-permute-start | bytes 196616 | tf_op jit(solution)/shard_map/ppermute | solution.py:17
  3.7 2.6 %collective-permute-start.1 = (f32[32,512]{1,0:T(8,128)}, f32[32,512]{1,0:T(8,128)S(1)}, u32[]{:S(2)}, u32[]{:S(2)}) collective-permute-start(f32[32,512]{1,0:T(8,128)} %bitcast.23), channel_id=1, source_target_pairs={{0,16},{2,18},{4,20},{6,22},{8,24},{10,26},{12,28},{14,30},{16,0},... | collective-permute-start | bytes 196616 | tf_op jit(solution)/shard_map/ppermute | solution.py:17
  6.3 4.9 %collective-permute-done.1 = f32[32,512]{1,0:T(8,128)S(1)} collective-permute-done((f32[32,512]{1,0:T(8,128)}, f32[32,512]{1,0:T(8,128)S(1)}, u32[]{:S(2)}, u32[]{:S(2)}) %collective-permute-start.1) | collective-permute-done | bytes 65568 | tf_op jit(solution)/shard_map/ppermute | solution.py:17
  21.8 4.4 %shard_map.85 = (bf16[3,2,512,512]{3,2,1,0:T(8,128)(2,1)S(1)}, bf16[3,2,512,512]{3,2,1,0:T(8,128)(2,1)S(1)}, bf16[3,2,512,512]{3,2,1,0:T(8,128)(2,1)S(1)}, bf16[3,2,512,512]{3,2,1,0:T(8,128)(2,1)S(1)}) custom-call(f32[3,1,512,512]{3,2,1,0:T(8,128)} %left_ref.1, f32[3,1,512,512]{3,2,1,0:T(8,128)} %right_ref.1), custom_call_target="tpu_custom_call" | custom-call | flops 786432000 | bytes 18874368 | tf_op jit(solution)/shard_map/pallas_call | solution.py:103
  39.1 6.4 %shard_map.86 = (f32[256,256]{1,0:T(8,128)S(1)}, f32[256,256]{1,0:T(8,128)S(1)}, f32[256,256]{1,0:T(8,128)S(1)}, f32[256,256]{1,0:T(8,128)S(1)}, f32[256,256]{1,...) custom-call(s32[1]{0:T(128)} %bitcast.me_ref, s32[3]{0:T(128)S(1)} %copy-done.14, ...), custom_call_target="tpu_custom_call" | custom-call | flops 4831838208 | bytes 6291456 | tf_op jit(solution)/shard_map/pallas_call | solution.py:195
  46.1 7.0 %shard_map.87 = (f32[256,256]{1,0:T(8,128)S(1)}, f32[256,256]{1,0:T(8,128)S(1)}, f32[256,256]{1,0:T(8,128)S(1)}, f32[256,256]{1,0:T(8,128)S(1)}, f32[8,128]{1,0:T(8,128)S(1)}) custom-call(s32[1]{0:T(128)} %bitcast.me_ref, s32[3]{0:T(128)S(1)} %copy-done.14, s32[1,3]{1,0:T(1,128)S(1)} %copy-done.15, f32[256,256]{1,0:T(8,128)S(1)} %pad_maximum_fusion.1.refs_0_, ...), custom_call_target="tpu_custom_call" | custom-call | flops 4831838208 | bytes 6291456 | tf_op jit(solution)/shard_map/pallas_call | solution.py:195
  59.9 3.1 %collective-permute-done.13 = f32[8,128]{1,0:T(8,128)S(1)} collective-permute-done((f32[8,128]{1,0:T(8,128)S(1)}, f32[8,128]{1,0:T(8,128)S(1)}, u32[]{:S(2)}, u32[]{:S(2)}) %collective-permute-start.13) | collective-permute-done | bytes 4128 | tf_op jit(solution)/shard_map/ppermute | solution.py:17
  63.0 2.3 %collective-permute-start.15 = (f32[8,128]{1,0:T(8,128)S(1)}, f32[8,128]{1,0:T(8,128)S(1)}, u32[]{:S(2)}, u32[]{:S(2)}) collective-permute-start(f32[8,128]{1,0:T(8,128)S(1)} %add.128), channel_id=1, source_target_pairs={{0,16},{2,18},{4,20},{6,22},{8,24},{10,26},{12,28},{14,30},{16,0},... | collective-permute-start | bytes 12296 | tf_op jit(solution)/shard_map/ppermute | solution.py:17
  72.4 4.4 %collective-permute-done.19 = f32[256,256]{1,0:T(8,128)S(1)} collective-permute-done((f32[256,256]{1,0:T(8,128)S(1)}, f32[256,256]{1,0:T(8,128)S(1)}, u32[]{:S(2)}, u32[]{:S(2)}) %collective-permute-start.19) | collective-permute-done | bytes 262176 | tf_op jit(solution)/shard_map/ppermute | solution.py:17
  79.1 2.8 %collective-permute-done.20 = f32[128,256]{1,0:T(8,128)S(1)} collective-permute-done((f32[128,256]{1,0:T(8,128)S(1)}, f32[128,256]{1,0:T(8,128)S(1)}, u32[]{:S(2)}, u32[]{:S(2)}) %collective-permute-start.20) | collective-permute-done | bytes 131104 | tf_op jit(solution)/shard_map/ppermute | solution.py:17
  82.6 3.2 %collective-permute-start.26 = (f32[32,512]{1,0:T(8,128)}, f32[32,512]{1,0:T(8,128)}, u32[]{:S(2)}, u32[]{:S(2)}) collective-permute-start(f32[32,512]{1,0:T(8,128)} %get-tuple-element.75), channel_id=1, source_target_pairs={{0,16},{2,18},{4,20},{6,22},{8,24},{10,26},{12,28},{14,30},{16,0},... | collective-permute-start | bytes 196616 | tf_op jit(solution)/shard_map/ppermute | solution.py:17
  88.9 3.0 %collective-permute-done.27 = f32[32,512]{1,0:T(8,128)} collective-permute-done((f32[32,512]{1,0:T(8,128)S(1)}, f32[32,512]{1,0:T(8,128)}, u32[]{:S(2)}, u32[]{:S(2)}) %collective-permute-start.27) | collective-permute-done | bytes 65568 | tf_op jit(solution)/shard_map/ppermute | solution.py:17
  91.9 2.3 %multiply_reduce_fusion.2 = (f32[]{:T(128)}, f32[]{:T(128)}, f32[]{:T(128)}, f32[32,512]{1,0:T(8,128)S(1)}, f32[32,512]{1,0:T(8,128)}) fusion(f32[1,32,512]{2,1,0:T(8,128)S(1)} %copy-done.16, f32[1,32,512]{2,1,0:T(8,128)} %param.7, f32[]{:T(128)} %div.22, f32[32,512]{1,0:T(8,128)} %collective-permute-done.27, f32[32,512]{1,0:T(8,128)} %collective-permute-done.26, ...), kind=kLoop, calls=%fused_computation.47 | loop fusion | flops 212989 | bytes 720912 | tf_op jit(solution)/shard_map/reduce_sum | solution.py:262
  95.9 2.6 %collective-permute-start.30 = (f32[32,512]{1,0:T(8,128)S(1)}, f32[32,512]{1,0:T(8,128)S(1)}, u32[]{:S(2)}, u32[]{:S(2)}) collective-permute-start(f32[32,512]{1,0:T(8,128)S(1)} %get-tuple-element.66), channel_id=1, source_target_pairs={{0,24},{2,26},{4,28},{6,30},{8,16},{10,18},{12,20},{14,22},{16,8},... | collective-permute-start | bytes 196616 | tf_op jit(solution)/shard_map/ppermute | solution.py:17
  99.3 2.7 %collective-permute-done.30 = f32[32,512]{1,0:T(8,128)S(1)} collective-permute-done((f32[32,512]{1,0:T(8,128)S(1)}, f32[32,512]{1,0:T(8,128)S(1)}, u32[]{:S(2)}, u32[]{:S(2)}) %collective-permute-start.30) | collective-permute-done | bytes 65568 | tf_op jit(solution)/shard_map/ppermute | solution.py:17
  104.7 3.8 %collective-permute-done.32 = f32[128,256]{1,0:T(8,128)S(1)} collective-permute-done((f32[128,256]{1,0:T(8,128)S(1)}, f32[128,256]{1,0:T(8,128)S(1)}, u32[]{:S(2)}, u32[]{:S(2)}) %collective-permute-start.32) | collective-permute-done | bytes 131104 | tf_op jit(solution)/shard_map/ppermute | solution.py:17
  112.5 2.5 %collective-permute-done.34.refs_3_ = f32[256,256]{1,0:T(8,128)S(1)} collective-permute-done((f32[256,256]{1,0:T(8,128)S(1)}, f32[256,256]{1,0:T(8,128)S(1)}, u32[]{:S(2)}, u32[]{:S(2)}) %collective-permute-start.34) | collective-permute-done | bytes 262176 | tf_op jit(solution)/shard_map/ppermute | solution.py:17
  118.4 7.2 %shard_map.88 = (f32[256,256]{1,0:T(8,128)S(1)}, f32[256,256]{1,0:T(8,128)S(1)}, f32[256,256]{1,0:T(8,128)S(1)}, f32[256,256]{1,0:T(8,128)S(1)}, f32[256,256]{1,...) custom-call(s32[1]{0:T(128)} %bitcast.me_ref, s32[3]{0:T(128)S(1)} %copy-done.14, ...), custom_call_target="tpu_custom_call" | custom-call | flops 4831838208 | bytes 6291456 | tf_op jit(solution)/shard_map/pallas_call | solution.py:195
  126.9 7.0 %shard_map.89 = (f32[256,256]{1,0:T(8,128)S(1)}, f32[256,256]{1,0:T(8,128)S(1)}, f32[256,256]{1,0:T(8,128)S(1)}, f32[256,256]{1,0:T(8,128)S(1)}, f32[8,128]{1,0:T(8,128)S(1)}) custom-call(s32[1]{0:T(128)} %bitcast.me_ref, s32[3]{0:T(128)S(1)} %copy-done.14, s32[1,3]{1,0:T(1,128)S(1)} %copy-done.15, f32[256,256]{1,0:T(8,128)S(1)} %pad_maximum_fusion.4.refs_0_, ...), custom_call_target="tpu_custom_call" | custom-call | flops 4831838208 | bytes 6291456 | tf_op jit(solution)/shard_map/pallas_call | solution.py:195
  138.5 3.1 %collective-permute-done.40 = f32[8,128]{1,0:T(8,128)S(1)} collective-permute-done((f32[8,128]{1,0:T(8,128)S(1)}, f32[8,128]{1,0:T(8,128)S(1)}, u32[]{:S(2)}, u32[]{:S(2)}) %collective-permute-start.40) | collective-permute-done | bytes 4128 | tf_op jit(solution)/shard_map/ppermute | solution.py:17
  142.7 2.5 %collective-permute-done.41 = f32[8,128]{1,0:T(8,128)S(1)} collective-permute-done((f32[8,128]{1,0:T(8,128)S(1)}, f32[8,128]{1,0:T(8,128)S(1)}, u32[]{:S(2)}, u32[]{:S(2)}) %collective-permute-start.41) | collective-permute-done | bytes 4128 | tf_op jit(solution)/shard_map/ppermute | solution.py:17
  147.0 2.6 %collective-permute-start.44 = (f32[8,128]{1,0:T(8,128)S(1)}, f32[8,128]{1,0:T(8,128)S(1)}, u32[]{:S(2)}, u32[]{:S(2)}) collective-permute-start(f32[8,128]{1,0:T(8,128)S(1)} %add.145), channel_id=1, source_target_pairs={{0,24},{2,26},{4,28},{6,30},{8,16},{10,18},{12,20},{14,22},{16,8},... | collective-permute-start | bytes 12296 | tf_op jit(solution)/shard_map/ppermute | solution.py:17
  163.3 2.4 %collective-permute-done.52 = f32[128,256]{1,0:T(8,128)S(1)} collective-permute-done((f32[128,256]{1,0:T(8,128)S(1)}, f32[128,256]{1,0:T(8,128)S(1)}, u32[]{:S(2)}, u32[]{:S(2)}) %collective-permute-start.52) | collective-permute-done | bytes 131104 | tf_op jit(solution)/shard_map/ppermute | solution.py:17
  169.3 2.6 %collective-permute-start.55 = (f32[32,512]{1,0:T(8,128)S(1)}, f32[32,512]{1,0:T(8,128)S(1)}, u32[]{:S(2)}, u32[]{:S(2)}) collective-permute-start(f32[32,512]{1,0:T(8,128)S(1)} %get-tuple-element.69), channel_id=1, source_target_pairs={{0,24},{2,26},{4,28},{6,30},{8,16},{10,18},{12,20},{14,22},{16,8},... | collective-permute-start | bytes 196616 | tf_op jit(solution)/shard_map/ppermute | solution.py:17
  (176 shorter events, 78.0 us)
Async XLA Ops:
  3.7 7.5 %collective-permute-start.1 = (f32[32,512]{1,0:T(8,128)}, f32[32,512]{1,0:T(8,128)S(1)}, u32[]{:S(2)}, u32[]{:S(2)}) collective-permute-start(f32[32,512]{1,0:T(8,128)} %bitcast.23), channel_id=1, source_target_pairs={{0,16},{2,18},{4,20},{6,22},{8,24},{10,26},{12,28},{14,30},{16,0},... | collective-permute-start | bytes 196616 | tf_op jit(solution)/shard_map/ppermute | solution.py:17
  18.6 16.2 %collective-permute-start.6 = (f32[256,256]{1,0:T(8,128)S(1)}, f32[256,256]{1,0:T(8,128)S(1)}, u32[]{:S(2)}, u32[]{:S(2)}) collective-permute-start(f32[256,256]{1,0:T(8,128)S(1)} %pad_maximum_fusion.2.refs_1_), channel_id=1, source_target_pairs={{0,2},{2,0},{4,6},{6,4},{8,10},{10,8},{12,14},{14,12},{16,18},{18,... | collective-permute-start | bytes 786440 | tf_op jit(solution)/shard_map/ppermute | solution.py:17
  21.5 13.4 %collective-permute-start.5 = (f32[256,256]{1,0:T(8,128)S(1)}, f32[256,256]{1,0:T(8,128)S(1)}, u32[]{:S(2)}, u32[]{:S(2)}) collective-permute-start(f32[256,256]{1,0:T(8,128)S(1)} %pad_maximum_fusion.1.refs_0_), channel_id=1, source_target_pairs={{0,4},{2,6},{4,0},{6,2},{8,12},{10,14},{12,8},{14,10},{16,20},{18,... | collective-permute-start | bytes 786440 | tf_op jit(solution)/shard_map/ppermute | solution.py:17
  34.2 11.4 %collective-permute-start.8 = (f32[256,256]{1,0:T(8,128)S(1)}, f32[256,256]{1,0:T(8,128)S(1)}, u32[]{:S(2)}, u32[]{:S(2)}) collective-permute-start(f32[256,256]{1,0:T(8,128)S(1)} %pad_maximum_fusion.2.refs_1_), channel_id=1, source_target_pairs={{1,0},{0,1},{3,2},{2,3},{5,4},{4,5},{7,6},{6,7},{9,8},{8,9},{11,10... | collective-permute-start | bytes 786440 | tf_op jit(solution)/shard_map/ppermute | solution.py:22
  34.3 11.8 %collective-permute-start.7 = (f32[256,256]{1,0:T(8,128)S(1)}, f32[256,256]{1,0:T(8,128)S(1)}, u32[]{:S(2)}, u32[]{:S(2)}) collective-permute-start(f32[256,256]{1,0:T(8,128)S(1)} %pad_maximum_fusion.1.refs_0_), channel_id=1, source_target_pairs={{1,0},{0,1},{3,2},{2,3},{5,4},{4,5},{7,6},{6,7},{9,8},{8,9},{11,10... | collective-permute-start | bytes 786440 | tf_op jit(solution)/shard_map/ppermute | solution.py:22
  34.8 11.3 %collective-permute-start.10 = (f32[256,256]{1,0:T(8,128)S(1)}, f32[256,256]{1,0:T(8,128)S(1)}, u32[]{:S(2)}, u32[]{:S(2)}) collective-permute-start(f32[256,256]{1,0:T(8,128)S(1)} %collective-permute-done.6.refs_3_), channel_id=1, source_target_pairs={{1,0},{0,1},{3,2},{2,3},{5,4},{4,5},{7,6},{6,7},{9,8},{8,9},{11,10... | collective-permute-start | bytes 786440 | tf_op jit(solution)/shard_map/ppermute | solution.py:22
  34.9 11.2 %collective-permute-start.9 = (f32[256,256]{1,0:T(8,128)S(1)}, f32[256,256]{1,0:T(8,128)S(1)}, u32[]{:S(2)}, u32[]{:S(2)}) collective-permute-start(f32[256,256]{1,0:T(8,128)S(1)} %collective-permute-done.5.refs_2_), channel_id=1, source_target_pairs={{1,0},{0,1},{3,2},{2,3},{5,4},{4,5},{7,6},{6,7},{9,8},{8,9},{11,10... | collective-permute-start | bytes 786440 | tf_op jit(solution)/shard_map/ppermute | solution.py:22
  45.5 8.2 %collective-permute-start.22 = (f32[256,256]{1,0:T(8,128)S(1)}, f32[256,256]{1,0:T(8,128)S(1)}, u32[]{:S(2)}, u32[]{:S(2)}) collective-permute-start(f32[256,256]{1,0:T(8,128)S(1)} %get-tuple-element.49), channel_id=1, source_target_pairs={{1,0},{0,1},{3,2},{2,3},{5,4},{4,5},{7,6},{6,7},{9,8},{8,9},{11,10... | collective-permute-start | bytes 786440 | tf_op jit(solution)/shard_map/ppermute | solution.py:22
  45.7 19.6 %collective-permute-start.18 = (f32[256,256]{1,0:T(8,128)S(1)}, f32[256,256]{1,0:T(8,128)S(1)}, u32[]{:S(2)}, u32[]{:S(2)}) collective-permute-start(f32[256,256]{1,0:T(8,128)S(1)} %get-tuple-element.45), channel_id=1, source_target_pairs={{1,0},{0,1},{3,2},{2,3},{5,4},{4,5},{7,6},{6,7},{9,8},{8,9},{11,10... | collective-permute-start | bytes 786440 | tf_op jit(solution)/shard_map/ppermute | solution.py:22
  53.3 17.4 %collective-permute-start.21 = (f32[256,256]{1,0:T(8,128)S(1)}, f32[256,256]{1,0:T(8,128)S(1)}, u32[]{:S(2)}, u32[]{:S(2)}) collective-permute-start(f32[256,256]{1,0:T(8,128)S(1)} %get-tuple-element.47), channel_id=1, source_target_pairs={{1,0},{0,1},{3,2},{2,3},{5,4},{4,5},{7,6},{6,7},{9,8},{8,9},{11,10... | collective-permute-start | bytes 786440 | tf_op jit(solution)/shard_map/ppermute | solution.py:22
  53.8 17.0 %collective-permute-start.23 = (f32[256,256]{1,0:T(8,128)S(1)}, f32[256,256]{1,0:T(8,128)S(1)}, u32[]{:S(2)}, u32[]{:S(2)}) collective-permute-start(f32[256,256]{1,0:T(8,128)S(1)} %add.137), channel_id=1, source_target_pairs={{0,4},{2,6},{4,0},{6,2},{8,12},{10,14},{12,8},{14,10},{16,20},{18,... | collective-permute-start | bytes 786440 | tf_op jit(solution)/shard_map/ppermute | solution.py:17
  67.5 9.2 %collective-permute-start.19 = (f32[256,256]{1,0:T(8,128)S(1)}, f32[256,256]{1,0:T(8,128)S(1)}, u32[]{:S(2)}, u32[]{:S(2)}) collective-permute-start(f32[256,256]{1,0:T(8,128)S(1)} %add.133), channel_id=1, source_target_pairs={{0,2},{2,0},{4,6},{6,4},{8,10},{10,8},{12,14},{14,12},{16,18},{18,... | collective-permute-start | bytes 786440 | tf_op jit(solution)/shard_map/ppermute | solution.py:17
  70.8 8.2 %collective-permute-start.24 = (f32[128,256]{1,0:T(8,128)S(1)}, f32[128,256]{1,0:T(8,128)S(1)}, u32[]{:S(2)}, u32[]{:S(2)}) collective-permute-start(f32[128,256]{1,0:T(8,128)S(1)} %slice.125), channel_id=1, source_target_pairs={{0,2},{2,0},{4,6},{6,4},{8,10},{10,8},{12,14},{14,12},{16,18},{18,... | collective-permute-start | bytes 393224 | tf_op jit(solution)/shard_map/ppermute | solution.py:17
  111.9 14.9 %collective-permute-start.36 = (f32[256,256]{1,0:T(8,128)S(1)}, f32[256,256]{1,0:T(8,128)S(1)}, u32[]{:S(2)}, u32[]{:S(2)}) collective-permute-start(f32[256,256]{1,0:T(8,128)S(1)} %pad_maximum_fusion.5.refs_1_), channel_id=1, source_target_pairs={{1,0},{0,1},{3,2},{2,3},{5,4},{4,5},{7,6},{6,7},{9,8},{8,9},{11,10... | collective-permute-start | bytes 786440 | tf_op jit(solution)/shard_map/ppermute | solution.py:22
  112.0 14.8 %collective-permute-start.35 = (f32[256,256]{1,0:T(8,128)S(1)}, f32[256,256]{1,0:T(8,128)S(1)}, u32[]{:S(2)}, u32[]{:S(2)}) collective-permute-start(f32[256,256]{1,0:T(8,128)S(1)} %pad_maximum_fusion.4.refs_0_), channel_id=1, source_target_pairs={{1,0},{0,1},{3,2},{2,3},{5,4},{4,5},{7,6},{6,7},{9,8},{8,9},{11,10... | collective-permute-start | bytes 786440 | tf_op jit(solution)/shard_map/ppermute | solution.py:22
  114.9 11.9 %collective-permute-start.38 = (f32[256,256]{1,0:T(8,128)S(1)}, f32[256,256]{1,0:T(8,128)S(1)}, u32[]{:S(2)}, u32[]{:S(2)}) collective-permute-start(f32[256,256]{1,0:T(8,128)S(1)} %collective-permute-done.34.refs_3_), channel_id=1, source_target_pairs={{1,0},{0,1},{3,2},{2,3},{5,4},{4,5},{7,6},{6,7},{9,8},{8,9},{11,10... | collective-permute-start | bytes 786440 | tf_op jit(solution)/shard_map/ppermute | solution.py:22
  116.5 10.3 %collective-permute-start.37 = (f32[256,256]{1,0:T(8,128)S(1)}, f32[256,256]{1,0:T(8,128)S(1)}, u32[]{:S(2)}, u32[]{:S(2)}) collective-permute-start(f32[256,256]{1,0:T(8,128)S(1)} %collective-permute-done.33.refs_2_), channel_id=1, source_target_pairs={{1,0},{0,1},{3,2},{2,3},{5,4},{4,5},{7,6},{6,7},{9,8},{8,9},{11,10... | collective-permute-start | bytes 786440 | tf_op jit(solution)/shard_map/ppermute | solution.py:22
  126.3 24.0 %collective-permute-start.50 = (f32[256,256]{1,0:T(8,128)}, f32[256,256]{1,0:T(8,128)S(1)}, u32[]{:S(2)}, u32[]{:S(2)}) collective-permute-start(f32[256,256]{1,0:T(8,128)} %get-tuple-element.62), channel_id=1, source_target_pairs={{1,0},{0,1},{3,2},{2,3},{5,4},{4,5},{7,6},{6,7},{9,8},{8,9},{11,10... | collective-permute-start | bytes 786440 | tf_op jit(solution)/shard_map/ppermute | solution.py:22
  126.8 23.6 %collective-permute-start.46 = (f32[256,256]{1,0:T(8,128)}, f32[256,256]{1,0:T(8,128)S(1)}, u32[]{:S(2)}, u32[]{:S(2)}) collective-permute-start(f32[256,256]{1,0:T(8,128)} %get-tuple-element.58), channel_id=1, source_target_pairs={{1,0},{0,1},{3,2},{2,3},{5,4},{4,5},{7,6},{6,7},{9,8},{8,9},{11,10... | collective-permute-start | bytes 786440 | tf_op jit(solution)/shard_map/ppermute | solution.py:22
  145.2 7.0 %collective-permute-start.43 = (f32[8,128]{1,0:T(8,128)S(1)}, f32[8,128]{1,0:T(8,128)S(1)}, u32[]{:S(2)}, u32[]{:S(2)}) collective-permute-start(f32[8,128]{1,0:T(8,128)S(1)} %add.145), channel_id=1, source_target_pairs={{0,16},{2,18},{4,20},{6,22},{8,24},{10,26},{12,28},{14,30},{16,0},... | collective-permute-start | bytes 12296 | tf_op jit(solution)/shard_map/ppermute | solution.py:17
  150.3 10.3 %collective-permute-start.49 = (f32[256,256]{1,0:T(8,128)S(1)}, f32[256,256]{1,0:T(8,128)S(1)}, u32[]{:S(2)}, u32[]{:S(2)}) collective-permute-start(f32[256,256]{1,0:T(8,128)S(1)} %copy-done.13), channel_id=1, source_target_pairs={{1,0},{0,1},{3,2},{2,3},{5,4},{4,5},{7,6},{6,7},{9,8},{8,9},{11,10... | collective-permute-start | bytes 786440 | tf_op jit(solution)/shard_map/ppermute | solution.py:22
  150.5 11.8 %collective-permute-start.45 = (f32[256,256]{1,0:T(8,128)S(1)}, f32[256,256]{1,0:T(8,128)S(1)}, u32[]{:S(2)}, u32[]{:S(2)}) collective-permute-start(f32[256,256]{1,0:T(8,128)S(1)} %get-tuple-element.56), channel_id=1, source_target_pairs={{1,0},{0,1},{3,2},{2,3},{5,4},{4,5},{7,6},{6,7},{9,8},{8,9},{11,10... | collective-permute-start | bytes 786440 | tf_op jit(solution)/shard_map/ppermute | solution.py:22
  151.1 9.6 %collective-permute-start.51 = (f32[256,256]{1,0:T(8,128)S(1)}, f32[256,256]{1,0:T(8,128)S(1)}, u32[]{:S(2)}, u32[]{:S(2)}) collective-permute-start(f32[256,256]{1,0:T(8,128)S(1)} %add.161), channel_id=1, source_target_pairs={{0,4},{2,6},{4,0},{6,2},{8,12},{10,14},{12,8},{14,10},{16,20},{18,... | collective-permute-start | bytes 786440 | tf_op jit(solution)/shard_map/ppermute | solution.py:17
  152.2 10.0 %collective-permute-start.47 = (f32[256,256]{1,0:T(8,128)S(1)}, f32[256,256]{1,0:T(8,128)S(1)}, u32[]{:S(2)}, u32[]{:S(2)}) collective-permute-start(f32[256,256]{1,0:T(8,128)S(1)} %add.157), channel_id=1, source_target_pairs={{0,2},{2,0},{4,6},{6,4},{8,10},{10,8},{12,14},{14,12},{16,18},{18,... | collective-permute-start | bytes 786440 | tf_op jit(solution)/shard_map/ppermute | solution.py:17
  (50 other events, 372.0 us)

commit v2 on v0

v2 whole, which is shorter than its diff:
```python
import functools
import math

import jax
import jax.numpy as jnp
from jax import lax
from jax.experimental import pallas as pl
from jax.experimental.pallas import tpu as pltpu
from jax.sharding import PartitionSpec as P

F32, BF16 = jnp.float32, jnp.bfloat16
LIMIT = 12 * 1024 * 1024
X, Y = 1, 2
EDGE = 8


def deep_masks(count):
    bits = [4 << b for b in range((count // 4).bit_length() - 1)]
    return bits[:1] + [bits[0] | bits[1]] + bits[2:] if len(bits) > 1 else bits


def streams(count):
    deep = deep_masks(count)
    return deep + [X, Y], deep[::-1] + [Y, X]


def offsets(masks):
    slots = [0]
    for mask in masks:
        slots = slots + [slot ^ mask for slot in slots]
    return slots


def row_order(count):
    a, b = (offsets(masks) for masks in streams(count))
    middle = count // 2
    return (
        [(s, 0) for s in a[:middle]] + [(s, 1) for s in b[:middle]]
        + [(s, 0) for s in a[middle:]] + [(s, 1) for s in b[middle:]]
    )


def swap(block, mask):
    return lax.ppermute(block, "pair", [(i, i ^ mask) for i in range(lax.axis_size("pair"))])


def shifted(block, distance):
    size = lax.axis_size("sector")
    return lax.ppermute(block, "sector", [((i - distance) % size, i) for i in range(size)])


def neighbours(block):
    if lax.axis_size("sector") == 2:
        return [shifted(block, 1)]
    return [shifted(block, 1), shifted(block, -1)]


def to_neighbours(blocks):
    if lax.axis_size("sector") == 2:
        return [shifted(blocks[0], 1)]
    return [shifted(blocks[0], -1), shifted(blocks[1], 1)]


def over_sectors(tile):
    if lax.axis_size("sector") == 2:
        return [tile, shifted(tile, 1)]
    return [lax.psum(tile, "sector")]


def array(*shape, kind=F32):
    return jax.ShapeDtypeStruct(shape, kind)


def kernel_call(body, outs, *groups, scalars=(), scratch=(), flops=0):
    flat = [value for group in groups for value in group]

    def kernel(*refs):
        refs = list(refs)
        take = lambda n: [refs.pop(0) for _ in range(n)]
        fixed = take(len(scalars))
        inputs = [take(len(group)) for group in groups]
        body(fixed, inputs, take(len(outs)), refs)

    traffic = sum(v.size * v.dtype.itemsize for v in flat)
    return pl.pallas_call(
        kernel,
        in_specs=[pl.BlockSpec(memory_space=pltpu.SMEM)] * len(scalars)
        + [pl.BlockSpec(memory_space=pltpu.VMEM)] * len(flat),
        out_specs=[pl.BlockSpec(memory_space=pltpu.VMEM)] * len(outs),
        out_shape=list(outs),
        scratch_shapes=list(scratch),
        compiler_params=pltpu.CompilerParams(vmem_limit_bytes=LIMIT),
        cost_estimate=pl.CostEstimate(flops=max(flops, traffic), bytes_accessed=traffic, transcendentals=0),
    )(*scalars, *flat)


def split(value):
    high = value.astype(BF16)
    return high, (value - high.astype(F32)).astype(BF16)


def dot(first, second):
    return jnp.dot(first, second, preferred_element_type=F32)


def dot3(first, second):
    return dot(first[0], second[0]) + dot(first[0], second[1]) + dot(first[1], second[0])


def tile_rows(values):
    shape = (EDGE, values[0].shape[1])
    row = lax.broadcasted_iota(jnp.int32, shape, 0)
    tile = jnp.zeros(shape, F32)
    for at, value in enumerate(values):
        tile = jnp.where(row == at, value, tile)
    return tile


def summed(value, width):
    return jnp.broadcast_to(jnp.sum(value, keepdims=True), (1, width))


def prepare(me, left_ops, right_ops, block, count):
    pairs, _, m, _ = left_ops.shape
    rows = m // count // 2
    order = row_order(count)

    def kernel(me_ref, left_ref, right_ref, block_ref, left_out, left_t_out, right_out, right_t_out, edge, held):
        def reorder(value):
            held[...] = value
            parts = []
            for slot, half in order:
                where = pl.multiple_of((me_ref[0] ^ slot) * (2 * rows) + half * rows, rows)
                parts.append(held[pl.ds(where, rows), :])
            return jnp.concatenate(parts, axis=0)

        turned = reorder(reorder(left_ref[...]).T)
        left_t_out[0], left_t_out[1] = split(turned)
        left_out[0], left_out[1] = split(turned.T)
        value = right_ref[...]
        right_out[0], right_out[1] = split(value)
        right_t_out[0], right_t_out[1] = split(value.T)
        edge[...] = tile_rows([jnp.zeros((1, m), F32), summed(block_ref[...] * block_ref[...], m)])

    source = pl.BlockSpec((None, None, m, m), lambda p, *_: (p, 0, 0, 0))
    target = pl.BlockSpec((None, 2, m, m), lambda p, *_: (p, 0, 0, 0))
    whole = pl.BlockSpec(memory_space=pltpu.VMEM)
    return pl.pallas_call(
        kernel,
        grid_spec=pltpu.PrefetchScalarGridSpec(
            num_scalar_prefetch=1,
            grid=(pairs,),
            in_specs=[source, source, whole],
            out_specs=[target] * 4 + [whole],
            scratch_shapes=[pltpu.VMEM((m, m), F32)],
        ),
        out_shape=[array(pairs, 2, m, m, kind=BF16)] * 4 + [array(EDGE, m)],
        compiler_params=pltpu.CompilerParams(vmem_limit_bytes=2 * LIMIT),
        cost_estimate=pl.CostEstimate(flops=pairs * m * m * 1500, bytes_accessed=24 * pairs * m * m, transcendentals=0),
    )(me, left_ops, right_ops, block)


def block_of(charge, sectors):
    return jnp.where(charge == 1, 0, 1 if sectors == 2 else jnp.where(charge == 0, 1, 2))


def double(a, b, masks_a, masks_b):
    for mask_a, mask_b in zip(masks_a, masks_b):
        more_a, more_b = swap(a, mask_a), swap(b, mask_b)
        rows, m = a.shape

        def body(_, inputs, outs, scratch):
            for (low, high), out in zip(inputs, outs):
                out[:rows, :] = low[...]
                out[rows:, :] = high[...]

        a, b = kernel_call(body, [array(2 * rows, m)] * 2, [a, more_a], [b, more_b])
    return a, b


def sigma_apply(column_a, column_b, ops, scalars, edge):
    left, left_t, right, right_t = ops
    pairs, m = left.shape[0], left.shape[2]
    count, sectors = lax.axis_size("pair"), lax.axis_size("sector")
    blocks = min(sectors, 3)
    half, quarter, eighth = m // 2, m // 4, m // 8
    rows_of = array(half, m)
    made = array(pairs, 2, half, m, kind=BF16)
    held = pltpu.VMEM((blocks, 2, half, m), BF16)
    cost = 6 * half * m * m * pairs

    def hold(scratch, groups):
        for block, group in enumerate(groups):
            at = 0
            for ref in group:
                size = ref.shape[0]
                scratch[block, 0, at : at + size, :], scratch[block, 1, at : at + size, :] = split(ref[...])
                at += size

    def gains(fixed, pair):
        charge = fixed[0][pair]
        return block_of(charge, sectors), fixed[1][0, charge].astype(F32)

    def parts(ref, *index):
        return ref[index[0], 0], ref[index[0], 1]

    more_a, more_b = swap(column_a, X), swap(column_b, Y)

    def join(_, inputs, outs, scratch):
        both, a, b = outs
        for at, (low, high), out in ((0, inputs[0], a), (quarter, inputs[1], b)):
            out[:eighth, :] = low[...]
            out[eighth:, :] = high[...]
            both[at : at + eighth, :] = low[...]
            both[at + eighth : at + quarter, :] = high[...]

    early, a, b = kernel_call(
        join, [rows_of, array(quarter, m), array(quarter, m)], [column_a, more_a], [column_b, more_b]
    )
    late = [swap(a, Y), swap(b, X)]
    early_others = neighbours(early)

    def first_inner(fixed, inputs, outs, scratch):
        (own, *others), rights, rights_t = inputs
        hold(scratch[0], [[own]] + [[other] for other in others])
        for pair in range(pairs):
            block, allowed = gains(fixed, pair)
            forward = dot3(parts(scratch[0], 0), parts(rights_t[0], pair)) * allowed
            outs[0][pair, 0], outs[0][pair, 1] = split(forward)
            backward = dot3((scratch[0][block, 0], scratch[0][block, 1]), parts(rights[0], pair)) * allowed
            outs[1][pair, 0], outs[1][pair, 1] = split(backward)

    early_z, early_y = kernel_call(
        first_inner, [made] * 2, [early] + early_others, [right], [right_t],
        scalars=scalars, scratch=[held], flops=2 * cost,
    )
    late_others = [neighbours(piece) for piece in late]
    late_others = [[late_others[q][b] for q in range(2)] for b in range(blocks - 1)]

    def outer(ref, pair, at, first, second):
        rows = slice(at, at + half)
        total = dot3((ref[pair, 0, rows, :half], ref[pair, 1, rows, :half]), first)
        return total + dot3((ref[pair, 0, rows, half:], ref[pair, 1, rows, half:]), second)

    def forward_late(fixed, inputs, outs, scratch):
        own, (early_ref,), (rights_t,), (lefts,) = inputs
        z_out, total = outs[0], scratch[1]
        hold(scratch[0], [own])
        total[...] = jnp.zeros_like(total)
        for pair in range(pairs):
            block, allowed = gains(fixed, pair)
            inner = split(dot3(parts(scratch[0], 0), parts(rights_t, pair)) * allowed)
            z_out[pair, 0], z_out[pair, 1] = inner
            total[block] = total[block] + outer(lefts, pair, half, parts(early_ref, pair), inner)
        for block in range(blocks):
            outs[1 + block][...] = total[block]

    late_z, own_sent, *aimed = kernel_call(
        forward_late, [made] + [rows_of] * blocks, late, [early_z], [right_t], [left],
        scalars=scalars, scratch=[held, pltpu.VMEM((blocks, half, m), F32)], flops=3 * cost,
    )
    aimed_sent = to_neighbours(aimed)

    def backward_late(fixed, inputs, outs, scratch):
        groups, (early_ref,), (rights,), (lefts_t,), (base,) = inputs
        y_out, sent, product = outs
        hold(scratch[0], [groups[2 * block : 2 * block + 2] for block in range(blocks)])
        total = jnp.zeros((half, m), F32)
        for pair in range(pairs):
            block, allowed = gains(fixed, pair)
            inner = split(dot3((scratch[0][block, 0], scratch[0][block, 1]), parts(rights, pair)) * allowed)
            y_out[pair, 0], y_out[pair, 1] = inner
            total = total + outer(lefts_t, pair, half, parts(early_ref, pair), inner)
        sent[...] = total + base[...]
        own = jnp.concatenate([groups[0][...], groups[1][...]], axis=0)
        product[...] = jnp.broadcast_to(summed(own * total, m), (EDGE, m))

    late_y, own_sent, product = kernel_call(
        backward_late, [made, rows_of, array(EDGE, m)], late + sum(late_others, []), [early_y], [right], [left_t],
        [own_sent], scalars=scalars, scratch=[held], flops=3 * cost,
    )

    def add_sent(_, inputs, outs, scratch):
        value = sum(ref[...] for ref in inputs[0])
        outs[0][...] = value[:quarter]
        outs[1][...] = value[quarter:]

    sent_a, sent_b = kernel_call(add_sent, [array(quarter, m)] * 2, [own_sent] + aimed_sent)
    got_a, got_b = swap(sent_a, Y), swap(sent_b, X)

    def keep(fixed, inputs, outs, scratch):
        (z0, z1), (y0, y1), (lefts,), (lefts_t,), (own, product_ref, edge_ref) = inputs
        total = scratch[0]
        total[...] = jnp.zeros_like(total)
        back = jnp.zeros((half, m), F32)
        for pair in range(pairs):
            block, _ = gains(fixed, pair)
            total[block] = total[block] + outer(lefts, pair, 0, parts(z0, pair), parts(z1, pair))
        for block in range(1, blocks):
            outs[1 + block][...] = total[block]
        for pair in range(pairs):
            back = back + outer(lefts_t, pair, 0, parts(y0, pair), parts(y1, pair))
        outs[0][...] = total[0] + back
        product_sum = 2.0 * (summed(own[...] * back, m) + product_ref[:1, :])
        row = lax.broadcasted_iota(jnp.int32, (EDGE, m), 0)
        outs[1][...] = jnp.where(row == 0, product_sum, edge_ref[...])

    own_kept, edge, *aimed = kernel_call(
        keep, [rows_of, array(EDGE, m)] + [rows_of] * (blocks - 1), [early_z, late_z], [early_y, late_y], [left],
        [left_t], [early, product, edge],
        scalars=scalars, scratch=[pltpu.VMEM((blocks, half, m), F32)], flops=4 * cost,
    )
    aimed_kept = to_neighbours(aimed)
    edges = over_sectors(edge)

    def first_sum(_, inputs, outs, scratch):
        kept, (a_ref, b_ref), edge_refs = inputs
        value = sum(ref[...] for ref in kept)
        edge_sum = sum(ref[...] for ref in edge_refs)
        a_value, b_value = value[:quarter] + a_ref[...], value[quarter:] + b_ref[...]
        for (stay, go), total in ((outs[:2], a_value), (outs[2:4], b_value)):
            stay[...] = total[:eighth]
            go[:eighth, :] = total[eighth:]
            go[eighth:, :] = edge_sum
        outs[4][...] = edge_sum

    stay_a, go_a, stay_b, go_b, edge = kernel_call(
        first_sum, [array(eighth, m), array(eighth + EDGE, m)] * 2 + [array(EDGE, m)],
        [own_kept] + aimed_kept, [got_a, got_b], edges,
    )
    got_a, got_b, corner = swap(go_a, X), swap(go_b, Y), swap(edge, X | Y)

    def second_sum(_, inputs, outs, scratch):
        (a_stay, a_got), (b_stay, b_got), (edge_ref, corner_ref) = inputs
        outs[0][:eighth, :] = a_stay[...] + a_got[:eighth, :]
        outs[0][eighth:, :] = edge_ref[...] + a_got[eighth:, :] + b_got[eighth:, :] + corner_ref[...]
        outs[1][...] = b_stay[...] + b_got[:eighth, :]

    return kernel_call(
        second_sum, [array(eighth + EDGE, m), array(eighth, m)], [stay_a, got_a], [stay_b, got_b], [edge, corner]
    )


def turned(value, slots, mask, rows):
    parts = [value[slots.index(slot ^ mask) * rows :][:rows] for slot in slots]
    rest = value[len(slots) * rows :]
    return jnp.concatenate(parts + ([rest] if rest.shape[0] else []), axis=0)


def per_device(wavefunction, preconditioner, left_ops, right_ops, charges, coupling):
    vector, divisor = wavefunction[0], preconditioner[0]
    count = lax.axis_size("pair")
    deep = deep_masks(count)
    rows, m = vector.shape[0] // 2, vector.shape[1]
    tall = rows * (count // 4)
    me = lax.axis_index("pair").astype(jnp.int32)[None]
    *ops, edge = prepare(me, left_ops, right_ops, vector, count)
    scalars = (charges, coupling)
    vector_a, vector_b = double(vector[:rows], vector[rows:], deep, deep[::-1])
    divisor, _ = lax.optimization_barrier((divisor, vector_a))
    divisor_a, divisor_b = double(divisor[:rows], divisor[rows:], deep, deep[::-1])

    image_a, image_b = sigma_apply(vector_a, vector_b, ops, scalars, edge)
    slots_a, slots_b = offsets(deep), offsets(deep[::-1])
    for mask_a, mask_b in zip(deep[:0:-1], deep[:-1]):

        def add_columns(_, inputs, outs, scratch):
            (a_ref, a_got), (b_ref, b_got) = inputs
            outs[0][...] = a_ref[...] + turned(a_got[...], slots_a, mask_a, rows)
            outs[1][...] = b_ref[...] + turned(b_got[...], slots_b, mask_b, rows)

        image_a, image_b = kernel_call(
            add_columns, [array(*image_a.shape), array(*image_b.shape)],
            [image_a, swap(image_a, mask_a)], [image_b, swap(image_b, mask_b)],
        )

    last_a, last_b = deep[0], deep[-1]

    def correct(_, inputs, outs, scratch):
        (a0, a1), (b0, b1), (wa, wb), (pa, pb) = inputs
        correction_a, correction_b, image_own, sums_out, edge_out = outs
        total_a = a0[...] + turned(a1[...], slots_a, last_a, rows)
        total_b = b0[...] + turned(b1[...], slots_b, last_b, rows)
        sums = total_a[tall:]
        theta = sums[0:1, :] / sums[1:2, :]
        ca = (total_a[:tall] - theta * wa[...]) / pa[...]
        cb = (total_b - theta * wb[...]) / pb[...]
        correction_a[...] = ca
        correction_b[...] = cb
        image_own[:rows, :] = total_a[:rows]
        image_own[rows:, :] = total_b[:rows]
        sums_out[...] = sums

        def inner(first, second):
            return summed(first[0] * second[0], m) + summed(first[1] * second[1], m)

        own_w, own_c = (wa[:rows, :], wb[:rows, :]), (ca[:rows], cb[:rows])
        own_a = (total_a[:rows], total_b[:rows])
        edge_out[...] = tile_rows(
            [jnp.zeros((1, m), F32), inner(own_w, own_c), inner(own_c, own_c), inner(own_a, own_c)]
        )

    ca, cb, image_own, sums, edge = kernel_call(
        correct, [array(tall, m), array(tall, m), array(2 * rows, m), array(EDGE, m), array(EDGE, m)],
        [image_a, swap(image_a, last_a)], [image_b, swap(image_b, last_b)], [vector_a, vector_b],
        [divisor_a, divisor_b],
    )
    own_c = (ca, cb)
    second_a, second_b = sigma_apply(ca, cb, ops, scalars, edge)

    for mask_a, mask_b in zip(deep[::-1], deep):
        size = second_b.shape[0] // 2

        def cut(_, inputs, outs, scratch):
            a_ref, b_ref = inputs[0]
            outs[0][...] = a_ref[size:, :]
            outs[1][...] = b_ref[size:, :]

        def meet(_, inputs, outs, scratch):
            (a_ref, a_got), (b_ref, b_got) = inputs
            outs[0][:size, :] = a_ref[:size, :] + a_got[:size, :]
            outs[0][size:, :] = a_ref[2 * size :, :] + a_got[size:, :]
            outs[1][...] = b_ref[:size, :] + b_got[...]

        go_a, go_b = kernel_call(cut, [array(size + EDGE, m), array(size, m)], [second_a, second_b])
        second_a, second_b = kernel_call(
            meet, [array(size + EDGE, m), array(size, m)],
            [second_a, swap(go_a, mask_a)], [second_b, swap(go_b, mask_b)],
        )

    scale = math.sqrt(lax.axis_size("sector") * count * vector.shape[0] * m)

    def finish(_, inputs, outs, scratch):
        (a_ref, b_ref), (vector_ref, image_ref, ca_ref, cb_ref), (first_ref,) = inputs
        sums = a_ref[rows:, :]
        correlation, norm_sq = first_ref[0:1, :], first_ref[1:2, :]
        theta = correlation / norm_sq
        inverse = lax.rsqrt(norm_sq)
        along = sums[1:2] / norm_sq
        length_sq = (sums[2:3] - along * sums[1:2]) / norm_sq
        factor = inverse * lax.rsqrt(length_sq + 1e-30)
        corner = factor * factor * (sums[0:1] - 2.0 * along * sums[3:4] + along * along * correlation)
        cross = inverse * factor * (sums[3:4] - along * correlation)
        spread = (theta - corner) / 2.0
        lowest = (theta + corner) / 2.0 - jnp.sqrt(spread * spread + cross * cross)
        first_weight = corner - lowest
        second_weight = -cross
        size_norm = jnp.sqrt(first_weight * first_weight + second_weight * second_weight + 1e-30)
        factor_two = scale * second_weight / size_norm * factor
        factor_one = scale * first_weight / size_norm * inverse - factor_two * along
        for at, c_ref, s_ref in ((0, ca_ref, a_ref), (rows, cb_ref, b_ref)):
            span = slice(at, at + rows)
            outs[0][span, :] = factor_one * vector_ref[span, :] + factor_two * c_ref[:rows, :]
            outs[1][span, :] = factor_one * image_ref[span, :] + factor_two * s_ref[:rows, :]
        row = lax.broadcasted_iota(jnp.int32, (EDGE, m), 1)
        outs[2][...] = jnp.where(row == 0, theta, lowest)

    state, image, energies = kernel_call(
        finish, [array(2 * rows, m), array(2 * rows, m), array(EDGE, m)], [second_a, second_b],
        [vector, image_own, own_c[0], own_c[1]], [sums],
    )
    return (state[None], image[None], energies[0, :2])


def solution(mesh):
    in_specs = (
        P("sector", "pair", None),
        P("sector", "pair", None),
        P("pair", "sector", None, None),
        P("pair", "sector", None, None),
        P("pair"),
        P("sector", None),
    )
    out_specs = (P("sector", "pair", None), P("sector", "pair", None), P())
    return jax.shard_map(
        per_device, mesh=mesh, in_specs=in_specs, out_specs=out_specs, check_vma=False
    )
```

time: 615 us -> 153 us (0.25); the launches traced: 604 us -> 153 us
  waiting for transfers between devices: 340 us -> 69.6 us
  blocking collectives: 116 us -> 0 us
  matrix products: 85 us -> 0 us
  starting transfers between devices: 2.17 us -> 43.4 us
  Pallas kernels: 0 us -> 32.8 us
  between operations: 30.9 us -> 0.91 us
  local copies, waits for them, and re-layouts: 22.4 us -> 5.93 us
  other arithmetic: 7.79 us -> 0 us
    all_gather x4 -> x0, waiting for transfers between devices: 178 us -> none  [the longest x2 101 us: sigma_apply(): lax.all_gather(vector, 'pair', axis=1, tiled=True)]
    reduce_scatter x2 -> x0, waiting for transfers between devices: 155 us -> none  [sigma_apply(): lax.psum_scatter(combined[None], 'pair', scatter_dimension=1, tiled=True)]
    psum x3 -> x0, blocking collectives: 116 us -> none  [the longest x1 41.4 us: per_device(): lax.psum((jnp.sum(vector * correction), jnp.sum(correction * correction))...]
    dot_general x24 -> x0, matrix products: 85 us -> none  [product(): jnp.dot(first, second, precision=highest, preferred_element_type=jnp.floa...]
    ppermute x6 -> x46, waiting for transfers between devices: 5.96 us -> 69.6 us  [the longest x34 67.2 us: swap(): lax.ppermute(block, 'pair', [(i, i ^ mask) for i in range(lax.axis_size('...]
    ppermute x6 -> x46, starting transfers between devices: 1.76 us -> 43.4 us  [the longest x34 41.2 us: swap(): lax.ppermute(block, 'pair', [(i, i ^ mask) for i in range(lax.axis_size('...]
    pallas_call x0 -> x28, Pallas kernels: none -> 32.8 us  [the longest x27 29.4 us: kernel_call(): pl.pallas_call(kernel, in_specs=[pl.BlockSpec(memory_space=pltpu.SMEM)] *...]
    dynamic_slice x5 -> x0, local copies, waits for them, and re-layouts: 6.61 us -> none  [the longest x4 5.17 us: sigma_apply(): current = lax.dynamic_index_in_dim(targets, charge_slot, 0, keepdims=False)]
  transfers between devices with their start and end apart: 12 -> 46, of which waited for: 12 -> 25; matrix products, arithmetic and copies ran while one was open for 7% -> 0% of each run, Pallas kernels for 0% -> 21%
where the time goes in v2:
time: 153 us
  waiting for transfers between devices  69.6 us (45%)
  starting transfers between devices  43.4 us (28%)
  Pallas kernels  32.8 us (21%)
  local copies, waits for them, and re-layouts  5.93 us (4%)
    ppermute x34, waiting for transfers between devices, swap(): lax.ppermute(block, 'pair', [(i, i ^ mask) for i in range(lax.axis_size('...  67.2 us
    ppermute x34, starting transfers between devices, swap(): lax.ppermute(block, 'pair', [(i, i ^ mask) for i in range(lax.axis_size('...  41.2 us
    pallas_call x27, Pallas kernels, kernel_call(): pl.pallas_call(kernel, in_specs=[pl.BlockSpec(memory_space=pltpu.SMEM)] *...  29.4 us
    unnamed x12, local copies, waits for them, and re-layouts  4.63 us
    pallas_call x1, Pallas kernels, prepare(): pl.pallas_call(kernel, grid_spec=pltpu.PrefetchScalarGridSpec(num_scalar_...  3.36 us
  transfers between devices with their start and end apart: 46, of which 25 were waited for; matrix products, arithmetic and copies ran while one was open for 0% of the time, Pallas kernels for 21%

profile of v2, /device:TPU:0, one launch (start us, length us, event | category | flops | bytes accessed | tf_op | source)
XLA Modules:
  0.0 152.6 jit_solution(16401866105950981107)
XLA Ops:
  1.4 3.1 %collective-permute-start = (f32[16,512]{1,0:T(8,128)S(1)}, f32[16,512]{1,0:T(8,128)S(1)}, u32[]{:S(2)}, u32[]{:S(2)}) collective-permute-start(f32[16,512]{1,0:T(8,128)S(1)} %get-tuple-element.162.refs_0_), channel_id=1, source_target_pairs={{0,8},{2,10},{4,12},{6,14},{8,0},{10,2},{12,4},{14,6},{16,24},{18,... | collective-permute-start | bytes 98312 | tf_op jit(solution)/shard_map/ppermute | solution.py:44
  6.9 3.2 %collective-permute-done.1.refs_3_ = f32[16,512]{1,0:T(8,128)S(1)} collective-permute-done((f32[16,512]{1,0:T(8,128)S(1)}, f32[16,512]{1,0:T(8,128)S(1)}, u32[]{:S(2)}, u32[]{:S(2)}) %collective-permute-start.1) | collective-permute-done | bytes 32800 | tf_op jit(solution)/shard_map/ppermute | solution.py:44
  10.2 2.5 %collective-permute-start.2 = (f32[32,512]{1,0:T(8,128)S(1)}, f32[32,512]{1,0:T(8,128)S(1)}, u32[]{:S(2)}, u32[]{:S(2)}) collective-permute-start(f32[32,512]{1,0:T(8,128)S(1)} %get-tuple-element.81.refs_0_), channel_id=1, source_target_pairs={{0,24},{2,26},{4,28},{6,30},{8,16},{10,18},{12,20},{14,22},{16,8},... | collective-permute-start | bytes 196616 | tf_op jit(solution)/shard_map/ppermute | solution.py:44
  12.7 3.6 %collective-permute-done.2.refs_1_ = f32[32,512]{1,0:T(8,128)S(1)} collective-permute-done((f32[32,512]{1,0:T(8,128)S(1)}, f32[32,512]{1,0:T(8,128)S(1)}, u32[]{:S(2)}, u32[]{:S(2)}) %collective-permute-start.2) | collective-permute-done | bytes 65568 | tf_op jit(solution)/shard_map/ppermute | solution.py:44
  30.5 3.4 %shard_map.88 = (bf16[3,2,512,512]{3,2,1,0:T(8,128)(2,1)S(1)}, bf16[3,2,512,512]{3,2,1,0:T(8,128)(2,1)S(1)}, bf16[3,2,512,512]{3,2,1,0:T(8,128)(2,1)S(1)}, bf16[...) custom-call(s32[1]{0:T(128)} %bitcast.2.me_ref, f32[3,1,512,512]{3,2,1,0:T(8,128)S(1)} %copy-done, ...), custom_call_target="tpu_custom_call" | custom-call | flops 1179648000 | bytes 18874368 | tf_op jit(solution)/shard_map/pallas_call | solution.py:148
  34.4 3.3 %shard_map.89 = (bf16[3,2,256,512]{3,2,1,0:T(8,128)(2,1)S(1)}, bf16[3,2,256,512]{3,2,1,0:T(8,128)(2,1)S(1)}) custom-call(s32[3]{0:T(128)S(1)} %copy-done.3, s32[1,3]{1,0:T(1,128)S(1)} %copy-done.4, f32[256,512]{1,0:T(8,128)S(1)} %get-tuple-element.85.refs_2_.refs_8_, f32[256,512]{1,0:T(8,128)S(1)} %collective-permute-done.6.refs_3_, ...), custom_call_target="tpu_custom_call" | custom-call | flops 2415919104 | bytes 7340032 | tf_op jit(solution)/shard_map/pallas_call | solution.py:85
  37.8 3.5 %shard_map.90 = (bf16[3,2,256,512]{3,2,1,0:T(8,128)(2,1)S(1)}, f32[256,512]{1,0:T(8,128)S(1)}, f32[256,512]{1,0:T(8,128)S(1)}) custom-call(s32[3]{0:T(128)S(1)} %copy-done.3, s32[1,3]{1,0:T(1,128)S(1)} %copy-done.4, f32[128,512]{1,0:T(8,128)S(1)} %collective-permute-done.7.refs_2_, f32[128,512]{1,0:T(8,128)S(1)} %collective-permute-done.8.refs_3_, ...), custom_call_target="tpu_custom_call" | custom-call | flops 3623878656 | bytes 8388608 | tf_op jit(solution)/shard_map/pallas_call | solution.py:85
  41.4 3.6 %shard_map.91 = (bf16[3,2,256,512]{3,2,1,0:T(8,128)(2,1)S(1)}, f32[256,512]{1,0:T(8,128)S(1)}, f32[8,512]{1,0:T(8,128)S(1)}) custom-call(s32[3]{0:T(128)S(1)} %copy-done.3, s32[1,3]{1,0:T(1,128)S(1)} %copy-done.4, f32[128,512]{1,0:T(8,128)S(1)} %collective-permute-done.7.refs_2_, f32[128,512]{1,0:T(8,128)S(1)} %collective-permute-done.8.refs_3_, ...), custom_call_target="tpu_custom_call" | custom-call | flops 3623878656 | bytes 9437184 | tf_op jit(solution)/shard_map/pallas_call | solution.py:85
  45.0 3.5 %shard_map.92 = (f32[256,512]{1,0:T(8,128)S(1)}, f32[8,512]{1,0:T(8,128)S(1)}, f32[256,512]{1,0:T(8,128)S(1)}) custom-call(s32[3]{0:T(128)S(1)} %copy-done.3, s32[1,3]{1,0:T(1,128)S(1)} %copy-done.4, bf16[3,2,256,512]{3,2,1,0:T(8,128)(2,1)S(1)} %get-tuple-element.88.refs_4_.refs_2_, bf16[3,2,256,512]{3,2,1,0:T(8,128)(2,1)S(1)} %get-tuple-element.92.refs_3_, ...), custom_call_target="tpu_custom_call" | custom-call | flops 4831838208 | bytes 13139968 | tf_op jit(solution)/shard_map/pallas_call | solution.py:85
  52.2 5.1 %collective-permute-done.13.refs_2_ = f32[128,512]{1,0:T(8,128)S(1)} collective-permute-done((f32[128,512]{1,0:T(8,128)S(1)}, f32[128,512]{1,0:T(8,128)S(1)}, u32[]{:S(2)}, u32[]{:S(2)}) %collective-permute-start.13) | collective-permute-done | bytes 262176 | tf_op jit(solution)/shard_map/ppermute | solution.py:44
  61.2 4.2 %collective-permute-done.18.refs_5_ = f32[8,512]{1,0:T(8,128)S(1)} collective-permute-done((f32[8,512]{1,0:T(8,128)S(1)}, f32[8,512]{1,0:T(8,128)S(1)}, u32[]{:S(2)}, u32[]{:S(2)}) %collective-permute-start.18) | collective-permute-done | bytes 16416 | tf_op jit(solution)/shard_map/ppermute | solution.py:44
  67.5 7.4 %collective-permute-done.20.refs_3_ = f32[64,512]{1,0:T(8,128)S(1)} collective-permute-done((f32[64,512]{1,0:T(8,128)S(1)}, f32[64,512]{1,0:T(8,128)S(1)}, u32[]{:S(2)}, u32[]{:S(2)}) %collective-permute-start.20) | collective-permute-done | bytes 131104 | tf_op jit(solution)/shard_map/ppermute | solution.py:44
  80.1 3.2 %collective-permute-done.23.refs_1_ = f32[16,512]{1,0:T(8,128)S(1)} collective-permute-done((f32[16,512]{1,0:T(8,128)S(1)}, f32[16,512]{1,0:T(8,128)S(1)}, u32[]{:S(2)}, u32[]{:S(2)}) %collective-permute-start.23) | collective-permute-done | bytes 32800 | tf_op jit(solution)/shard_map/ppermute | solution.py:44
  86.4 4.1 %collective-permute-done.25.refs_1_ = f32[32,512]{1,0:T(8,128)S(1)} collective-permute-done((f32[32,512]{1,0:T(8,128)S(1)}, f32[32,512]{1,0:T(8,128)S(1)}, u32[]{:S(2)}, u32[]{:S(2)}) %collective-permute-start.25) | collective-permute-done | bytes 65568 | tf_op jit(solution)/shard_map/ppermute | solution.py:44
  92.6 3.9 %collective-permute-done.27.refs_1_ = f32[64,512]{1,0:T(8,128)S(1)} collective-permute-done((f32[64,512]{1,0:T(8,128)S(1)}, f32[64,512]{1,0:T(8,128)S(1)}, u32[]{:S(2)}, u32[]{:S(2)}) %collective-permute-start.27) | collective-permute-done | bytes 131104 | tf_op jit(solution)/shard_map/ppermute | solution.py:44
  99.0 6.8 %collective-permute-done.30.refs_2_ = f32[128,512]{1,0:T(8,128)S(1)} collective-permute-done((f32[128,512]{1,0:T(8,128)S(1)}, f32[128,512]{1,0:T(8,128)S(1)}, u32[]{:S(2)}, u32[]{:S(2)}) %collective-permute-start.30) | collective-permute-done | bytes 262176 | tf_op jit(solution)/shard_map/ppermute | solution.py:44
  106.4 3.5 %shard_map.101 = (bf16[3,2,256,512]{3,2,1,0:T(8,128)(2,1)S(1)}, bf16[3,2,256,512]{3,2,1,0:T(8,128)(2,1)S(1)}) custom-call(s32[3]{0:T(128)S(1)} %copy-done.3, s32[1,3]{1,0:T(1,128)S(1)} %copy-done.4, f32[256,512]{1,0:T(8,128)S(1)} %get-tuple-element.122.refs_2_.refs_8_, f32[256,512]{1,0:T(8,128)S(1)} %collective-permute-done.29.refs_3_, ...), custom_call_target="tpu_custom_call" | custom-call | flops 2415919104 | bytes 7340032 | tf_op jit(solution)/shard_map/pallas_call | solution.py:85
  109.9 3.5 %shard_map.102 = (bf16[3,2,256,512]{3,2,1,0:T(8,128)(2,1)S(1)}, f32[256,512]{1,0:T(8,128)S(1)}, f32[256,512]{1,0:T(8,128)S(1)}) custom-call(s32[3]{0:T(128)S(1)} %copy-done.3, s32[1,3]{1,0:T(1,128)S(1)} %copy-done.4, f32[128,512]{1,0:T(8,128)S(1)} %collective-permute-done.30.refs_2_, f32[128,512]{1,0:T(8,128)S(1)} %collective-permute-done.31.refs_3_, ...), custom_call_target="tpu_custom_call" | custom-call | flops 3623878656 | bytes 8388608 | tf_op jit(solution)/shard_map/pallas_call | solution.py:85
  113.7 3.6 %shard_map.103 = (bf16[3,2,256,512]{3,2,1,0:T(8,128)(2,1)S(1)}, f32[256,512]{1,0:T(8,128)S(1)}, f32[8,512]{1,0:T(8,128)S(1)}) custom-call(s32[3]{0:T(128)S(1)} %copy-done.3, s32[1,3]{1,0:T(1,128)S(1)} %copy-done.4, f32[128,512]{1,0:T(8,128)S(1)} %collective-permute-done.30.refs_2_, f32[128,512]{1,0:T(8,128)S(1)} %collective-permute-done.31.refs_3_, ...), custom_call_target="tpu_custom_call" | custom-call | flops 3623878656 | bytes 9437184 | tf_op jit(solution)/shard_map/pallas_call | solution.py:85
  117.3 3.5 %shard_map.104 = (f32[256,512]{1,0:T(8,128)S(1)}, f32[8,512]{1,0:T(8,128)S(1)}, f32[256,512]{1,0:T(8,128)S(1)}) custom-call(s32[3]{0:T(128)S(1)} %copy-done.3, s32[1,3]{1,0:T(1,128)S(1)} %copy-done.4, bf16[3,2,256,512]{3,2,1,0:T(8,128)(2,1)S(1)} %get-tuple-element.123.refs_4_.refs_2_, bf16[3,2,256,512]{3,2,1,0:T(8,128)(2,1)S(1)} %get-tuple-element.126.refs_3_, ...), custom_call_target="tpu_custom_call" | custom-call | flops 4831838208 | bytes 13139968 | tf_op jit(solution)/shard_map/pallas_call | solution.py:85
  125.1 4.6 %collective-permute-done.36.refs_2_ = f32[128,512]{1,0:T(8,128)S(1)} collective-permute-done((f32[128,512]{1,0:T(8,128)S(1)}, f32[128,512]{1,0:T(8,128)S(1)}, u32[]{:S(2)}, u32[]{:S(2)}) %collective-permute-start.36) | collective-permute-done | bytes 262176 | tf_op jit(solution)/shard_map/ppermute | solution.py:44
  134.5 3.1 %collective-permute-done.41.refs_5_ = f32[8,512]{1,0:T(8,128)S(1)} collective-permute-done((f32[8,512]{1,0:T(8,128)S(1)}, f32[8,512]{1,0:T(8,128)S(1)}, u32[]{:S(2)}, u32[]{:S(2)}) %collective-permute-start.41) | collective-permute-done | bytes 16416 | tf_op jit(solution)/shard_map/ppermute | solution.py:44
  139.8 5.6 %collective-permute-done.43.refs_3_ = f32[32,512]{1,0:T(8,128)S(1)} collective-permute-done((f32[32,512]{1,0:T(8,128)S(1)}, f32[32,512]{1,0:T(8,128)S(1)}, u32[]{:S(2)}, u32[]{:S(2)}) %collective-permute-start.43) | collective-permute-done | bytes 65568 | tf_op jit(solution)/shard_map/ppermute | solution.py:44
  147.2 4.1 %collective-permute-done.45.refs_3_ = f32[16,512]{1,0:T(8,128)S(1)} collective-permute-done((f32[16,512]{1,0:T(8,128)S(1)}, f32[16,512]{1,0:T(8,128)S(1)}, u32[]{:S(2)}, u32[]{:S(2)}) %collective-permute-start.45) | collective-permute-done | bytes 32800 | tf_op jit(solution)/shard_map/ppermute | solution.py:44
  (111 shorter events, 56.0 us)
Async XLA Ops:
  23.6 10.8 %collective-permute-start.6 = (f32[256,512]{1,0:T(8,128)S(1)}, f32[256,512]{1,0:T(8,128)S(1)}, u32[]{:S(2)}, u32[]{:S(2)}) collective-permute-start(f32[256,512]{1,0:T(8,128)S(1)} %get-tuple-element.85.refs_2_.refs_8_), channel_id=1, source_target_pairs={{1,0},{0,1},{3,2},{2,3},{5,4},{4,5},{7,6},{6,7},{9,8},{8,9},{11,10... | collective-permute-start | bytes 1572872 | tf_op jit(solution)/shard_map/ppermute | solution.py:49
  23.7 10.1 %collective-permute-start.8 = (f32[128,512]{1,0:T(8,128)S(1)}, f32[128,512]{1,0:T(8,128)S(1)}, u32[]{:S(2)}, u32[]{:S(2)}) collective-permute-start(f32[128,512]{1,0:T(8,128)S(1)} %get-tuple-element.90), channel_id=1, source_target_pairs={{0,2},{2,0},{4,6},{6,4},{8,10},{10,8},{12,14},{14,12},{16,18},{18,... | collective-permute-start | bytes 786440 | tf_op jit(solution)/shard_map/ppermute | solution.py:44
  24.3 9.6 %collective-permute-start.7 = (f32[128,512]{1,0:T(8,128)S(1)}, f32[128,512]{1,0:T(8,128)S(1)}, u32[]{:S(2)}, u32[]{:S(2)}) collective-permute-start(f32[128,512]{1,0:T(8,128)S(1)} %get-tuple-element.89), channel_id=1, source_target_pairs={{0,4},{2,6},{4,0},{6,2},{8,12},{10,14},{12,8},{14,10},{16,20},{18,... | collective-permute-start | bytes 786440 | tf_op jit(solution)/shard_map/ppermute | solution.py:44
  33.8 7.5 %collective-permute-start.10 = (f32[128,512]{1,0:T(8,128)S(1)}, f32[128,512]{1,0:T(8,128)S(1)}, u32[]{:S(2)}, u32[]{:S(2)}) collective-permute-start(f32[128,512]{1,0:T(8,128)S(1)} %collective-permute-done.8.refs_3_), channel_id=1, source_target_pairs={{1,0},{0,1},{3,2},{2,3},{5,4},{4,5},{7,6},{6,7},{9,8},{8,9},{11,10... | collective-permute-start | bytes 786440 | tf_op jit(solution)/shard_map/ppermute | solution.py:49
  33.9 7.5 %collective-permute-start.9 = (f32[128,512]{1,0:T(8,128)S(1)}, f32[128,512]{1,0:T(8,128)S(1)}, u32[]{:S(2)}, u32[]{:S(2)}) collective-permute-start(f32[128,512]{1,0:T(8,128)S(1)} %collective-permute-done.7.refs_2_), channel_id=1, source_target_pairs={{1,0},{0,1},{3,2},{2,3},{5,4},{4,5},{7,6},{6,7},{9,8},{8,9},{11,10... | collective-permute-start | bytes 786440 | tf_op jit(solution)/shard_map/ppermute | solution.py:49
  41.2 7.7 %collective-permute-start.12 = (f32[256,512]{1,0:T(8,128)S(1)}, f32[256,512]{1,0:T(8,128)S(1)}, u32[]{:S(2)}, u32[]{:S(2)}) collective-permute-start(f32[256,512]{1,0:T(8,128)S(1)} %get-tuple-element.102), channel_id=1, source_target_pairs={{1,0},{0,1},{3,2},{2,3},{5,4},{4,5},{7,6},{6,7},{9,8},{8,9},{11,10... | collective-permute-start | bytes 1572872 | tf_op jit(solution)/shard_map/ppermute | solution.py:49
  49.0 8.4 %collective-permute-start.13 = (f32[128,512]{1,0:T(8,128)S(1)}, f32[128,512]{1,0:T(8,128)S(1)}, u32[]{:S(2)}, u32[]{:S(2)}) collective-permute-start(f32[128,512]{1,0:T(8,128)S(1)} %get-tuple-element.103), channel_id=1, source_target_pairs={{0,4},{2,6},{4,0},{6,2},{8,12},{10,14},{12,8},{14,10},{16,20},{18,... | collective-permute-start | bytes 786440 | tf_op jit(solution)/shard_map/ppermute | solution.py:44
  49.6 8.0 %collective-permute-start.14 = (f32[128,512]{1,0:T(8,128)S(1)}, f32[128,512]{1,0:T(8,128)S(1)}, u32[]{:S(2)}, u32[]{:S(2)}) collective-permute-start(f32[128,512]{1,0:T(8,128)S(1)} %get-tuple-element.104), channel_id=1, source_target_pairs={{0,2},{2,0},{4,6},{6,4},{8,10},{10,8},{12,14},{14,12},{16,18},{18,... | collective-permute-start | bytes 786440 | tf_op jit(solution)/shard_map/ppermute | solution.py:44
  57.7 7.7 %collective-permute-start.16 = (f32[72,512]{1,0:T(8,128)S(1)}, f32[72,512]{1,0:T(8,128)S(1)}, u32[]{:S(2)}, u32[]{:S(2)}) collective-permute-start(f32[72,512]{1,0:T(8,128)S(1)} %get-tuple-element.107), channel_id=1, source_target_pairs={{0,2},{2,0},{4,6},{6,4},{8,10},{10,8},{12,14},{14,12},{16,18},{18,... | collective-permute-start | bytes 442376 | tf_op jit(solution)/shard_map/ppermute | solution.py:44
  65.4 9.5 %collective-permute-start.19 = (f32[72,512]{1,0:T(8,128)S(1)}, f32[72,512]{1,0:T(8,128)S(1)}, u32[]{:S(2)}, u32[]{:S(2)}) collective-permute-start(f32[72,512]{1,0:T(8,128)S(1)} %get-tuple-element.111.refs_0_), channel_id=1, source_target_pairs={{0,24},{2,26},{4,28},{6,30},{8,16},{10,18},{12,20},{14,22},{16,8},... | collective-permute-start | bytes 442376 | tf_op jit(solution)/shard_map/ppermute | solution.py:44
  67.5 7.4 %collective-permute-start.20 = (f32[64,512]{1,0:T(8,128)S(1)}, f32[64,512]{1,0:T(8,128)S(1)}, u32[]{:S(2)}, u32[]{:S(2)}) collective-permute-start(f32[64,512]{1,0:T(8,128)S(1)} %get-tuple-element.112.refs_2_), channel_id=1, source_target_pairs={{0,8},{2,10},{4,12},{6,14},{8,0},{10,2},{12,4},{14,6},{16,24},{18,... | collective-permute-start | bytes 393224 | tf_op jit(solution)/shard_map/ppermute | solution.py:44
  75.0 16.2 %collective-permute-start.21 = (f32[72,512]{1,0:T(8,128)S(1)}, f32[72,512]{1,0:T(8,128)S(1)}, u32[]{:S(2)}, u32[]{:S(2)}) collective-permute-start(f32[72,512]{1,0:T(8,128)S(1)} %get-tuple-element.113.refs_0_), channel_id=1, source_target_pairs={{0,8},{2,10},{4,12},{6,14},{8,0},{10,2},{12,4},{14,6},{16,24},{18,... | collective-permute-start | bytes 442376 | tf_op jit(solution)/shard_map/ppermute | solution.py:44
  75.0 16.1 %collective-permute-start.22 = (f32[64,512]{1,0:T(8,128)S(1)}, f32[64,512]{1,0:T(8,128)S(1)}, u32[]{:S(2)}, u32[]{:S(2)}) collective-permute-start(f32[64,512]{1,0:T(8,128)S(1)} %get-tuple-element.114.refs_2_), channel_id=1, source_target_pairs={{0,24},{2,26},{4,28},{6,30},{8,16},{10,18},{12,20},{14,22},{16,8},... | collective-permute-start | bytes 393224 | tf_op jit(solution)/shard_map/ppermute | solution.py:44
  84.3 6.2 %collective-permute-start.25 = (f32[32,512]{1,0:T(8,128)S(1)}, f32[32,512]{1,0:T(8,128)S(1)}, u32[]{:S(2)}, u32[]{:S(2)}) collective-permute-start(f32[32,512]{1,0:T(8,128)S(1)} %get-tuple-element.116.refs_0_), channel_id=1, source_target_pairs={{0,24},{2,26},{4,28},{6,30},{8,16},{10,18},{12,20},{14,22},{16,8},... | collective-permute-start | bytes 196616 | tf_op jit(solution)/shard_map/ppermute | solution.py:44
  97.1 9.3 %collective-permute-start.29 = (f32[256,512]{1,0:T(8,128)S(1)}, f32[256,512]{1,0:T(8,128)S(1)}, u32[]{:S(2)}, u32[]{:S(2)}) collective-permute-start(f32[256,512]{1,0:T(8,128)S(1)} %get-tuple-element.122.refs_2_.refs_8_), channel_id=1, source_target_pairs={{1,0},{0,1},{3,2},{2,3},{5,4},{4,5},{7,6},{6,7},{9,8},{8,9},{11,10... | collective-permute-start | bytes 1572872 | tf_op jit(solution)/shard_map/ppermute | solution.py:49
  97.1 8.7 %collective-permute-start.30 = (f32[128,512]{1,0:T(8,128)S(1)}, f32[128,512]{1,0:T(8,128)S(1)}, u32[]{:S(2)}, u32[]{:S(2)}) collective-permute-start(f32[128,512]{1,0:T(8,128)S(1)} %get-tuple-element.124), channel_id=1, source_target_pairs={{0,4},{2,6},{4,0},{6,2},{8,12},{10,14},{12,8},{14,10},{16,20},{18,... | collective-permute-start | bytes 786440 | tf_op jit(solution)/shard_map/ppermute | solution.py:44
  97.8 8.4 %collective-permute-start.31 = (f32[128,512]{1,0:T(8,128)S(1)}, f32[128,512]{1,0:T(8,128)S(1)}, u32[]{:S(2)}, u32[]{:S(2)}) collective-permute-start(f32[128,512]{1,0:T(8,128)S(1)} %get-tuple-element.125), channel_id=1, source_target_pairs={{0,2},{2,0},{4,6},{6,4},{8,10},{10,8},{12,14},{14,12},{16,18},{18,... | collective-permute-start | bytes 786440 | tf_op jit(solution)/shard_map/ppermute | solution.py:44
  105.8 7.9 %collective-permute-start.32 = (f32[128,512]{1,0:T(8,128)S(1)}, f32[128,512]{1,0:T(8,128)S(1)}, u32[]{:S(2)}, u32[]{:S(2)}) collective-permute-start(f32[128,512]{1,0:T(8,128)S(1)} %collective-permute-done.30.refs_2_), channel_id=1, source_target_pairs={{1,0},{0,1},{3,2},{2,3},{5,4},{4,5},{7,6},{6,7},{9,8},{8,9},{11,10... | collective-permute-start | bytes 786440 | tf_op jit(solution)/shard_map/ppermute | solution.py:49
  106.1 7.6 %collective-permute-start.33 = (f32[128,512]{1,0:T(8,128)S(1)}, f32[128,512]{1,0:T(8,128)S(1)}, u32[]{:S(2)}, u32[]{:S(2)}) collective-permute-start(f32[128,512]{1,0:T(8,128)S(1)} %collective-permute-done.31.refs_3_), channel_id=1, source_target_pairs={{1,0},{0,1},{3,2},{2,3},{5,4},{4,5},{7,6},{6,7},{9,8},{8,9},{11,10... | collective-permute-start | bytes 786440 | tf_op jit(solution)/shard_map/ppermute | solution.py:49
  113.4 7.7 %collective-permute-start.35 = (f32[256,512]{1,0:T(8,128)S(1)}, f32[256,512]{1,0:T(8,128)S(1)}, u32[]{:S(2)}, u32[]{:S(2)}) collective-permute-start(f32[256,512]{1,0:T(8,128)S(1)} %get-tuple-element.135), channel_id=1, source_target_pairs={{1,0},{0,1},{3,2},{2,3},{5,4},{4,5},{7,6},{6,7},{9,8},{8,9},{11,10... | collective-permute-start | bytes 1572872 | tf_op jit(solution)/shard_map/ppermute | solution.py:49
  121.1 8.6 %collective-permute-start.36 = (f32[128,512]{1,0:T(8,128)S(1)}, f32[128,512]{1,0:T(8,128)S(1)}, u32[]{:S(2)}, u32[]{:S(2)}) collective-permute-start(f32[128,512]{1,0:T(8,128)S(1)} %get-tuple-element.136), channel_id=1, source_target_pairs={{0,4},{2,6},{4,0},{6,2},{8,12},{10,14},{12,8},{14,10},{16,20},{18,... | collective-permute-start | bytes 786440 | tf_op jit(solution)/shard_map/ppermute | solution.py:44
  122.4 8.4 %collective-permute-start.37 = (f32[128,512]{1,0:T(8,128)S(1)}, f32[128,512]{1,0:T(8,128)S(1)}, u32[]{:S(2)}, u32[]{:S(2)}) collective-permute-start(f32[128,512]{1,0:T(8,128)S(1)} %get-tuple-element.137), channel_id=1, source_target_pairs={{0,2},{2,0},{4,6},{6,4},{8,10},{10,8},{12,14},{14,12},{16,18},{18,... | collective-permute-start | bytes 786440 | tf_op jit(solution)/shard_map/ppermute | solution.py:44
  131.0 6.7 %collective-permute-start.39 = (f32[72,512]{1,0:T(8,128)S(1)}, f32[72,512]{1,0:T(8,128)S(1)}, u32[]{:S(2)}, u32[]{:S(2)}) collective-permute-start(f32[72,512]{1,0:T(8,128)S(1)} %get-tuple-element.140), channel_id=1, source_target_pairs={{0,2},{2,0},{4,6},{6,4},{8,10},{10,8},{12,14},{14,12},{16,18},{18,... | collective-permute-start | bytes 442376 | tf_op jit(solution)/shard_map/ppermute | solution.py:44
  137.9 7.5 %collective-permute-start.42 = (f32[40,512]{1,0:T(8,128)S(1)}, f32[40,512]{1,0:T(8,128)S(1)}, u32[]{:S(2)}, u32[]{:S(2)}) collective-permute-start(f32[40,512]{1,0:T(8,128)S(1)} %get-tuple-element.146), channel_id=1, source_target_pairs={{0,24},{2,26},{4,28},{6,30},{8,16},{10,18},{12,20},{14,22},{16,8},... | collective-permute-start | bytes 245768 | tf_op jit(solution)/shard_map/ppermute | solution.py:44
  (28 other events, 147.9 us)

commit v3 on v2

--- a/solution.py
+++ b/solution.py
@@ -1,4 +1,3 @@
-import functools
 import math
 
 import jax
@@ -8,6 +7,7 @@
 from jax.experimental.pallas import tpu as pltpu
 from jax.sharding import PartitionSpec as P
 
+
 F32, BF16 = jnp.float32, jnp.bfloat16
 LIMIT = 12 * 1024 * 1024
 X, Y = 1, 2
@@ -21,7 +21,7 @@
 
 def streams(count):
     deep = deep_masks(count)
-    return deep + [X, Y], deep[::-1] + [Y, X]
+    return deep + [X, Y], deep + [Y, X]
 
 
 def offsets(masks):
@@ -155,7 +155,7 @@
             scratch_shapes=[pltpu.VMEM((m, m), F32)],
         ),
         out_shape=[array(pairs, 2, m, m, kind=BF16)] * 4 + [array(EDGE, m)],
-        compiler_params=pltpu.CompilerParams(vmem_limit_bytes=2 * LIMIT),
+        compiler_params=pltpu.CompilerParams(vmem_limit_bytes=10 * LIMIT // 3),
         cost_estimate=pl.CostEstimate(flops=pairs * m * m * 1500, bytes_accessed=24 * pairs * m * m, transcendentals=0),
     )(me, left_ops, right_ops, block)
 
@@ -164,24 +164,26 @@
     return jnp.where(charge == 1, 0, 1 if sectors == 2 else jnp.where(charge == 0, 1, 2))
 
 
-def double(a, b, masks_a, masks_b):
-    for mask_a, mask_b in zip(masks_a, masks_b):
-        more_a, more_b = swap(a, mask_a), swap(b, mask_b)
-        rows, m = a.shape
-
-        def body(_, inputs, outs, scratch):
-            for (low, high), out in zip(inputs, outs):
-                out[:rows, :] = low[...]
-                out[rows:, :] = high[...]
-
-        a, b = kernel_call(body, [array(2 * rows, m)] * 2, [a, more_a], [b, more_b])
-    return a, b
+def double(block, masks):
+    for mask in masks:
+        more = swap(block, mask)
+        rows, m = block.shape[0] // 2, block.shape[1]
+
+        def meet_column(_, inputs, outs, scratch):
+            (low, high), (out,) = inputs[0], outs
+            for part in (0, 1):
+                span = slice(part * rows, (part + 1) * rows)
+                out[2 * part * rows : (2 * part + 1) * rows, :] = low[span, :]
+                out[(2 * part + 1) * rows : (2 * part + 2) * rows, :] = high[span, :]
+
+        (block,) = kernel_call(meet_column, [array(4 * rows, m)], [block, more])
+    return block
 
 
 def sigma_apply(column_a, column_b, ops, scalars, edge):
     left, left_t, right, right_t = ops
     pairs, m = left.shape[0], left.shape[2]
-    count, sectors = lax.axis_size("pair"), lax.axis_size("sector")
+    sectors = lax.axis_size("sector")
     blocks = min(sectors, 3)
     half, quarter, eighth = m // 2, m // 4, m // 8
     rows_of = array(half, m)
@@ -217,8 +219,8 @@
     early, a, b = kernel_call(
         join, [rows_of, array(quarter, m), array(quarter, m)], [column_a, more_a], [column_b, more_b]
     )
+    early_others = neighbours(early)
     late = [swap(a, Y), swap(b, X)]
-    early_others = neighbours(early)
 
     def first_inner(fixed, inputs, outs, scratch):
         (own, *others), rights, rights_t = inputs
@@ -333,106 +335,97 @@
     def second_sum(_, inputs, outs, scratch):
         (a_stay, a_got), (b_stay, b_got), (edge_ref, corner_ref) = inputs
         outs[0][:eighth, :] = a_stay[...] + a_got[:eighth, :]
-        outs[0][eighth:, :] = edge_ref[...] + a_got[eighth:, :] + b_got[eighth:, :] + corner_ref[...]
-        outs[1][...] = b_stay[...] + b_got[:eighth, :]
-
-    return kernel_call(
-        second_sum, [array(eighth + EDGE, m), array(eighth, m)], [stay_a, got_a], [stay_b, got_b], [edge, corner]
-    )
+        outs[0][eighth:quarter, :] = b_stay[...] + b_got[:eighth, :]
+        outs[0][quarter:, :] = edge_ref[...] + a_got[eighth:, :] + b_got[eighth:, :] + corner_ref[...]
+
+    return kernel_call(second_sum, [array(quarter + EDGE, m)], [stay_a, got_a], [stay_b, got_b], [edge, corner])[0]
 
 
 def turned(value, slots, mask, rows):
-    parts = [value[slots.index(slot ^ mask) * rows :][:rows] for slot in slots]
-    rest = value[len(slots) * rows :]
-    return jnp.concatenate(parts + ([rest] if rest.shape[0] else []), axis=0)
+    size = len(slots) * rows
+    parts = [
+        value[part * size + slots.index(slot ^ mask) * rows :][:rows] for part in (0, 1) for slot in slots
+    ]
+    return jnp.concatenate(parts + [value[2 * size :]], axis=0)
 
 
 def per_device(wavefunction, preconditioner, left_ops, right_ops, charges, coupling):
     vector, divisor = wavefunction[0], preconditioner[0]
     count = lax.axis_size("pair")
     deep = deep_masks(count)
+    slots = offsets(deep)
     rows, m = vector.shape[0] // 2, vector.shape[1]
-    tall = rows * (count // 4)
+    tall = rows * len(slots)
     me = lax.axis_index("pair").astype(jnp.int32)[None]
+    scalars = (charges, coupling)
     *ops, edge = prepare(me, left_ops, right_ops, vector, count)
-    scalars = (charges, coupling)
-    vector_a, vector_b = double(vector[:rows], vector[rows:], deep, deep[::-1])
-    divisor, _ = lax.optimization_barrier((divisor, vector_a))
-    divisor_a, divisor_b = double(divisor[:rows], divisor[rows:], deep, deep[::-1])
-
-    image_a, image_b = sigma_apply(vector_a, vector_b, ops, scalars, edge)
-    slots_a, slots_b = offsets(deep), offsets(deep[::-1])
-    for mask_a, mask_b in zip(deep[:0:-1], deep[:-1]):
+    column = double(vector, deep)
+    divisor = double(divisor, deep)
+
+    def part(_, inputs, outs, scratch):
+        outs[0][...] = inputs[0][0][:tall, :]
+        outs[1][...] = inputs[0][0][tall:, :]
+
+    vector_a, vector_b = kernel_call(part, [array(tall, m)] * 2, [column])
+    image = sigma_apply(vector_a, vector_b, ops, scalars, edge)
+    for mask in deep[:0:-1]:
 
         def add_columns(_, inputs, outs, scratch):
-            (a_ref, a_got), (b_ref, b_got) = inputs
-            outs[0][...] = a_ref[...] + turned(a_got[...], slots_a, mask_a, rows)
-            outs[1][...] = b_ref[...] + turned(b_got[...], slots_b, mask_b, rows)
-
-        image_a, image_b = kernel_call(
-            add_columns, [array(*image_a.shape), array(*image_b.shape)],
-            [image_a, swap(image_a, mask_a)], [image_b, swap(image_b, mask_b)],
-        )
-
-    last_a, last_b = deep[0], deep[-1]
+            own, got = inputs[0]
+            outs[0][...] = own[...] + turned(got[...], slots, mask, rows)
+
+        (image,) = kernel_call(add_columns, [array(*image.shape)], [image, swap(image, mask)])
 
     def correct(_, inputs, outs, scratch):
-        (a0, a1), (b0, b1), (wa, wb), (pa, pb) = inputs
+        own, got, w_ref, p_ref = inputs[0]
         correction_a, correction_b, image_own, sums_out, edge_out = outs
-        total_a = a0[...] + turned(a1[...], slots_a, last_a, rows)
-        total_b = b0[...] + turned(b1[...], slots_b, last_b, rows)
-        sums = total_a[tall:]
+        total = own[...] + turned(got[...], slots, deep[0], rows)
+        sums = total[2 * tall :]
         theta = sums[0:1, :] / sums[1:2, :]
-        ca = (total_a[:tall] - theta * wa[...]) / pa[...]
-        cb = (total_b - theta * wb[...]) / pb[...]
-        correction_a[...] = ca
-        correction_b[...] = cb
-        image_own[:rows, :] = total_a[:rows]
-        image_own[rows:, :] = total_b[:rows]
+        c = (total[: 2 * tall] - theta * w_ref[...]) / p_ref[...]
+        correction_a[...] = c[:tall]
+        correction_b[...] = c[tall:]
         sums_out[...] = sums
 
-        def inner(first, second):
-            return summed(first[0] * second[0], m) + summed(first[1] * second[1], m)
-
-        own_w, own_c = (wa[:rows, :], wb[:rows, :]), (ca[:rows], cb[:rows])
-        own_a = (total_a[:rows], total_b[:rows])
+        def owned(value):
+            return jnp.concatenate([value[:rows], value[tall : tall + rows]], axis=0)
+
+        own_w, own_c, own_a = owned(w_ref[...]), owned(c), owned(total)
+        image_own[...] = own_a
         edge_out[...] = tile_rows(
-            [jnp.zeros((1, m), F32), inner(own_w, own_c), inner(own_c, own_c), inner(own_a, own_c)]
+            [jnp.zeros((1, m), F32), summed(own_w * own_c, m), summed(own_c * own_c, m), summed(own_a * own_c, m)]
         )
 
     ca, cb, image_own, sums, edge = kernel_call(
         correct, [array(tall, m), array(tall, m), array(2 * rows, m), array(EDGE, m), array(EDGE, m)],
-        [image_a, swap(image_a, last_a)], [image_b, swap(image_b, last_b)], [vector_a, vector_b],
-        [divisor_a, divisor_b],
+        [image, swap(image, deep[0]), column, divisor],
     )
     own_c = (ca, cb)
-    second_a, second_b = sigma_apply(ca, cb, ops, scalars, edge)
-
-    for mask_a, mask_b in zip(deep[::-1], deep):
-        size = second_b.shape[0] // 2
+    second = sigma_apply(ca, cb, ops, scalars, edge)
+
+    for mask in deep[::-1]:
+        size = (second.shape[0] - EDGE) // 4
 
         def cut(_, inputs, outs, scratch):
-            a_ref, b_ref = inputs[0]
-            outs[0][...] = a_ref[size:, :]
-            outs[1][...] = b_ref[size:, :]
+            ref, out = inputs[0][0], outs[0]
+            out[:size, :] = ref[size : 2 * size, :]
+            out[size:, :] = ref[3 * size :, :]
 
         def meet(_, inputs, outs, scratch):
-            (a_ref, a_got), (b_ref, b_got) = inputs
-            outs[0][:size, :] = a_ref[:size, :] + a_got[:size, :]
-            outs[0][size:, :] = a_ref[2 * size :, :] + a_got[size:, :]
-            outs[1][...] = b_ref[:size, :] + b_got[...]
-
-        go_a, go_b = kernel_call(cut, [array(size + EDGE, m), array(size, m)], [second_a, second_b])
-        second_a, second_b = kernel_call(
-            meet, [array(size + EDGE, m), array(size, m)],
-            [second_a, swap(go_a, mask_a)], [second_b, swap(go_b, mask_b)],
-        )
+            (ref, got), out = inputs[0], outs[0]
+            out[:size, :] = ref[:size, :] + got[:size, :]
+            out[size : 2 * size, :] = ref[2 * size : 3 * size, :] + got[size : 2 * size, :]
+            out[2 * size :, :] = ref[4 * size :, :] + got[2 * size :, :]
+
+        shape = [array(2 * size + EDGE, m)]
+        (go,) = kernel_call(cut, shape, [second])
+        (second,) = kernel_call(meet, shape, [second, swap(go, mask)])
 
     scale = math.sqrt(lax.axis_size("sector") * count * vector.shape[0] * m)
 
     def finish(_, inputs, outs, scratch):
-        (a_ref, b_ref), (vector_ref, image_ref, ca_ref, cb_ref), (first_ref,) = inputs
-        sums = a_ref[rows:, :]
+        (second_ref,), (vector_ref, image_ref, ca_ref, cb_ref), (first_ref,) = inputs
+        sums = second_ref[2 * rows :, :]
         correlation, norm_sq = first_ref[0:1, :], first_ref[1:2, :]
         theta = correlation / norm_sq
         inverse = lax.rsqrt(norm_sq)
@@ -448,15 +441,15 @@
         size_norm = jnp.sqrt(first_weight * first_weight + second_weight * second_weight + 1e-30)
         factor_two = scale * second_weight / size_norm * factor
         factor_one = scale * first_weight / size_norm * inverse - factor_two * along
-        for at, c_ref, s_ref in ((0, ca_ref, a_ref), (rows, cb_ref, b_ref)):
+        for at, c_ref in ((0, ca_ref), (rows, cb_ref)):
             span = slice(at, at + rows)
             outs[0][span, :] = factor_one * vector_ref[span, :] + factor_two * c_ref[:rows, :]
-            outs[1][span, :] = factor_one * image_ref[span, :] + factor_two * s_ref[:rows, :]
+            outs[1][span, :] = factor_one * image_ref[span, :] + factor_two * second_ref[span, :]
         row = lax.broadcasted_iota(jnp.int32, (EDGE, m), 1)
         outs[2][...] = jnp.where(row == 0, theta, lowest)
 
     state, image, energies = kernel_call(
-        finish, [array(2 * rows, m), array(2 * rows, m), array(EDGE, m)], [second_a, second_b],
+        finish, [array(2 * rows, m), array(2 * rows, m), array(EDGE, m)], [second],
         [vector, image_own, own_c[0], own_c[1]], [sums],
     )
     return (state[None], image[None], energies[0, :2])

time: 153 us -> 151 us (0.987)
  local copies, waits for them, and re-layouts: 5.93 us -> 1.37 us
  Pallas kernels: 32.8 us -> 34.7 us
    unnamed x12 -> x10, local copies, waits for them, and re-layouts: 4.63 us -> 0.85 us
    pallas_call x1, Pallas kernels: 3.36 us -> 5.33 us  [prepare(): pl.pallas_call(kernel, grid_spec=pltpu.PrefetchScalarGridSpec(num_scalar_...]
    ppermute x34 -> x26, waiting for transfers between devices: 67.2 us -> 68.1 us  [swap(): lax.ppermute(block, 'pair', [(i, i ^ mask) for i in range(lax.axis_size('...]
    ppermute x34 -> x26, starting transfers between devices: 41.2 us -> 41.9 us  [swap(): lax.ppermute(block, 'pair', [(i, i ^ mask) for i in range(lax.axis_size('...]
    pallas_call x27 -> x28, Pallas kernels: 29.4 us -> 29.4 us  [kernel_call(): pl.pallas_call(kernel, in_specs=[pl.BlockSpec(memory_space=pltpu.SMEM)] *...]
  transfers between devices with their start and end apart: 46 -> 38, of which waited for: 25 -> 23; matrix products, arithmetic and copies ran while one was open for 0% -> 0% of each run, Pallas kernels for 21% -> 22%
where the time goes in v3:
time: 151 us
  waiting for transfers between devices  70.5 us (47%)
  starting transfers between devices  43.4 us (29%)
  Pallas kernels  34.7 us (23%)
    ppermute x26, waiting for transfers between devices, swap(): lax.ppermute(block, 'pair', [(i, i ^ mask) for i in range(lax.axis_size('...  68.1 us
    ppermute x26, starting transfers between devices, swap(): lax.ppermute(block, 'pair', [(i, i ^ mask) for i in range(lax.axis_size('...  41.9 us
    pallas_call x28, Pallas kernels, kernel_call(): pl.pallas_call(kernel, in_specs=[pl.BlockSpec(memory_space=pltpu.SMEM)] *...  29.4 us
    pallas_call x1, Pallas kernels, prepare(): pl.pallas_call(kernel, grid_spec=pltpu.PrefetchScalarGridSpec(num_scalar_...  5.33 us
  transfers between devices with their start and end apart: 38, of which 23 were waited for; matrix products, arithmetic and copies ran while one was open for 0% of the time, Pallas kernels for 22%

profile of v3, /device:TPU:0, one launch (start us, length us, event | category | flops | bytes accessed | tf_op | source)
XLA Modules:
  0.0 150.8 jit_solution(16545547237119945065)
XLA Ops:
  0.6 3.1 %collective-permute-start = (f32[32,512]{1,0:T(8,128)}, f32[32,512]{1,0:T(8,128)S(1)}, u32[]{:S(2)}, u32[]{:S(2)}) collective-permute-start(f32[32,512]{1,0:T(8,128)} %bitcast.7), channel_id=1, source_target_pairs={{0,8},{2,10},{4,12},{6,14},{8,0},{10,2},{12,4},{14,6},{16,24},{18,... | collective-permute-start | bytes 196616 | tf_op jit(solution)/shard_map/ppermute | solution.py:44
  7.1 4.1 %collective-permute-start.1 = (f32[64,512]{1,0:T(8,128)S(1)}, f32[64,512]{1,0:T(8,128)S(1)}, u32[]{:S(2)}, u32[]{:S(2)}) collective-permute-start(f32[64,512]{1,0:T(8,128)S(1)} %shard_map.85.refs_0_), channel_id=1, source_target_pairs={{0,24},{2,26},{4,28},{6,30},{8,16},{10,18},{12,20},{14,22},{16,8},... | collective-permute-start | bytes 393224 | tf_op jit(solution)/shard_map/ppermute | solution.py:44
  11.2 3.1 %collective-permute-done.1.refs_1_ = f32[64,512]{1,0:T(8,128)S(1)} collective-permute-done((f32[64,512]{1,0:T(8,128)S(1)}, f32[64,512]{1,0:T(8,128)S(1)}, u32[]{:S(2)}, u32[]{:S(2)}) %collective-permute-start.1) | collective-permute-done | bytes 131104 | tf_op jit(solution)/shard_map/ppermute | solution.py:44
  23.3 5.3 %shard_map.89 = (bf16[3,2,512,512]{3,2,1,0:T(8,128)(2,1)S(1)}, bf16[3,2,512,512]{3,2,1,0:T(8,128)(2,1)S(1)}, bf16[3,2,512,512]{3,2,1,0:T(8,128)(2,1)S(1)}, bf16[...) custom-call(s32[1]{0:T(128)} %bitcast.1.me_ref, f32[3,1,512,512]{3,2,1,0:T(8,128)} %left_ref.1, f32[3,1,512,512]{3,2,1,0:T(8,128)} %right_ref.1, ...), custom_call_target="tpu_custom_call" | custom-call | flops 1179648000 | bytes 18874368 | tf_op jit(solution)/shard_map/pallas_call | solution.py:148
  31.1 3.3 %shard_map.90 = (bf16[3,2,256,512]{3,2,1,0:T(8,128)(2,1)S(1)}, bf16[3,2,256,512]{3,2,1,0:T(8,128)(2,1)S(1)}) custom-call(s32[3]{0:T(128)S(1)} %copy-done.3, s32[1,3]{1,0:T(1,128)S(1)} %copy-done.4, f32[256,512]{1,0:T(8,128)S(1)} %get-tuple-element.62.refs_2_.refs_8_, f32[256,512]{1,0:T(8,128)S(1)} %collective-permute-done.4.refs_3_, ...), custom_call_target="tpu_custom_call" | custom-call | flops 2415919104 | bytes 7340032 | tf_op jit(solution)/shard_map/pallas_call | solution.py:85
  34.5 3.5 %shard_map.91 = (bf16[3,2,256,512]{3,2,1,0:T(8,128)(2,1)S(1)}, f32[256,512]{1,0:T(8,128)S(1)}, f32[256,512]{1,0:T(8,128)S(1)}) custom-call(s32[3]{0:T(128)S(1)} %copy-done.3, s32[1,3]{1,0:T(1,128)S(1)} %copy-done.4, f32[128,512]{1,0:T(8,128)S(1)} %collective-permute-done.5.refs_2_, f32[128,512]{1,0:T(8,128)S(1)} %collective-permute-done.6.refs_3_, ...), custom_call_target="tpu_custom_call" | custom-call | flops 3623878656 | bytes 8388608 | tf_op jit(solution)/shard_map/pallas_call | solution.py:85
  38.5 3.5 %shard_map.92 = (bf16[3,2,256,512]{3,2,1,0:T(8,128)(2,1)S(1)}, f32[256,512]{1,0:T(8,128)S(1)}, f32[8,512]{1,0:T(8,128)S(1)}) custom-call(s32[3]{0:T(128)S(1)} %copy-done.3, s32[1,3]{1,0:T(1,128)S(1)} %copy-done.4, f32[128,512]{1,0:T(8,128)S(1)} %collective-permute-done.5.refs_2_, f32[128,512]{1,0:T(8,128)S(1)} %collective-permute-done.6.refs_3_, ...), custom_call_target="tpu_custom_call" | custom-call | flops 3623878656 | bytes 9437184 | tf_op jit(solution)/shard_map/pallas_call | solution.py:85
  42.1 3.5 %shard_map.93 = (f32[256,512]{1,0:T(8,128)S(1)}, f32[8,512]{1,0:T(8,128)S(1)}, f32[256,512]{1,0:T(8,128)S(1)}) custom-call(s32[3]{0:T(128)S(1)} %copy-done.3, s32[1,3]{1,0:T(1,128)S(1)} %copy-done.4, bf16[3,2,256,512]{3,2,1,0:T(8,128)(2,1)S(1)} %get-tuple-element.65.refs_4_.refs_2_, bf16[3,2,256,512]{3,2,1,0:T(8,128)(2,1)S(1)} %get-tuple-element.69.refs_3_, ...), custom_call_target="tpu_custom_call" | custom-call | flops 4831838208 | bytes 13139968 | tf_op jit(solution)/shard_map/pallas_call | solution.py:85
  48.2 6.2 %collective-permute-done.11.refs_2_ = f32[128,512]{1,0:T(8,128)S(1)} collective-permute-done((f32[128,512]{1,0:T(8,128)S(1)}, f32[128,512]{1,0:T(8,128)S(1)}, u32[]{:S(2)}, u32[]{:S(2)}) %collective-permute-start.11) | collective-permute-done | bytes 262176 | tf_op jit(solution)/shard_map/ppermute | solution.py:44
  58.3 3.2 %collective-permute-done.16.refs_5_ = f32[8,512]{1,0:T(8,128)S(1)} collective-permute-done((f32[8,512]{1,0:T(8,128)S(1)}, f32[8,512]{1,0:T(8,128)S(1)}, u32[]{:S(2)}, u32[]{:S(2)}) %collective-permute-start.16) | collective-permute-done | bytes 16416 | tf_op jit(solution)/shard_map/ppermute | solution.py:44
  61.6 3.7 %collective-permute-start.17 = (f32[136,512]{1,0:T(8,128)S(1)}, f32[136,512]{1,0:T(8,128)S(1)}, u32[]{:S(2)}, u32[]{:S(2)}) collective-permute-start(f32[136,512]{1,0:T(8,128)S(1)} %shard_map.96.refs_0_), channel_id=1, source_target_pairs={{0,24},{2,26},{4,28},{6,30},{8,16},{10,18},{12,20},{14,22},{16,8},... | collective-permute-start | bytes 835592 | tf_op jit(solution)/shard_map/ppermute | solution.py:44
  65.3 4.8 %collective-permute-done.17.refs_1_ = f32[136,512]{1,0:T(8,128)S(1)} collective-permute-done((f32[136,512]{1,0:T(8,128)S(1)}, f32[136,512]{1,0:T(8,128)S(1)}, u32[]{:S(2)}, u32[]{:S(2)}) %collective-permute-start.17) | collective-permute-done | bytes 278560 | tf_op jit(solution)/shard_map/ppermute | solution.py:44
  70.1 6.0 %collective-permute-start.18 = (f32[136,512]{1,0:T(8,128)S(1)}, f32[136,512]{1,0:T(8,128)S(1)}, u32[]{:S(2)}, u32[]{:S(2)}) collective-permute-start(f32[136,512]{1,0:T(8,128)S(1)} %shard_map.97.refs_0_), channel_id=1, source_target_pairs={{0,8},{2,10},{4,12},{6,14},{8,0},{10,2},{12,4},{14,6},{16,24},{18,... | collective-permute-start | bytes 835592 | tf_op jit(solution)/shard_map/ppermute | solution.py:44
  76.2 7.7 %collective-permute-done.19.refs_1_ = f32[32,512]{1,0:T(8,128)S(1)} collective-permute-done((f32[32,512]{1,0:T(8,128)S(1)}, f32[32,512]{1,0:T(8,128)S(1)}, u32[]{:S(2)}, u32[]{:S(2)}) %collective-permute-start.19) | collective-permute-done | bytes 65568 | tf_op jit(solution)/shard_map/ppermute | solution.py:44
  85.7 5.1 %collective-permute-done.20.refs_1_ = f32[64,512]{1,0:T(8,128)S(1)} collective-permute-done((f32[64,512]{1,0:T(8,128)S(1)}, f32[64,512]{1,0:T(8,128)S(1)}, u32[]{:S(2)}, u32[]{:S(2)}) %collective-permute-start.20) | collective-permute-done | bytes 131104 | tf_op jit(solution)/shard_map/ppermute | solution.py:44
  99.3 7.0 %collective-permute-done.24.refs_2_ = f32[128,512]{1,0:T(8,128)S(1)} collective-permute-done((f32[128,512]{1,0:T(8,128)S(1)}, f32[128,512]{1,0:T(8,128)S(1)}, u32[]{:S(2)}, u32[]{:S(2)}) %collective-permute-start.24) | collective-permute-done | bytes 262176 | tf_op jit(solution)/shard_map/ppermute | solution.py:44
  107.1 3.3 %shard_map.102 = (bf16[3,2,256,512]{3,2,1,0:T(8,128)(2,1)S(1)}, bf16[3,2,256,512]{3,2,1,0:T(8,128)(2,1)S(1)}) custom-call(s32[3]{0:T(128)S(1)} %copy-done.3, s32[1,3]{1,0:T(1,128)S(1)} %copy-done.4, f32[256,512]{1,0:T(8,128)S(1)} %get-tuple-element.90.refs_2_.refs_8_, f32[256,512]{1,0:T(8,128)S(1)} %collective-permute-done.23.refs_3_, ...), custom_call_target="tpu_custom_call" | custom-call | flops 2415919104 | bytes 7340032 | tf_op jit(solution)/shard_map/pallas_call | solution.py:85
  110.5 3.6 %shard_map.103 = (bf16[3,2,256,512]{3,2,1,0:T(8,128)(2,1)S(1)}, f32[256,512]{1,0:T(8,128)S(1)}, f32[256,512]{1,0:T(8,128)S(1)}) custom-call(s32[3]{0:T(128)S(1)} %copy-done.3, s32[1,3]{1,0:T(1,128)S(1)} %copy-done.4, f32[128,512]{1,0:T(8,128)S(1)} %collective-permute-done.24.refs_2_, f32[128,512]{1,0:T(8,128)S(1)} %collective-permute-done.25.refs_3_, ...), custom_call_target="tpu_custom_call" | custom-call | flops 3623878656 | bytes 8388608 | tf_op jit(solution)/shard_map/pallas_call | solution.py:85
  114.7 3.6 %shard_map.104 = (bf16[3,2,256,512]{3,2,1,0:T(8,128)(2,1)S(1)}, f32[256,512]{1,0:T(8,128)S(1)}, f32[8,512]{1,0:T(8,128)S(1)}) custom-call(s32[3]{0:T(128)S(1)} %copy-done.3, s32[1,3]{1,0:T(1,128)S(1)} %copy-done.4, f32[128,512]{1,0:T(8,128)S(1)} %collective-permute-done.24.refs_2_, f32[128,512]{1,0:T(8,128)S(1)} %collective-permute-done.25.refs_3_, ...), custom_call_target="tpu_custom_call" | custom-call | flops 3623878656 | bytes 9437184 | tf_op jit(solution)/shard_map/pallas_call | solution.py:85
  118.2 3.5 %shard_map.105 = (f32[256,512]{1,0:T(8,128)S(1)}, f32[8,512]{1,0:T(8,128)S(1)}, f32[256,512]{1,0:T(8,128)S(1)}) custom-call(s32[3]{0:T(128)S(1)} %copy-done.3, s32[1,3]{1,0:T(1,128)S(1)} %copy-done.4, bf16[3,2,256,512]{3,2,1,0:T(8,128)(2,1)S(1)} %get-tuple-element.91.refs_4_.refs_2_, bf16[3,2,256,512]{3,2,1,0:T(8,128)(2,1)S(1)} %get-tuple-element.94.refs_3_, ...), custom_call_target="tpu_custom_call" | custom-call | flops 4831838208 | bytes 13139968 | tf_op jit(solution)/shard_map/pallas_call | solution.py:85
  124.7 5.9 %collective-permute-done.30.refs_2_ = f32[128,512]{1,0:T(8,128)S(1)} collective-permute-done((f32[128,512]{1,0:T(8,128)S(1)}, f32[128,512]{1,0:T(8,128)S(1)}, u32[]{:S(2)}, u32[]{:S(2)}) %collective-permute-start.30) | collective-permute-done | bytes 262176 | tf_op jit(solution)/shard_map/ppermute | solution.py:44
  135.0 2.8 %collective-permute-done.35.refs_5_ = f32[8,512]{1,0:T(8,128)S(1)} collective-permute-done((f32[8,512]{1,0:T(8,128)S(1)}, f32[8,512]{1,0:T(8,128)S(1)}, u32[]{:S(2)}, u32[]{:S(2)}) %collective-permute-start.35) | collective-permute-done | bytes 16416 | tf_op jit(solution)/shard_map/ppermute | solution.py:44
  139.6 5.4 %collective-permute-done.36.refs_1_ = f32[72,512]{1,0:T(8,128)S(1)} collective-permute-done((f32[72,512]{1,0:T(8,128)S(1)}, f32[72,512]{1,0:T(8,128)S(1)}, u32[]{:S(2)}, u32[]{:S(2)}) %collective-permute-start.36) | collective-permute-done | bytes 147488 | tf_op jit(solution)/shard_map/ppermute | solution.py:44
  146.6 3.0 %collective-permute-done.37.refs_1_ = f32[40,512]{1,0:T(8,128)S(1)} collective-permute-done((f32[40,512]{1,0:T(8,128)S(1)}, f32[40,512]{1,0:T(8,128)S(1)}, u32[]{:S(2)}, u32[]{:S(2)}) %collective-permute-start.37) | collective-permute-done | bytes 81952 | tf_op jit(solution)/shard_map/ppermute | solution.py:44
  (92 shorter events, 45.8 us)
Async XLA Ops:
  7.1 7.2 %collective-permute-start.1 = (f32[64,512]{1,0:T(8,128)S(1)}, f32[64,512]{1,0:T(8,128)S(1)}, u32[]{:S(2)}, u32[]{:S(2)}) collective-permute-start(f32[64,512]{1,0:T(8,128)S(1)} %shard_map.85.refs_0_), channel_id=1, source_target_pairs={{0,24},{2,26},{4,28},{6,30},{8,16},{10,18},{12,20},{14,22},{16,8},... | collective-permute-start | bytes 393224 | tf_op jit(solution)/shard_map/ppermute | solution.py:44
  21.1 10.0 %collective-permute-start.4 = (f32[256,512]{1,0:T(8,128)S(1)}, f32[256,512]{1,0:T(8,128)S(1)}, u32[]{:S(2)}, u32[]{:S(2)}) collective-permute-start(f32[256,512]{1,0:T(8,128)S(1)} %get-tuple-element.62.refs_2_.refs_8_), channel_id=1, source_target_pairs={{1,0},{0,1},{3,2},{2,3},{5,4},{4,5},{7,6},{6,7},{9,8},{8,9},{11,10... | collective-permute-start | bytes 1572872 | tf_op jit(solution)/shard_map/ppermute | solution.py:49
  21.2 8.7 %collective-permute-start.5 = (f32[128,512]{1,0:T(8,128)S(1)}, f32[128,512]{1,0:T(8,128)S(1)}, u32[]{:S(2)}, u32[]{:S(2)}) collective-permute-start(f32[128,512]{1,0:T(8,128)S(1)} %get-tuple-element.66), channel_id=1, source_target_pairs={{0,4},{2,6},{4,0},{6,2},{8,12},{10,14},{12,8},{14,10},{16,20},{18,... | collective-permute-start | bytes 786440 | tf_op jit(solution)/shard_map/ppermute | solution.py:44
  22.7 8.4 %collective-permute-start.6 = (f32[128,512]{1,0:T(8,128)S(1)}, f32[128,512]{1,0:T(8,128)S(1)}, u32[]{:S(2)}, u32[]{:S(2)}) collective-permute-start(f32[128,512]{1,0:T(8,128)S(1)} %get-tuple-element.67), channel_id=1, source_target_pairs={{0,2},{2,0},{4,6},{6,4},{8,10},{10,8},{12,14},{14,12},{16,18},{18,... | collective-permute-start | bytes 786440 | tf_op jit(solution)/shard_map/ppermute | solution.py:44
  29.9 8.6 %collective-permute-start.7 = (f32[128,512]{1,0:T(8,128)S(1)}, f32[128,512]{1,0:T(8,128)S(1)}, u32[]{:S(2)}, u32[]{:S(2)}) collective-permute-start(f32[128,512]{1,0:T(8,128)S(1)} %collective-permute-done.5.refs_2_), channel_id=1, source_target_pairs={{1,0},{0,1},{3,2},{2,3},{5,4},{4,5},{7,6},{6,7},{9,8},{8,9},{11,10... | collective-permute-start | bytes 786440 | tf_op jit(solution)/shard_map/ppermute | solution.py:49
  31.1 7.4 %collective-permute-start.8 = (f32[128,512]{1,0:T(8,128)S(1)}, f32[128,512]{1,0:T(8,128)S(1)}, u32[]{:S(2)}, u32[]{:S(2)}) collective-permute-start(f32[128,512]{1,0:T(8,128)S(1)} %collective-permute-done.6.refs_3_), channel_id=1, source_target_pairs={{1,0},{0,1},{3,2},{2,3},{5,4},{4,5},{7,6},{6,7},{9,8},{8,9},{11,10... | collective-permute-start | bytes 786440 | tf_op jit(solution)/shard_map/ppermute | solution.py:49
  37.9 7.7 %collective-permute-start.10 = (f32[256,512]{1,0:T(8,128)S(1)}, f32[256,512]{1,0:T(8,128)S(1)}, u32[]{:S(2)}, u32[]{:S(2)}) collective-permute-start(f32[256,512]{1,0:T(8,128)S(1)} %get-tuple-element.79), channel_id=1, source_target_pairs={{1,0},{0,1},{3,2},{2,3},{5,4},{4,5},{7,6},{6,7},{9,8},{8,9},{11,10... | collective-permute-start | bytes 1572872 | tf_op jit(solution)/shard_map/ppermute | solution.py:49
  45.7 8.8 %collective-permute-start.11 = (f32[128,512]{1,0:T(8,128)S(1)}, f32[128,512]{1,0:T(8,128)S(1)}, u32[]{:S(2)}, u32[]{:S(2)}) collective-permute-start(f32[128,512]{1,0:T(8,128)S(1)} %get-tuple-element.80), channel_id=1, source_target_pairs={{0,4},{2,6},{4,0},{6,2},{8,12},{10,14},{12,8},{14,10},{16,20},{18,... | collective-permute-start | bytes 786440 | tf_op jit(solution)/shard_map/ppermute | solution.py:44
  46.5 8.2 %collective-permute-start.12 = (f32[128,512]{1,0:T(8,128)S(1)}, f32[128,512]{1,0:T(8,128)S(1)}, u32[]{:S(2)}, u32[]{:S(2)}) collective-permute-start(f32[128,512]{1,0:T(8,128)S(1)} %get-tuple-element.81), channel_id=1, source_target_pairs={{0,2},{2,0},{4,6},{6,4},{8,10},{10,8},{12,14},{14,12},{16,18},{18,... | collective-permute-start | bytes 786440 | tf_op jit(solution)/shard_map/ppermute | solution.py:44
  54.8 6.8 %collective-permute-start.14 = (f32[72,512]{1,0:T(8,128)S(1)}, f32[72,512]{1,0:T(8,128)S(1)}, u32[]{:S(2)}, u32[]{:S(2)}) collective-permute-start(f32[72,512]{1,0:T(8,128)S(1)} %get-tuple-element.84), channel_id=1, source_target_pairs={{0,2},{2,0},{4,6},{6,4},{8,10},{10,8},{12,14},{14,12},{16,18},{18,... | collective-permute-start | bytes 442376 | tf_op jit(solution)/shard_map/ppermute | solution.py:44
  61.6 8.5 %collective-permute-start.17 = (f32[136,512]{1,0:T(8,128)S(1)}, f32[136,512]{1,0:T(8,128)S(1)}, u32[]{:S(2)}, u32[]{:S(2)}) collective-permute-start(f32[136,512]{1,0:T(8,128)S(1)} %shard_map.96.refs_0_), channel_id=1, source_target_pairs={{0,24},{2,26},{4,28},{6,30},{8,16},{10,18},{12,20},{14,22},{16,8},... | collective-permute-start | bytes 835592 | tf_op jit(solution)/shard_map/ppermute | solution.py:44
  70.1 20.8 %collective-permute-start.18 = (f32[136,512]{1,0:T(8,128)S(1)}, f32[136,512]{1,0:T(8,128)S(1)}, u32[]{:S(2)}, u32[]{:S(2)}) collective-permute-start(f32[136,512]{1,0:T(8,128)S(1)} %shard_map.97.refs_0_), channel_id=1, source_target_pairs={{0,8},{2,10},{4,12},{6,14},{8,0},{10,2},{12,4},{14,6},{16,24},{18,... | collective-permute-start | bytes 835592 | tf_op jit(solution)/shard_map/ppermute | solution.py:44
  76.1 7.8 %collective-permute-start.19 = (f32[32,512]{1,0:T(8,128)S(1)}, f32[32,512]{1,0:T(8,128)S(1)}, u32[]{:S(2)}, u32[]{:S(2)}) collective-permute-start(f32[32,512]{1,0:T(8,128)S(1)} %bitcast.11), channel_id=1, source_target_pairs={{0,8},{2,10},{4,12},{6,14},{8,0},{10,2},{12,4},{14,6},{16,24},{18,... | collective-permute-start | bytes 196616 | tf_op jit(solution)/shard_map/ppermute | solution.py:44
  83.9 6.9 %collective-permute-start.20 = (f32[64,512]{1,0:T(8,128)S(1)}, f32[64,512]{1,0:T(8,128)S(1)}, u32[]{:S(2)}, u32[]{:S(2)}) collective-permute-start(f32[64,512]{1,0:T(8,128)S(1)} %shard_map.98.refs_0_), channel_id=1, source_target_pairs={{0,24},{2,26},{4,28},{6,30},{8,16},{10,18},{12,20},{14,22},{16,8},... | collective-permute-start | bytes 393224 | tf_op jit(solution)/shard_map/ppermute | solution.py:44
  97.5 9.6 %collective-permute-start.23 = (f32[256,512]{1,0:T(8,128)S(1)}, f32[256,512]{1,0:T(8,128)S(1)}, u32[]{:S(2)}, u32[]{:S(2)}) collective-permute-start(f32[256,512]{1,0:T(8,128)S(1)} %get-tuple-element.90.refs_2_.refs_8_), channel_id=1, source_target_pairs={{1,0},{0,1},{3,2},{2,3},{5,4},{4,5},{7,6},{6,7},{9,8},{8,9},{11,10... | collective-permute-start | bytes 1572872 | tf_op jit(solution)/shard_map/ppermute | solution.py:49
  97.6 8.7 %collective-permute-start.24 = (f32[128,512]{1,0:T(8,128)S(1)}, f32[128,512]{1,0:T(8,128)S(1)}, u32[]{:S(2)}, u32[]{:S(2)}) collective-permute-start(f32[128,512]{1,0:T(8,128)S(1)} %get-tuple-element.92), channel_id=1, source_target_pairs={{0,4},{2,6},{4,0},{6,2},{8,12},{10,14},{12,8},{14,10},{16,20},{18,... | collective-permute-start | bytes 786440 | tf_op jit(solution)/shard_map/ppermute | solution.py:44
  98.8 8.4 %collective-permute-start.25 = (f32[128,512]{1,0:T(8,128)S(1)}, f32[128,512]{1,0:T(8,128)S(1)}, u32[]{:S(2)}, u32[]{:S(2)}) collective-permute-start(f32[128,512]{1,0:T(8,128)S(1)} %get-tuple-element.93), channel_id=1, source_target_pairs={{0,2},{2,0},{4,6},{6,4},{8,10},{10,8},{12,14},{14,12},{16,18},{18,... | collective-permute-start | bytes 786440 | tf_op jit(solution)/shard_map/ppermute | solution.py:44
  106.3 8.3 %collective-permute-start.26 = (f32[128,512]{1,0:T(8,128)S(1)}, f32[128,512]{1,0:T(8,128)S(1)}, u32[]{:S(2)}, u32[]{:S(2)}) collective-permute-start(f32[128,512]{1,0:T(8,128)S(1)} %collective-permute-done.24.refs_2_), channel_id=1, source_target_pairs={{1,0},{0,1},{3,2},{2,3},{5,4},{4,5},{7,6},{6,7},{9,8},{8,9},{11,10... | collective-permute-start | bytes 786440 | tf_op jit(solution)/shard_map/ppermute | solution.py:49
  107.1 7.5 %collective-permute-start.27 = (f32[128,512]{1,0:T(8,128)S(1)}, f32[128,512]{1,0:T(8,128)S(1)}, u32[]{:S(2)}, u32[]{:S(2)}) collective-permute-start(f32[128,512]{1,0:T(8,128)S(1)} %collective-permute-done.25.refs_3_), channel_id=1, source_target_pairs={{1,0},{0,1},{3,2},{2,3},{5,4},{4,5},{7,6},{6,7},{9,8},{8,9},{11,10... | collective-permute-start | bytes 786440 | tf_op jit(solution)/shard_map/ppermute | solution.py:49
  114.1 7.7 %collective-permute-start.29 = (f32[256,512]{1,0:T(8,128)S(1)}, f32[256,512]{1,0:T(8,128)S(1)}, u32[]{:S(2)}, u32[]{:S(2)}) collective-permute-start(f32[256,512]{1,0:T(8,128)S(1)} %get-tuple-element.103), channel_id=1, source_target_pairs={{1,0},{0,1},{3,2},{2,3},{5,4},{4,5},{7,6},{6,7},{9,8},{8,9},{11,10... | collective-permute-start | bytes 1572872 | tf_op jit(solution)/shard_map/ppermute | solution.py:49
  121.9 8.8 %collective-permute-start.30 = (f32[128,512]{1,0:T(8,128)S(1)}, f32[128,512]{1,0:T(8,128)S(1)}, u32[]{:S(2)}, u32[]{:S(2)}) collective-permute-start(f32[128,512]{1,0:T(8,128)S(1)} %get-tuple-element.104), channel_id=1, source_target_pairs={{0,4},{2,6},{4,0},{6,2},{8,12},{10,14},{12,8},{14,10},{16,20},{18,... | collective-permute-start | bytes 786440 | tf_op jit(solution)/shard_map/ppermute | solution.py:44
  122.9 8.4 %collective-permute-start.31 = (f32[128,512]{1,0:T(8,128)S(1)}, f32[128,512]{1,0:T(8,128)S(1)}, u32[]{:S(2)}, u32[]{:S(2)}) collective-permute-start(f32[128,512]{1,0:T(8,128)S(1)} %get-tuple-element.105), channel_id=1, source_target_pairs={{0,2},{2,0},{4,6},{6,4},{8,10},{10,8},{12,14},{14,12},{16,18},{18,... | collective-permute-start | bytes 786440 | tf_op jit(solution)/shard_map/ppermute | solution.py:44
  131.4 6.3 %collective-permute-start.33 = (f32[72,512]{1,0:T(8,128)S(1)}, f32[72,512]{1,0:T(8,128)S(1)}, u32[]{:S(2)}, u32[]{:S(2)}) collective-permute-start(f32[72,512]{1,0:T(8,128)S(1)} %get-tuple-element.108), channel_id=1, source_target_pairs={{0,2},{2,0},{4,6},{6,4},{8,10},{10,8},{12,14},{14,12},{16,18},{18,... | collective-permute-start | bytes 442376 | tf_op jit(solution)/shard_map/ppermute | solution.py:44
  137.8 7.2 %collective-permute-start.36 = (f32[72,512]{1,0:T(8,128)S(1)}, f32[72,512]{1,0:T(8,128)S(1)}, u32[]{:S(2)}, u32[]{:S(2)}) collective-permute-start(f32[72,512]{1,0:T(8,128)S(1)} %shard_map.109), channel_id=1, source_target_pairs={{0,24},{2,26},{4,28},{6,30},{8,16},{10,18},{12,20},{14,22},{16,8},... | collective-permute-start | bytes 442376 | tf_op jit(solution)/shard_map/ppermute | solution.py:44
  (19 other events, 113.6 us)

commit v4 on v3

--- a/solution.py
+++ b/solution.py
@@ -71,27 +71,26 @@
     return jax.ShapeDtypeStruct(shape, kind)
 
 
-def kernel_call(body, outs, *groups, scalars=(), scratch=(), flops=0):
+def kernel_call(body, outs, *groups, scratch=(), flops=0, scalar_outs=0):
     flat = [value for group in groups for value in group]
 
     def kernel(*refs):
         refs = list(refs)
         take = lambda n: [refs.pop(0) for _ in range(n)]
-        fixed = take(len(scalars))
         inputs = [take(len(group)) for group in groups]
-        body(fixed, inputs, take(len(outs)), refs)
+        body(inputs, take(len(outs)), refs)
 
     traffic = sum(v.size * v.dtype.itemsize for v in flat)
     return pl.pallas_call(
         kernel,
-        in_specs=[pl.BlockSpec(memory_space=pltpu.SMEM)] * len(scalars)
-        + [pl.BlockSpec(memory_space=pltpu.VMEM)] * len(flat),
-        out_specs=[pl.BlockSpec(memory_space=pltpu.VMEM)] * len(outs),
+        in_specs=[pl.BlockSpec(memory_space=pltpu.VMEM)] * len(flat),
+        out_specs=[pl.BlockSpec(memory_space=pltpu.VMEM)] * (len(outs) - scalar_outs)
+        + [pl.BlockSpec(memory_space=pltpu.SMEM)] * scalar_outs,
         out_shape=list(outs),
         scratch_shapes=list(scratch),
         compiler_params=pltpu.CompilerParams(vmem_limit_bytes=LIMIT),
         cost_estimate=pl.CostEstimate(flops=max(flops, traffic), bytes_accessed=traffic, transcendentals=0),
-    )(*scalars, *flat)
+    )(*flat)
 
 
 def split(value):
@@ -120,12 +119,19 @@
     return jnp.broadcast_to(jnp.sum(value, keepdims=True), (1, width))
 
 
-def prepare(me, left_ops, right_ops, block, count):
+def block_of(charge, sectors):
+    return jnp.where(charge == 1, 0, 1 if sectors == 2 else jnp.where(charge == 0, 1, 2))
+
+
+def prepare(me, charges, coupling, left_ops, right_ops, block, count):
     pairs, _, m, _ = left_ops.shape
     rows = m // count // 2
     order = row_order(count)
-
-    def kernel(me_ref, left_ref, right_ref, block_ref, left_out, left_t_out, right_out, right_t_out, edge, held):
+    sectors = lax.axis_size("sector")
+
+    def kernel(me_ref, charges_ref, coupling_ref, left_ref, right_ref, block_ref, *refs):
+        left_out, left_t_out, right_out, right_t_out, edge, table, held = refs
+
         def reorder(value):
             held[...] = value
             parts = []
@@ -141,6 +147,13 @@
         right_out[0], right_out[1] = split(value)
         right_t_out[0], right_t_out[1] = split(value.T)
         edge[...] = tile_rows([jnp.zeros((1, m), F32), summed(block_ref[...] * block_ref[...], m)])
+        row = lax.broadcasted_iota(jnp.int32, table.shape, 0)
+        values = jnp.zeros(table.shape, jnp.int32)
+        for pair in range(pairs):
+            charge = charges_ref[pair]
+            values = jnp.where(row == 2 * pair, block_of(charge, sectors), values)
+            values = jnp.where(row == 2 * pair + 1, coupling_ref[0, charge], values)
+        table[...] = values
 
     source = pl.BlockSpec((None, None, m, m), lambda p, *_: (p, 0, 0, 0))
     target = pl.BlockSpec((None, 2, m, m), lambda p, *_: (p, 0, 0, 0))
@@ -148,20 +161,17 @@
     return pl.pallas_call(
         kernel,
         grid_spec=pltpu.PrefetchScalarGridSpec(
-            num_scalar_prefetch=1,
+            num_scalar_prefetch=3,
             grid=(pairs,),
             in_specs=[source, source, whole],
-            out_specs=[target] * 4 + [whole],
+            out_specs=[target] * 4 + [whole] * 2,
             scratch_shapes=[pltpu.VMEM((m, m), F32)],
         ),
-        out_shape=[array(pairs, 2, m, m, kind=BF16)] * 4 + [array(EDGE, m)],
+        out_shape=[array(pairs, 2, m, m, kind=BF16)] * 4
+        + [array(EDGE, m), array(-(-2 * pairs // 8) * 8, 128, kind=jnp.int32)],
         compiler_params=pltpu.CompilerParams(vmem_limit_bytes=10 * LIMIT // 3),
         cost_estimate=pl.CostEstimate(flops=pairs * m * m * 1500, bytes_accessed=24 * pairs * m * m, transcendentals=0),
-    )(me, left_ops, right_ops, block)
-
-
-def block_of(charge, sectors):
-    return jnp.where(charge == 1, 0, 1 if sectors == 2 else jnp.where(charge == 0, 1, 2))
+    )(me, charges, coupling, left_ops, right_ops, block)
 
 
 def double(block, masks):
@@ -169,7 +179,7 @@
         more = swap(block, mask)
         rows, m = block.shape[0] // 2, block.shape[1]
 
-        def meet_column(_, inputs, outs, scratch):
+        def meet_column(inputs, outs, scratch):
             (low, high), (out,) = inputs[0], outs
             for part in (0, 1):
                 span = slice(part * rows, (part + 1) * rows)
@@ -180,7 +190,7 @@
     return block
 
 
-def sigma_apply(column_a, column_b, ops, scalars, edge):
+def sigma_apply(column_a, column_b, ops, table, edge):
     left, left_t, right, right_t = ops
     pairs, m = left.shape[0], left.shape[2]
     sectors = lax.axis_size("sector")
@@ -200,15 +210,15 @@
                 at += size
 
     def gains(fixed, pair):
-        charge = fixed[0][pair]
-        return block_of(charge, sectors), fixed[1][0, charge].astype(F32)
+        block = jnp.max(fixed[2 * pair : 2 * pair + 1, :])
+        return block, fixed[2 * pair + 1 : 2 * pair + 2, :1].astype(F32)
 
     def parts(ref, *index):
         return ref[index[0], 0], ref[index[0], 1]
 
     more_a, more_b = swap(column_a, X), swap(column_b, Y)
 
-    def join(_, inputs, outs, scratch):
+    def join(inputs, outs, scratch):
         both, a, b = outs
         for at, (low, high), out in ((0, inputs[0], a), (quarter, inputs[1], b)):
             out[:eighth, :] = low[...]
@@ -222,67 +232,77 @@
     early_others = neighbours(early)
     late = [swap(a, Y), swap(b, X)]
 
-    def first_inner(fixed, inputs, outs, scratch):
-        (own, *others), rights, rights_t = inputs
-        hold(scratch[0], [[own]] + [[other] for other in others])
+    def outer(ref, pair, at, start, inner):
+        rows, columns = slice(at, at + half), slice(start, start + half)
+        return dot3((ref[pair, 0, rows, columns], ref[pair, 1, rows, columns]), inner)
+
+    def first_inner(inputs, outs, scratch):
+        (own, *others), (rights,), (rights_t,), (lefts,), (lefts_t,), (fixed,) = inputs
+        z_out, y_out, back_out = outs[:3]
+        held_ref, total = scratch
+        hold(held_ref, [[own]] + [[other] for other in others])
+        total[...] = jnp.zeros_like(total)
+        back = jnp.zeros((half, m), F32)
         for pair in range(pairs):
             block, allowed = gains(fixed, pair)
-            forward = dot3(parts(scratch[0], 0), parts(rights_t[0], pair)) * allowed
-            outs[0][pair, 0], outs[0][pair, 1] = split(forward)
-            backward = dot3((scratch[0][block, 0], scratch[0][block, 1]), parts(rights[0], pair)) * allowed
-            outs[1][pair, 0], outs[1][pair, 1] = split(backward)
-
-    early_z, early_y = kernel_call(
-        first_inner, [made] * 2, [early] + early_others, [right], [right_t],
-        scalars=scalars, scratch=[held], flops=2 * cost,
+            forward = split(dot3(parts(held_ref, 0), parts(rights_t, pair)) * allowed)
+            z_out[pair, 0], z_out[pair, 1] = forward
+            total[block] = total[block] + outer(lefts, pair, half, 0, forward)
+            backward = split(dot3((held_ref[block, 0], held_ref[block, 1]), parts(rights, pair)) * allowed)
+            y_out[pair, 0], y_out[pair, 1] = backward
+            back = back + outer(lefts_t, pair, half, 0, backward)
+        back_out[...] = back
+        for block in range(blocks):
+            outs[3 + block][...] = total[block]
+
+    totals = pltpu.VMEM((blocks, half, m), F32)
+    early_z, early_y, early_back, *early_terms = kernel_call(
+        first_inner, [made] * 2 + [rows_of] * (1 + blocks), [early] + early_others, [right], [right_t], [left],
+        [left_t], [table], scratch=[held, totals], flops=3 * cost,
     )
     late_others = [neighbours(piece) for piece in late]
     late_others = [[late_others[q][b] for q in range(2)] for b in range(blocks - 1)]
 
-    def outer(ref, pair, at, first, second):
-        rows = slice(at, at + half)
-        total = dot3((ref[pair, 0, rows, :half], ref[pair, 1, rows, :half]), first)
-        return total + dot3((ref[pair, 0, rows, half:], ref[pair, 1, rows, half:]), second)
-
-    def forward_late(fixed, inputs, outs, scratch):
-        own, (early_ref,), (rights_t,), (lefts,) = inputs
-        z_out, total = outs[0], scratch[1]
-        hold(scratch[0], [own])
-        total[...] = jnp.zeros_like(total)
+    def forward_late(inputs, outs, scratch):
+        own, terms, (rights_t,), (lefts,), (fixed,) = inputs
+        z_out, (held_ref, total) = outs[0], scratch
+        hold(held_ref, [own])
+        for block in range(blocks):
+            total[block] = terms[block][...]
         for pair in range(pairs):
             block, allowed = gains(fixed, pair)
-            inner = split(dot3(parts(scratch[0], 0), parts(rights_t, pair)) * allowed)
+            inner = split(dot3(parts(held_ref, 0), parts(rights_t, pair)) * allowed)
             z_out[pair, 0], z_out[pair, 1] = inner
-            total[block] = total[block] + outer(lefts, pair, half, parts(early_ref, pair), inner)
+            total[block] = total[block] + outer(lefts, pair, half, half, inner)
         for block in range(blocks):
             outs[1 + block][...] = total[block]
 
     late_z, own_sent, *aimed = kernel_call(
-        forward_late, [made] + [rows_of] * blocks, late, [early_z], [right_t], [left],
-        scalars=scalars, scratch=[held, pltpu.VMEM((blocks, half, m), F32)], flops=3 * cost,
+        forward_late, [made] + [rows_of] * blocks, late, early_terms, [right_t], [left], [table],
+        scratch=[held, totals], flops=2 * cost,
     )
     aimed_sent = to_neighbours(aimed)
 
-    def backward_late(fixed, inputs, outs, scratch):
-        groups, (early_ref,), (rights,), (lefts_t,), (base,) = inputs
+    def backward_late(inputs, outs, scratch):
+        groups, (rights,), (lefts_t,), (base, back_ref), (fixed,) = inputs
         y_out, sent, product = outs
         hold(scratch[0], [groups[2 * block : 2 * block + 2] for block in range(blocks)])
-        total = jnp.zeros((half, m), F32)
+        total = back_ref[...]
         for pair in range(pairs):
             block, allowed = gains(fixed, pair)
             inner = split(dot3((scratch[0][block, 0], scratch[0][block, 1]), parts(rights, pair)) * allowed)
             y_out[pair, 0], y_out[pair, 1] = inner
-            total = total + outer(lefts_t, pair, half, parts(early_ref, pair), inner)
+            total = total + outer(lefts_t, pair, half, half, inner)
         sent[...] = total + base[...]
         own = jnp.concatenate([groups[0][...], groups[1][...]], axis=0)
         product[...] = jnp.broadcast_to(summed(own * total, m), (EDGE, m))
 
     late_y, own_sent, product = kernel_call(
-        backward_late, [made, rows_of, array(EDGE, m)], late + sum(late_others, []), [early_y], [right], [left_t],
-        [own_sent], scalars=scalars, scratch=[held], flops=3 * cost,
-    )
-
-    def add_sent(_, inputs, outs, scratch):
+        backward_late, [made, rows_of, array(EDGE, m)], late + sum(late_others, []), [right], [left_t],
+        [own_sent, early_back], [table], scratch=[held], flops=2 * cost,
+    )
+
+    def add_sent(inputs, outs, scratch):
         value = sum(ref[...] for ref in inputs[0])
         outs[0][...] = value[:quarter]
         outs[1][...] = value[quarter:]
@@ -290,18 +310,20 @@
     sent_a, sent_b = kernel_call(add_sent, [array(quarter, m)] * 2, [own_sent] + aimed_sent)
     got_a, got_b = swap(sent_a, Y), swap(sent_b, X)
 
-    def keep(fixed, inputs, outs, scratch):
-        (z0, z1), (y0, y1), (lefts,), (lefts_t,), (own, product_ref, edge_ref) = inputs
+    def keep(inputs, outs, scratch):
+        (z0, z1), (y0, y1), (lefts,), (lefts_t,), (own, product_ref, edge_ref), (fixed,) = inputs
         total = scratch[0]
         total[...] = jnp.zeros_like(total)
         back = jnp.zeros((half, m), F32)
         for pair in range(pairs):
             block, _ = gains(fixed, pair)
-            total[block] = total[block] + outer(lefts, pair, 0, parts(z0, pair), parts(z1, pair))
+            term = outer(lefts, pair, 0, 0, parts(z0, pair)) + outer(lefts, pair, 0, half, parts(z1, pair))
+            total[block] = total[block] + term
         for block in range(1, blocks):
             outs[1 + block][...] = total[block]
         for pair in range(pairs):
-            back = back + outer(lefts_t, pair, 0, parts(y0, pair), parts(y1, pair))
+            back = back + outer(lefts_t, pair, 0, 0, parts(y0, pair))
+            back = back + outer(lefts_t, pair, 0, half, parts(y1, pair))
         outs[0][...] = total[0] + back
         product_sum = 2.0 * (summed(own[...] * back, m) + product_ref[:1, :])
         row = lax.broadcasted_iota(jnp.int32, (EDGE, m), 0)
@@ -309,13 +331,13 @@
 
     own_kept, edge, *aimed = kernel_call(
         keep, [rows_of, array(EDGE, m)] + [rows_of] * (blocks - 1), [early_z, late_z], [early_y, late_y], [left],
-        [left_t], [early, product, edge],
-        scalars=scalars, scratch=[pltpu.VMEM((blocks, half, m), F32)], flops=4 * cost,
+        [left_t], [early, product, edge], [table],
+        scratch=[totals], flops=2 * cost,
     )
     aimed_kept = to_neighbours(aimed)
     edges = over_sectors(edge)
 
-    def first_sum(_, inputs, outs, scratch):
+    def first_sum(inputs, outs, scratch):
         kept, (a_ref, b_ref), edge_refs = inputs
         value = sum(ref[...] for ref in kept)
         edge_sum = sum(ref[...] for ref in edge_refs)
@@ -332,7 +354,7 @@
     )
     got_a, got_b, corner = swap(go_a, X), swap(go_b, Y), swap(edge, X | Y)
 
-    def second_sum(_, inputs, outs, scratch):
+    def second_sum(inputs, outs, scratch):
         (a_stay, a_got), (b_stay, b_got), (edge_ref, corner_ref) = inputs
         outs[0][:eighth, :] = a_stay[...] + a_got[:eighth, :]
         outs[0][eighth:quarter, :] = b_stay[...] + b_got[:eighth, :]
@@ -357,26 +379,30 @@
     rows, m = vector.shape[0] // 2, vector.shape[1]
     tall = rows * len(slots)
     me = lax.axis_index("pair").astype(jnp.int32)[None]
-    scalars = (charges, coupling)
-    *ops, edge = prepare(me, left_ops, right_ops, vector, count)
+
+    def load(inputs, outs, scratch):
+        outs[0][...] = inputs[0][0][...]
+
+    (vector,) = kernel_call(load, [array(2 * rows, m)], [vector])
+    *ops, edge, table = prepare(me, charges, coupling, left_ops, right_ops, vector, count)
     column = double(vector, deep)
     divisor = double(divisor, deep)
 
-    def part(_, inputs, outs, scratch):
+    def part(inputs, outs, scratch):
         outs[0][...] = inputs[0][0][:tall, :]
         outs[1][...] = inputs[0][0][tall:, :]
 
     vector_a, vector_b = kernel_call(part, [array(tall, m)] * 2, [column])
-    image = sigma_apply(vector_a, vector_b, ops, scalars, edge)
+    image = sigma_apply(vector_a, vector_b, ops, table, edge)
     for mask in deep[:0:-1]:
 
-        def add_columns(_, inputs, outs, scratch):
+        def add_columns(inputs, outs, scratch):
             own, got = inputs[0]
             outs[0][...] = own[...] + turned(got[...], slots, mask, rows)
 
         (image,) = kernel_call(add_columns, [array(*image.shape)], [image, swap(image, mask)])
 
-    def correct(_, inputs, outs, scratch):
+    def correct(inputs, outs, scratch):
         own, got, w_ref, p_ref = inputs[0]
         correction_a, correction_b, image_own, sums_out, edge_out = outs
         total = own[...] + turned(got[...], slots, deep[0], rows)
@@ -401,17 +427,17 @@
         [image, swap(image, deep[0]), column, divisor],
     )
     own_c = (ca, cb)
-    second = sigma_apply(ca, cb, ops, scalars, edge)
+    second = sigma_apply(ca, cb, ops, table, edge)
 
     for mask in deep[::-1]:
         size = (second.shape[0] - EDGE) // 4
 
-        def cut(_, inputs, outs, scratch):
+        def cut(inputs, outs, scratch):
             ref, out = inputs[0][0], outs[0]
             out[:size, :] = ref[size : 2 * size, :]
             out[size:, :] = ref[3 * size :, :]
 
-        def meet(_, inputs, outs, scratch):
+        def meet(inputs, outs, scratch):
             (ref, got), out = inputs[0], outs[0]
             out[:size, :] = ref[:size, :] + got[:size, :]
             out[size : 2 * size, :] = ref[2 * size : 3 * size, :] + got[size : 2 * size, :]
@@ -423,7 +449,7 @@
 
     scale = math.sqrt(lax.axis_size("sector") * count * vector.shape[0] * m)
 
-    def finish(_, inputs, outs, scratch):
+    def finish(inputs, outs, scratch):
         (second_ref,), (vector_ref, image_ref, ca_ref, cb_ref), (first_ref,) = inputs
         sums = second_ref[2 * rows :, :]
         correlation, norm_sq = first_ref[0:1, :], first_ref[1:2, :]
@@ -445,14 +471,14 @@
             span = slice(at, at + rows)
             outs[0][span, :] = factor_one * vector_ref[span, :] + factor_two * c_ref[:rows, :]
             outs[1][span, :] = factor_one * image_ref[span, :] + factor_two * second_ref[span, :]
-        row = lax.broadcasted_iota(jnp.int32, (EDGE, m), 1)
-        outs[2][...] = jnp.where(row == 0, theta, lowest)
+        outs[2][0] = jnp.max(theta)
+        outs[2][1] = jnp.max(lowest)
 
     state, image, energies = kernel_call(
-        finish, [array(2 * rows, m), array(2 * rows, m), array(EDGE, m)], [second],
-        [vector, image_own, own_c[0], own_c[1]], [sums],
-    )
-    return (state[None], image[None], energies[0, :2])
+        finish, [array(2 * rows, m), array(2 * rows, m), array(2)], [second],
+        [vector, image_own, own_c[0], own_c[1]], [sums], scalar_outs=1,
+    )
+    return (state[None], image[None], energies)
 
 
 def solution(mesh):

time: 151 us -> 150 us (level)
    pallas_call x28 -> x29, Pallas kernels: 29.4 us -> 29 us  [kernel_call(): pl.pallas_call(kernel, in_specs=[pl.BlockSpec(memory_space=pltpu.VMEM)] *...]
where the time goes in v4:
time: 150 us
  waiting for transfers between devices  69.6 us (46%)
  starting transfers between devices  43.4 us (29%)
  Pallas kernels  34.9 us (23%)
    ppermute x26, waiting for transfers between devices, swap(): lax.ppermute(block, 'pair', [(i, i ^ mask) for i in range(lax.axis_size('...  67.3 us
    ppermute x26, starting transfers between devices, swap(): lax.ppermute(block, 'pair', [(i, i ^ mask) for i in range(lax.axis_size('...  41.9 us
    pallas_call x29, Pallas kernels, kernel_call(): pl.pallas_call(kernel, in_specs=[pl.BlockSpec(memory_space=pltpu.VMEM)] *...  29 us
    pallas_call x1, Pallas kernels, prepare(): pl.pallas_call(kernel, grid_spec=pltpu.PrefetchScalarGridSpec(num_scalar_...  5.86 us
  transfers between devices with their start and end apart: 38, of which 23 were waited for; matrix products, arithmetic and copies ran while one was open for 0% of the time, Pallas kernels for 22%

profile of v4, /device:TPU:0, one launch (start us, length us, event | category | flops | bytes accessed | tf_op | source)
XLA Modules:
  0.0 149.8 jit_solution(14857463504242250196)
XLA Ops:
  1.5 3.1 %collective-permute-start = (f32[32,512]{1,0:T(8,128)S(1)}, f32[32,512]{1,0:T(8,128)S(1)}, u32[]{:S(2)}, u32[]{:S(2)}) collective-permute-start(f32[32,512]{1,0:T(8,128)S(1)} %shard_map.85.refs_0_.block_ref.refs_1_), channel_id=1, source_target_pairs={{0,8},{2,10},{4,12},{6,14},{8,0},{10,2},{12,4},{14,6},{16,24},{18,... | collective-permute-start | bytes 196616 | tf_op jit(solution)/shard_map/ppermute | solution.py:44
  6.8 4.1 %collective-permute-start.1 = (f32[64,512]{1,0:T(8,128)S(1)}, f32[64,512]{1,0:T(8,128)S(1)}, u32[]{:S(2)}, u32[]{:S(2)}) collective-permute-start(f32[64,512]{1,0:T(8,128)S(1)} %shard_map.86.refs_0_), channel_id=1, source_target_pairs={{0,24},{2,26},{4,28},{6,30},{8,16},{10,18},{12,20},{14,22},{16,8},... | collective-permute-start | bytes 393224 | tf_op jit(solution)/shard_map/ppermute | solution.py:44
  10.9 3.1 %collective-permute-done.1.refs_1_ = f32[64,512]{1,0:T(8,128)S(1)} collective-permute-done((f32[64,512]{1,0:T(8,128)S(1)}, f32[64,512]{1,0:T(8,128)S(1)}, u32[]{:S(2)}, u32[]{:S(2)}) %collective-permute-start.1) | collective-permute-done | bytes 131104 | tf_op jit(solution)/shard_map/ppermute | solution.py:44
  23.0 5.9 %shard_map.90 = (bf16[3,2,512,512]{3,2,1,0:T(8,128)(2,1)S(1)}, bf16[3,2,512,512]{3,2,1,0:T(8,128)(2,1)S(1)}, bf16[3,2,512,512]{3,2,1,0:T(8,128)(2,1)S(1)}, bf16[...) custom-call(s32[1]{0:T(128)} %bitcast.1.me_ref, s32[3]{0:T(128)S(1)} %copy-done.2, ...), custom_call_target="tpu_custom_call" | custom-call | flops 1179648000 | bytes 18874368 | tf_op jit(solution)/shard_map/pallas_call | solution.py:161
  30.9 5.1 %shard_map.91 = (bf16[3,2,256,512]{3,2,1,0:T(8,128)(2,1)S(1)}, bf16[3,2,256,512]{3,2,1,0:T(8,128)(2,1)S(1)}, f32[256,512]{1,0:T(8,128)S(1)}, f32[256,512]{1,0:T(8,128)S(1)}, f32[256,512]{1,0:T(8,128)S(1)}) custom-call(f32[256,512]{1,0:T(8,128)S(1)} %get-tuple-element.69.refs_0_.refs_6_, f32[256,512]{1,0:T(8,128)S(1)} %collective-permute-done.4.refs_1_, ...), custom_call_target="tpu_custom_call" | custom-call | flops 3623878656 | bytes 13635584 | tf_op jit(solution)/shard_map/pallas_call | solution.py:84
  36.0 2.7 %shard_map.92 = (bf16[3,2,256,512]{3,2,1,0:T(8,128)(2,1)S(1)}, f32[256,512]{1,0:T(8,128)S(1)}, f32[256,512]{1,0:T(8,128)S(1)}) custom-call(f32[128,512]{1,0:T(8,128)S(1)} %collective-permute-done.5.refs_0_, f32[128,512]{1,0:T(8,128)S(1)} %collective-permute-done.6.refs_1_, f32[256,512]{1,0:T(8,128)S(1)} %get-tuple-element.78.refs_2_, ...), custom_call_target="tpu_custom_call" | custom-call | flops 2415919104 | bytes 7868416 | tf_op jit(solution)/shard_map/pallas_call | solution.py:84
  39.2 3.0 %shard_map.93 = (bf16[3,2,256,512]{3,2,1,0:T(8,128)(2,1)S(1)}, f32[256,512]{1,0:T(8,128)S(1)}, f32[8,512]{1,0:T(8,128)S(1)}) custom-call(f32[128,512]{1,0:T(8,128)S(1)} %collective-permute-done.5.refs_0_, f32[128,512]{1,0:T(8,128)S(1)} %collective-permute-done.6.refs_1_, f32[128,512]{1,0:T(8,128)S(1)} %collective-permute-done.7.refs_2_, ...), custom_call_target="tpu_custom_call" | custom-call | flops 2415919104 | bytes 8392704 | tf_op jit(solution)/shard_map/pallas_call | solution.py:84
  42.3 2.9 %shard_map.94 = (f32[256,512]{1,0:T(8,128)S(1)}, f32[8,512]{1,0:T(8,128)S(1)}, f32[256,512]{1,0:T(8,128)S(1)}) custom-call(bf16[3,2,256,512]{3,2,1,0:T(8,128)(2,1)S(1)} %get-tuple-element.75.refs_0_, bf16[3,2,256,512]{3,2,1,0:T(8,128)(2,1)S(1)} %get-tuple-element.80.refs_1_, bf16[3,2,256,512]{3,2,1,0:T(8,128)(2,1)S(1)} %get-tuple-element.81.refs_2_, ...), custom_call_target="tpu_custom_call" | custom-call | flops 2415919104 | bytes 13144064 | tf_op jit(solution)/shard_map/pallas_call | solution.py:84
  47.8 6.2 %collective-permute-done.11.refs_2_ = f32[128,512]{1,0:T(8,128)S(1)} collective-permute-done((f32[128,512]{1,0:T(8,128)S(1)}, f32[128,512]{1,0:T(8,128)S(1)}, u32[]{:S(2)}, u32[]{:S(2)}) %collective-permute-start.11) | collective-permute-done | bytes 262176 | tf_op jit(solution)/shard_map/ppermute | solution.py:44
  57.9 3.2 %collective-permute-done.16.refs_5_ = f32[8,512]{1,0:T(8,128)S(1)} collective-permute-done((f32[8,512]{1,0:T(8,128)S(1)}, f32[8,512]{1,0:T(8,128)S(1)}, u32[]{:S(2)}, u32[]{:S(2)}) %collective-permute-start.16) | collective-permute-done | bytes 16416 | tf_op jit(solution)/shard_map/ppermute | solution.py:44
  61.2 3.7 %collective-permute-start.17 = (f32[136,512]{1,0:T(8,128)S(1)}, f32[136,512]{1,0:T(8,128)S(1)}, u32[]{:S(2)}, u32[]{:S(2)}) collective-permute-start(f32[136,512]{1,0:T(8,128)S(1)} %shard_map.97.refs_0_), channel_id=1, source_target_pairs={{0,24},{2,26},{4,28},{6,30},{8,16},{10,18},{12,20},{14,22},{16,8},... | collective-permute-start | bytes 835592 | tf_op jit(solution)/shard_map/ppermute | solution.py:44
  64.9 4.8 %collective-permute-done.17.refs_1_ = f32[136,512]{1,0:T(8,128)S(1)} collective-permute-done((f32[136,512]{1,0:T(8,128)S(1)}, f32[136,512]{1,0:T(8,128)S(1)}, u32[]{:S(2)}, u32[]{:S(2)}) %collective-permute-start.17) | collective-permute-done | bytes 278560 | tf_op jit(solution)/shard_map/ppermute | solution.py:44
  69.7 6.0 %collective-permute-start.18 = (f32[136,512]{1,0:T(8,128)S(1)}, f32[136,512]{1,0:T(8,128)S(1)}, u32[]{:S(2)}, u32[]{:S(2)}) collective-permute-start(f32[136,512]{1,0:T(8,128)S(1)} %shard_map.98.refs_0_), channel_id=1, source_target_pairs={{0,8},{2,10},{4,12},{6,14},{8,0},{10,2},{12,4},{14,6},{16,24},{18,... | collective-permute-start | bytes 835592 | tf_op jit(solution)/shard_map/ppermute | solution.py:44
  75.8 7.7 %collective-permute-done.19.refs_1_ = f32[32,512]{1,0:T(8,128)S(1)} collective-permute-done((f32[32,512]{1,0:T(8,128)S(1)}, f32[32,512]{1,0:T(8,128)S(1)}, u32[]{:S(2)}, u32[]{:S(2)}) %collective-permute-start.19) | collective-permute-done | bytes 65568 | tf_op jit(solution)/shard_map/ppermute | solution.py:44
  85.3 5.1 %collective-permute-done.20.refs_1_ = f32[64,512]{1,0:T(8,128)S(1)} collective-permute-done((f32[64,512]{1,0:T(8,128)S(1)}, f32[64,512]{1,0:T(8,128)S(1)}, u32[]{:S(2)}, u32[]{:S(2)}) %collective-permute-start.20) | collective-permute-done | bytes 131104 | tf_op jit(solution)/shard_map/ppermute | solution.py:44
  98.9 7.1 %collective-permute-done.24.refs_0_ = f32[128,512]{1,0:T(8,128)S(1)} collective-permute-done((f32[128,512]{1,0:T(8,128)S(1)}, f32[128,512]{1,0:T(8,128)S(1)}, u32[]{:S(2)}, u32[]{:S(2)}) %collective-permute-start.24) | collective-permute-done | bytes 262176 | tf_op jit(solution)/shard_map/ppermute | solution.py:44
  106.8 5.3 %shard_map.103 = (bf16[3,2,256,512]{3,2,1,0:T(8,128)(2,1)S(1)}, bf16[3,2,256,512]{3,2,1,0:T(8,128)(2,1)S(1)}, f32[256,512]{1,0:T(8,128)S(1)}, f32[256,512]{1,0:T(8,128)S(1)}, f32[256,512]{1,0:T(8,128)S(1)}) custom-call(f32[256,512]{1,0:T(8,128)S(1)} %get-tuple-element.101.refs_0_.refs_6_, f32[256,512]{1,0:T(8,128)S(1)} %collective-permute-done.23.refs_1_, ...), custom_call_target="tpu_custom_call" | custom-call | flops 3623878656 | bytes 13635584 | tf_op jit(solution)/shard_map/pallas_call | solution.py:84
  112.1 2.7 %shard_map.104 = (bf16[3,2,256,512]{3,2,1,0:T(8,128)(2,1)S(1)}, f32[256,512]{1,0:T(8,128)S(1)}, f32[256,512]{1,0:T(8,128)S(1)}) custom-call(f32[128,512]{1,0:T(8,128)S(1)} %collective-permute-done.24.refs_0_, f32[128,512]{1,0:T(8,128)S(1)} %collective-permute-done.25.refs_1_, f32[256,512]{1,0:T(8,128)S(1)} %get-tuple-element.105.refs_2_, ...), custom_call_target="tpu_custom_call" | custom-call | flops 2415919104 | bytes 7868416 | tf_op jit(solution)/shard_map/pallas_call | solution.py:84
  115.3 3.0 %shard_map.105 = (bf16[3,2,256,512]{3,2,1,0:T(8,128)(2,1)S(1)}, f32[256,512]{1,0:T(8,128)S(1)}, f32[8,512]{1,0:T(8,128)S(1)}) custom-call(f32[128,512]{1,0:T(8,128)S(1)} %collective-permute-done.24.refs_0_, f32[128,512]{1,0:T(8,128)S(1)} %collective-permute-done.25.refs_1_, f32[128,512]{1,0:T(8,128)S(1)} %collective-permute-done.26.refs_2_, ...), custom_call_target="tpu_custom_call" | custom-call | flops 2415919104 | bytes 8392704 | tf_op jit(solution)/shard_map/pallas_call | solution.py:84
  118.3 2.9 %shard_map.106 = (f32[256,512]{1,0:T(8,128)S(1)}, f32[8,512]{1,0:T(8,128)S(1)}, f32[256,512]{1,0:T(8,128)S(1)}) custom-call(bf16[3,2,256,512]{3,2,1,0:T(8,128)(2,1)S(1)} %get-tuple-element.102.refs_0_, bf16[3,2,256,512]{3,2,1,0:T(8,128)(2,1)S(1)} %get-tuple-element.107.refs_1_, bf16[3,2,256,512]{3,2,1,0:T(8,128)(2,1)S(1)} %get-tuple-element.108.refs_2_, ...), custom_call_target="tpu_custom_call" | custom-call | flops 2415919104 | bytes 13144064 | tf_op jit(solution)/shard_map/pallas_call | solution.py:84
  124.2 5.9 %collective-permute-done.30.refs_2_ = f32[128,512]{1,0:T(8,128)S(1)} collective-permute-done((f32[128,512]{1,0:T(8,128)S(1)}, f32[128,512]{1,0:T(8,128)S(1)}, u32[]{:S(2)}, u32[]{:S(2)}) %collective-permute-start.30) | collective-permute-done | bytes 262176 | tf_op jit(solution)/shard_map/ppermute | solution.py:44
  134.4 2.7 %collective-permute-done.35.refs_5_ = f32[8,512]{1,0:T(8,128)S(1)} collective-permute-done((f32[8,512]{1,0:T(8,128)S(1)}, f32[8,512]{1,0:T(8,128)S(1)}, u32[]{:S(2)}, u32[]{:S(2)}) %collective-permute-start.35) | collective-permute-done | bytes 16416 | tf_op jit(solution)/shard_map/ppermute | solution.py:44
  139.0 5.3 %collective-permute-done.36.refs_1_ = f32[72,512]{1,0:T(8,128)S(1)} collective-permute-done((f32[72,512]{1,0:T(8,128)S(1)}, f32[72,512]{1,0:T(8,128)S(1)}, u32[]{:S(2)}, u32[]{:S(2)}) %collective-permute-start.36) | collective-permute-done | bytes 147488 | tf_op jit(solution)/shard_map/ppermute | solution.py:44
  146.0 2.9 %collective-permute-done.37.refs_1_ = f32[40,512]{1,0:T(8,128)S(1)} collective-permute-done((f32[40,512]{1,0:T(8,128)S(1)}, f32[40,512]{1,0:T(8,128)S(1)}, u32[]{:S(2)}, u32[]{:S(2)}) %collective-permute-start.37) | collective-permute-done | bytes 81952 | tf_op jit(solution)/shard_map/ppermute | solution.py:44
  (90 shorter events, 44.5 us)
Async XLA Ops:
  6.8 7.2 %collective-permute-start.1 = (f32[64,512]{1,0:T(8,128)S(1)}, f32[64,512]{1,0:T(8,128)S(1)}, u32[]{:S(2)}, u32[]{:S(2)}) collective-permute-start(f32[64,512]{1,0:T(8,128)S(1)} %shard_map.86.refs_0_), channel_id=1, source_target_pairs={{0,24},{2,26},{4,28},{6,30},{8,16},{10,18},{12,20},{14,22},{16,8},... | collective-permute-start | bytes 393224 | tf_op jit(solution)/shard_map/ppermute | solution.py:44
  20.8 10.0 %collective-permute-start.4 = (f32[256,512]{1,0:T(8,128)S(1)}, f32[256,512]{1,0:T(8,128)S(1)}, u32[]{:S(2)}, u32[]{:S(2)}) collective-permute-start(f32[256,512]{1,0:T(8,128)S(1)} %get-tuple-element.69.refs_0_.refs_6_), channel_id=1, source_target_pairs={{1,0},{0,1},{3,2},{2,3},{5,4},{4,5},{7,6},{6,7},{9,8},{8,9},{11,10... | collective-permute-start | bytes 1572872 | tf_op jit(solution)/shard_map/ppermute | solution.py:49
  20.9 8.7 %collective-permute-start.5 = (f32[128,512]{1,0:T(8,128)S(1)}, f32[128,512]{1,0:T(8,128)S(1)}, u32[]{:S(2)}, u32[]{:S(2)}) collective-permute-start(f32[128,512]{1,0:T(8,128)S(1)} %get-tuple-element.76), channel_id=1, source_target_pairs={{0,4},{2,6},{4,0},{6,2},{8,12},{10,14},{12,8},{14,10},{16,20},{18,... | collective-permute-start | bytes 786440 | tf_op jit(solution)/shard_map/ppermute | solution.py:44
  22.5 8.4 %collective-permute-start.6 = (f32[128,512]{1,0:T(8,128)S(1)}, f32[128,512]{1,0:T(8,128)S(1)}, u32[]{:S(2)}, u32[]{:S(2)}) collective-permute-start(f32[128,512]{1,0:T(8,128)S(1)} %get-tuple-element.77), channel_id=1, source_target_pairs={{0,2},{2,0},{4,6},{6,4},{8,10},{10,8},{12,14},{14,12},{16,18},{18,... | collective-permute-start | bytes 786440 | tf_op jit(solution)/shard_map/ppermute | solution.py:44
  29.6 9.6 %collective-permute-start.7 = (f32[128,512]{1,0:T(8,128)S(1)}, f32[128,512]{1,0:T(8,128)S(1)}, u32[]{:S(2)}, u32[]{:S(2)}) collective-permute-start(f32[128,512]{1,0:T(8,128)S(1)} %collective-permute-done.5.refs_0_), channel_id=1, source_target_pairs={{1,0},{0,1},{3,2},{2,3},{5,4},{4,5},{7,6},{6,7},{9,8},{8,9},{11,10... | collective-permute-start | bytes 786440 | tf_op jit(solution)/shard_map/ppermute | solution.py:49
  30.9 8.4 %collective-permute-start.8 = (f32[128,512]{1,0:T(8,128)S(1)}, f32[128,512]{1,0:T(8,128)S(1)}, u32[]{:S(2)}, u32[]{:S(2)}) collective-permute-start(f32[128,512]{1,0:T(8,128)S(1)} %collective-permute-done.6.refs_1_), channel_id=1, source_target_pairs={{1,0},{0,1},{3,2},{2,3},{5,4},{4,5},{7,6},{6,7},{9,8},{8,9},{11,10... | collective-permute-start | bytes 786440 | tf_op jit(solution)/shard_map/ppermute | solution.py:49
  38.6 6.6 %collective-permute-start.10 = (f32[256,512]{1,0:T(8,128)S(1)}, f32[256,512]{1,0:T(8,128)S(1)}, u32[]{:S(2)}, u32[]{:S(2)}) collective-permute-start(f32[256,512]{1,0:T(8,128)S(1)} %get-tuple-element.90), channel_id=1, source_target_pairs={{1,0},{0,1},{3,2},{2,3},{5,4},{4,5},{7,6},{6,7},{9,8},{8,9},{11,10... | collective-permute-start | bytes 1572872 | tf_op jit(solution)/shard_map/ppermute | solution.py:49
  45.3 8.8 %collective-permute-start.11 = (f32[128,512]{1,0:T(8,128)S(1)}, f32[128,512]{1,0:T(8,128)S(1)}, u32[]{:S(2)}, u32[]{:S(2)}) collective-permute-start(f32[128,512]{1,0:T(8,128)S(1)} %get-tuple-element.91), channel_id=1, source_target_pairs={{0,4},{2,6},{4,0},{6,2},{8,12},{10,14},{12,8},{14,10},{16,20},{18,... | collective-permute-start | bytes 786440 | tf_op jit(solution)/shard_map/ppermute | solution.py:44
  46.1 8.2 %collective-permute-start.12 = (f32[128,512]{1,0:T(8,128)S(1)}, f32[128,512]{1,0:T(8,128)S(1)}, u32[]{:S(2)}, u32[]{:S(2)}) collective-permute-start(f32[128,512]{1,0:T(8,128)S(1)} %get-tuple-element.92), channel_id=1, source_target_pairs={{0,2},{2,0},{4,6},{6,4},{8,10},{10,8},{12,14},{14,12},{16,18},{18,... | collective-permute-start | bytes 786440 | tf_op jit(solution)/shard_map/ppermute | solution.py:44
  54.4 6.7 %collective-permute-start.14 = (f32[72,512]{1,0:T(8,128)S(1)}, f32[72,512]{1,0:T(8,128)S(1)}, u32[]{:S(2)}, u32[]{:S(2)}) collective-permute-start(f32[72,512]{1,0:T(8,128)S(1)} %get-tuple-element.95), channel_id=1, source_target_pairs={{0,2},{2,0},{4,6},{6,4},{8,10},{10,8},{12,14},{14,12},{16,18},{18,... | collective-permute-start | bytes 442376 | tf_op jit(solution)/shard_map/ppermute | solution.py:44
  54.8 6.3 %collective-permute-start.15 = (f32[72,512]{1,0:T(8,128)S(1)}, f32[72,512]{1,0:T(8,128)S(1)}, u32[]{:S(2)}, u32[]{:S(2)}) collective-permute-start(f32[72,512]{1,0:T(8,128)S(1)} %get-tuple-element.97), channel_id=1, source_target_pairs={{0,4},{2,6},{4,0},{6,2},{8,12},{10,14},{12,8},{14,10},{16,20},{18,... | collective-permute-start | bytes 442376 | tf_op jit(solution)/shard_map/ppermute | solution.py:44
  61.2 8.5 %collective-permute-start.17 = (f32[136,512]{1,0:T(8,128)S(1)}, f32[136,512]{1,0:T(8,128)S(1)}, u32[]{:S(2)}, u32[]{:S(2)}) collective-permute-start(f32[136,512]{1,0:T(8,128)S(1)} %shard_map.97.refs_0_), channel_id=1, source_target_pairs={{0,24},{2,26},{4,28},{6,30},{8,16},{10,18},{12,20},{14,22},{16,8},... | collective-permute-start | bytes 835592 | tf_op jit(solution)/shard_map/ppermute | solution.py:44
  69.7 20.8 %collective-permute-start.18 = (f32[136,512]{1,0:T(8,128)S(1)}, f32[136,512]{1,0:T(8,128)S(1)}, u32[]{:S(2)}, u32[]{:S(2)}) collective-permute-start(f32[136,512]{1,0:T(8,128)S(1)} %shard_map.98.refs_0_), channel_id=1, source_target_pairs={{0,8},{2,10},{4,12},{6,14},{8,0},{10,2},{12,4},{14,6},{16,24},{18,... | collective-permute-start | bytes 835592 | tf_op jit(solution)/shard_map/ppermute | solution.py:44
  75.7 7.8 %collective-permute-start.19 = (f32[32,512]{1,0:T(8,128)S(1)}, f32[32,512]{1,0:T(8,128)S(1)}, u32[]{:S(2)}, u32[]{:S(2)}) collective-permute-start(f32[32,512]{1,0:T(8,128)S(1)} %bitcast.6), channel_id=1, source_target_pairs={{0,8},{2,10},{4,12},{6,14},{8,0},{10,2},{12,4},{14,6},{16,24},{18,... | collective-permute-start | bytes 196616 | tf_op jit(solution)/shard_map/ppermute | solution.py:44
  83.5 6.9 %collective-permute-start.20 = (f32[64,512]{1,0:T(8,128)S(1)}, f32[64,512]{1,0:T(8,128)S(1)}, u32[]{:S(2)}, u32[]{:S(2)}) collective-permute-start(f32[64,512]{1,0:T(8,128)S(1)} %shard_map.99.refs_0_), channel_id=1, source_target_pairs={{0,24},{2,26},{4,28},{6,30},{8,16},{10,18},{12,20},{14,22},{16,8},... | collective-permute-start | bytes 393224 | tf_op jit(solution)/shard_map/ppermute | solution.py:44
  97.2 9.6 %collective-permute-start.23 = (f32[256,512]{1,0:T(8,128)S(1)}, f32[256,512]{1,0:T(8,128)S(1)}, u32[]{:S(2)}, u32[]{:S(2)}) collective-permute-start(f32[256,512]{1,0:T(8,128)S(1)} %get-tuple-element.101.refs_0_.refs_6_), channel_id=1, source_target_pairs={{1,0},{0,1},{3,2},{2,3},{5,4},{4,5},{7,6},{6,7},{9,8},{8,9},{11,10... | collective-permute-start | bytes 1572872 | tf_op jit(solution)/shard_map/ppermute | solution.py:49
  97.3 8.7 %collective-permute-start.24 = (f32[128,512]{1,0:T(8,128)S(1)}, f32[128,512]{1,0:T(8,128)S(1)}, u32[]{:S(2)}, u32[]{:S(2)}) collective-permute-start(f32[128,512]{1,0:T(8,128)S(1)} %get-tuple-element.103), channel_id=1, source_target_pairs={{0,4},{2,6},{4,0},{6,2},{8,12},{10,14},{12,8},{14,10},{16,20},{18,... | collective-permute-start | bytes 786440 | tf_op jit(solution)/shard_map/ppermute | solution.py:44
  98.4 8.4 %collective-permute-start.25 = (f32[128,512]{1,0:T(8,128)S(1)}, f32[128,512]{1,0:T(8,128)S(1)}, u32[]{:S(2)}, u32[]{:S(2)}) collective-permute-start(f32[128,512]{1,0:T(8,128)S(1)} %get-tuple-element.104), channel_id=1, source_target_pairs={{0,2},{2,0},{4,6},{6,4},{8,10},{10,8},{12,14},{14,12},{16,18},{18,... | collective-permute-start | bytes 786440 | tf_op jit(solution)/shard_map/ppermute | solution.py:44
  106.0 9.3 %collective-permute-start.26 = (f32[128,512]{1,0:T(8,128)S(1)}, f32[128,512]{1,0:T(8,128)S(1)}, u32[]{:S(2)}, u32[]{:S(2)}) collective-permute-start(f32[128,512]{1,0:T(8,128)S(1)} %collective-permute-done.24.refs_0_), channel_id=1, source_target_pairs={{1,0},{0,1},{3,2},{2,3},{5,4},{4,5},{7,6},{6,7},{9,8},{8,9},{11,10... | collective-permute-start | bytes 786440 | tf_op jit(solution)/shard_map/ppermute | solution.py:49
  106.8 8.5 %collective-permute-start.27 = (f32[128,512]{1,0:T(8,128)S(1)}, f32[128,512]{1,0:T(8,128)S(1)}, u32[]{:S(2)}, u32[]{:S(2)}) collective-permute-start(f32[128,512]{1,0:T(8,128)S(1)} %collective-permute-done.25.refs_1_), channel_id=1, source_target_pairs={{1,0},{0,1},{3,2},{2,3},{5,4},{4,5},{7,6},{6,7},{9,8},{8,9},{11,10... | collective-permute-start | bytes 786440 | tf_op jit(solution)/shard_map/ppermute | solution.py:49
  114.7 6.6 %collective-permute-start.29 = (f32[256,512]{1,0:T(8,128)S(1)}, f32[256,512]{1,0:T(8,128)S(1)}, u32[]{:S(2)}, u32[]{:S(2)}) collective-permute-start(f32[256,512]{1,0:T(8,128)S(1)} %get-tuple-element.117), channel_id=1, source_target_pairs={{1,0},{0,1},{3,2},{2,3},{5,4},{4,5},{7,6},{6,7},{9,8},{8,9},{11,10... | collective-permute-start | bytes 1572872 | tf_op jit(solution)/shard_map/ppermute | solution.py:49
  121.4 8.8 %collective-permute-start.30 = (f32[128,512]{1,0:T(8,128)S(1)}, f32[128,512]{1,0:T(8,128)S(1)}, u32[]{:S(2)}, u32[]{:S(2)}) collective-permute-start(f32[128,512]{1,0:T(8,128)S(1)} %get-tuple-element.118), channel_id=1, source_target_pairs={{0,4},{2,6},{4,0},{6,2},{8,12},{10,14},{12,8},{14,10},{16,20},{18,... | collective-permute-start | bytes 786440 | tf_op jit(solution)/shard_map/ppermute | solution.py:44
  122.4 8.4 %collective-permute-start.31 = (f32[128,512]{1,0:T(8,128)S(1)}, f32[128,512]{1,0:T(8,128)S(1)}, u32[]{:S(2)}, u32[]{:S(2)}) collective-permute-start(f32[128,512]{1,0:T(8,128)S(1)} %get-tuple-element.119), channel_id=1, source_target_pairs={{0,2},{2,0},{4,6},{6,4},{8,10},{10,8},{12,14},{14,12},{16,18},{18,... | collective-permute-start | bytes 786440 | tf_op jit(solution)/shard_map/ppermute | solution.py:44
  137.2 7.1 %collective-permute-start.36 = (f32[72,512]{1,0:T(8,128)S(1)}, f32[72,512]{1,0:T(8,128)S(1)}, u32[]{:S(2)}, u32[]{:S(2)}) collective-permute-start(f32[72,512]{1,0:T(8,128)S(1)} %shard_map.110), channel_id=1, source_target_pairs={{0,24},{2,26},{4,28},{6,30},{8,16},{10,18},{12,20},{14,22},{16,8},... | collective-permute-start | bytes 442376 | tf_op jit(solution)/shard_map/ppermute | solution.py:44
  (18 other events, 126.1 us)

commit v5 on v4

--- a/solution.py
+++ b/solution.py
@@ -10,6 +10,7 @@
 
 F32, BF16 = jnp.float32, jnp.bfloat16
 LIMIT = 12 * 1024 * 1024
+PREPARE_LIMIT = 40 * 1024 * 1024
 X, Y = 1, 2
 EDGE = 8
 
@@ -123,14 +124,35 @@
     return jnp.where(charge == 1, 0, 1 if sectors == 2 else jnp.where(charge == 0, 1, 2))
 
 
-def prepare(me, charges, coupling, left_ops, right_ops, block, count):
+def tabulate(charges, coupling):
+    pairs, sectors = charges.shape[0], lax.axis_size("sector")
+
+    def kernel(charges_ref, coupling_ref, table):
+        row = lax.broadcasted_iota(jnp.int32, table.shape, 0)
+        values = jnp.zeros(table.shape, jnp.int32)
+        for pair in range(pairs):
+            charge = charges_ref[pair]
+            values = jnp.where(row == 2 * pair, block_of(charge, sectors), values)
+            values = jnp.where(row == 2 * pair + 1, coupling_ref[0, charge], values)
+        table[...] = values
+
+    return pl.pallas_call(
+        kernel,
+        in_specs=[pl.BlockSpec(memory_space=pltpu.SMEM)] * 2,
+        out_specs=pl.BlockSpec(memory_space=pltpu.VMEM),
+        out_shape=array(-(-2 * pairs // 8) * 8, 128, kind=jnp.int32),
+        compiler_params=pltpu.CompilerParams(vmem_limit_bytes=LIMIT),
+        cost_estimate=pl.CostEstimate(flops=10**6, bytes_accessed=4096, transcendentals=0),
+    )(charges, coupling)
+
+
+def prepare(me, left_ops, right_ops, block, count):
     pairs, _, m, _ = left_ops.shape
     rows = m // count // 2
     order = row_order(count)
-    sectors = lax.axis_size("sector")
-
-    def kernel(me_ref, charges_ref, coupling_ref, left_ref, right_ref, block_ref, *refs):
-        left_out, left_t_out, right_out, right_t_out, edge, table, held = refs
+
+    def kernel(me_ref, left_ref, right_ref, block_ref, *refs):
+        left_out, left_t_out, right_out, right_t_out, edge, held = refs
 
         def reorder(value):
             held[...] = value
@@ -147,13 +169,6 @@
         right_out[0], right_out[1] = split(value)
         right_t_out[0], right_t_out[1] = split(value.T)
         edge[...] = tile_rows([jnp.zeros((1, m), F32), summed(block_ref[...] * block_ref[...], m)])
-        row = lax.broadcasted_iota(jnp.int32, table.shape, 0)
-        values = jnp.zeros(table.shape, jnp.int32)
-        for pair in range(pairs):
-            charge = charges_ref[pair]
-            values = jnp.where(row == 2 * pair, block_of(charge, sectors), values)
-            values = jnp.where(row == 2 * pair + 1, coupling_ref[0, charge], values)
-        table[...] = values
 
     source = pl.BlockSpec((None, None, m, m), lambda p, *_: (p, 0, 0, 0))
     target = pl.BlockSpec((None, 2, m, m), lambda p, *_: (p, 0, 0, 0))
@@ -161,17 +176,16 @@
     return pl.pallas_call(
         kernel,
         grid_spec=pltpu.PrefetchScalarGridSpec(
-            num_scalar_prefetch=3,
+            num_scalar_prefetch=1,
             grid=(pairs,),
             in_specs=[source, source, whole],
-            out_specs=[target] * 4 + [whole] * 2,
+            out_specs=[target] * 4 + [whole],
             scratch_shapes=[pltpu.VMEM((m, m), F32)],
         ),
-        out_shape=[array(pairs, 2, m, m, kind=BF16)] * 4
-        + [array(EDGE, m), array(-(-2 * pairs // 8) * 8, 128, kind=jnp.int32)],
-        compiler_params=pltpu.CompilerParams(vmem_limit_bytes=10 * LIMIT // 3),
+        out_shape=[array(pairs, 2, m, m, kind=BF16)] * 4 + [array(EDGE, m)],
+        compiler_params=pltpu.CompilerParams(vmem_limit_bytes=PREPARE_LIMIT),
         cost_estimate=pl.CostEstimate(flops=pairs * m * m * 1500, bytes_accessed=24 * pairs * m * m, transcendentals=0),
-    )(me, charges, coupling, left_ops, right_ops, block)
+    )(me, left_ops, right_ops, block)
 
 
 def double(block, masks):
@@ -384,7 +398,8 @@
         outs[0][...] = inputs[0][0][...]
 
     (vector,) = kernel_call(load, [array(2 * rows, m)], [vector])
-    *ops, edge, table = prepare(me, charges, coupling, left_ops, right_ops, vector, count)
+    table = tabulate(charges, coupling)
+    *ops, edge = prepare(me, left_ops, right_ops, vector, count)
     column = double(vector, deep)
     divisor = double(divisor, deep)
 

time: 150 us -> 150 us (level)
  no operation moved by 1% of the time
where the time goes in v5:
time: 150 us
  waiting for transfers between devices  69.6 us (46%)
  starting transfers between devices  43.4 us (29%)
  Pallas kernels  34.9 us (23%)
    ppermute x26, waiting for transfers between devices, swap(): lax.ppermute(block, 'pair', [(i, i ^ mask) for i in range(lax.axis_size('...  67.2 us
    ppermute x26, starting transfers between devices, swap(): lax.ppermute(block, 'pair', [(i, i ^ mask) for i in range(lax.axis_size('...  41.9 us
    pallas_call x29, Pallas kernels, kernel_call(): pl.pallas_call(kernel, in_specs=[pl.BlockSpec(memory_space=pltpu.VMEM)] *...  29 us
    pallas_call x1, Pallas kernels, prepare(): pl.pallas_call(kernel, grid_spec=pltpu.PrefetchScalarGridSpec(num_scalar_...  5.33 us
  transfers between devices with their start and end apart: 38, of which 23 were waited for; matrix products, arithmetic and copies ran while one was open for 0% of the time, Pallas kernels for 22%

profile of v5, /device:TPU:0, one launch (start us, length us, event | category | flops | bytes accessed | tf_op | source)
XLA Modules:
  0.0 149.8 jit_solution(7691638321065885206)
XLA Ops:
  1.5 3.1 %collective-permute-start = (f32[32,512]{1,0:T(8,128)S(1)}, f32[32,512]{1,0:T(8,128)S(1)}, u32[]{:S(2)}, u32[]{:S(2)}) collective-permute-start(f32[32,512]{1,0:T(8,128)S(1)} %shard_map.85.refs_0_.block_ref.refs_1_), channel_id=1, source_target_pairs={{0,8},{2,10},{4,12},{6,14},{8,0},{10,2},{12,4},{14,6},{16,24},{18,... | collective-permute-start | bytes 196616 | tf_op jit(solution)/shard_map/ppermute | solution.py:45
  6.8 4.1 %collective-permute-start.1 = (f32[64,512]{1,0:T(8,128)S(1)}, f32[64,512]{1,0:T(8,128)S(1)}, u32[]{:S(2)}, u32[]{:S(2)}) collective-permute-start(f32[64,512]{1,0:T(8,128)S(1)} %shard_map.86.refs_0_), channel_id=1, source_target_pairs={{0,24},{2,26},{4,28},{6,30},{8,16},{10,18},{12,20},{14,22},{16,8},... | collective-permute-start | bytes 393224 | tf_op jit(solution)/shard_map/ppermute | solution.py:45
  10.9 3.1 %collective-permute-done.1.refs_1_ = f32[64,512]{1,0:T(8,128)S(1)} collective-permute-done((f32[64,512]{1,0:T(8,128)S(1)}, f32[64,512]{1,0:T(8,128)S(1)}, u32[]{:S(2)}, u32[]{:S(2)}) %collective-permute-start.1) | collective-permute-done | bytes 131104 | tf_op jit(solution)/shard_map/ppermute | solution.py:45
  23.6 5.3 %shard_map.90 = (bf16[3,2,512,512]{3,2,1,0:T(8,128)(2,1)S(1)}, bf16[3,2,512,512]{3,2,1,0:T(8,128)(2,1)S(1)}, bf16[3,2,512,512]{3,2,1,0:T(8,128)(2,1)S(1)}, bf16[...) custom-call(s32[1]{0:T(128)} %bitcast.1.me_ref, f32[3,1,512,512]{3,2,1,0:T(8,128)} %left_ref.1, f32[3,1,512,512]{3,2,1,0:T(8,128)} %right_ref.1, ...), custom_call_target="tpu_custom_call" | custom-call | flops 1179648000 | bytes 18874368 | tf_op jit(solution)/shard_map/pallas_call | solution.py:176
  30.9 5.1 %shard_map.92 = (bf16[3,2,256,512]{3,2,1,0:T(8,128)(2,1)S(1)}, bf16[3,2,256,512]{3,2,1,0:T(8,128)(2,1)S(1)}, f32[256,512]{1,0:T(8,128)S(1)}, f32[256,512]{1,0:T(8,128)S(1)}, f32[256,512]{1,0:T(8,128)S(1)}) custom-call(f32[256,512]{1,0:T(8,128)S(1)} %get-tuple-element.68.refs_0_.refs_6_, f32[256,512]{1,0:T(8,128)S(1)} %collective-permute-done.4.refs_1_, ...), custom_call_target="tpu_custom_call" | custom-call | flops 3623878656 | bytes 13635584 | tf_op jit(solution)/shard_map/pallas_call | solution.py:85
  36.0 2.7 %shard_map.93 = (bf16[3,2,256,512]{3,2,1,0:T(8,128)(2,1)S(1)}, f32[256,512]{1,0:T(8,128)S(1)}, f32[256,512]{1,0:T(8,128)S(1)}) custom-call(f32[128,512]{1,0:T(8,128)S(1)} %collective-permute-done.5.refs_0_, f32[128,512]{1,0:T(8,128)S(1)} %collective-permute-done.6.refs_1_, f32[256,512]{1,0:T(8,128)S(1)} %get-tuple-element.76.refs_2_, ...), custom_call_target="tpu_custom_call" | custom-call | flops 2415919104 | bytes 7868416 | tf_op jit(solution)/shard_map/pallas_call | solution.py:85
  39.2 3.0 %shard_map.94 = (bf16[3,2,256,512]{3,2,1,0:T(8,128)(2,1)S(1)}, f32[256,512]{1,0:T(8,128)S(1)}, f32[8,512]{1,0:T(8,128)S(1)}) custom-call(f32[128,512]{1,0:T(8,128)S(1)} %collective-permute-done.5.refs_0_, f32[128,512]{1,0:T(8,128)S(1)} %collective-permute-done.6.refs_1_, f32[128,512]{1,0:T(8,128)S(1)} %collective-permute-done.7.refs_2_, ...), custom_call_target="tpu_custom_call" | custom-call | flops 2415919104 | bytes 8392704 | tf_op jit(solution)/shard_map/pallas_call | solution.py:85
  42.3 2.9 %shard_map.95 = (f32[256,512]{1,0:T(8,128)S(1)}, f32[8,512]{1,0:T(8,128)S(1)}, f32[256,512]{1,0:T(8,128)S(1)}) custom-call(bf16[3,2,256,512]{3,2,1,0:T(8,128)(2,1)S(1)} %get-tuple-element.73.refs_0_, bf16[3,2,256,512]{3,2,1,0:T(8,128)(2,1)S(1)} %get-tuple-element.78.refs_1_, bf16[3,2,256,512]{3,2,1,0:T(8,128)(2,1)S(1)} %get-tuple-element.79.refs_2_, ...), custom_call_target="tpu_custom_call" | custom-call | flops 2415919104 | bytes 13144064 | tf_op jit(solution)/shard_map/pallas_call | solution.py:85
  47.8 6.2 %collective-permute-done.11.refs_2_ = f32[128,512]{1,0:T(8,128)S(1)} collective-permute-done((f32[128,512]{1,0:T(8,128)S(1)}, f32[128,512]{1,0:T(8,128)S(1)}, u32[]{:S(2)}, u32[]{:S(2)}) %collective-permute-start.11) | collective-permute-done | bytes 262176 | tf_op jit(solution)/shard_map/ppermute | solution.py:45
  57.9 3.2 %collective-permute-done.16.refs_5_ = f32[8,512]{1,0:T(8,128)S(1)} collective-permute-done((f32[8,512]{1,0:T(8,128)S(1)}, f32[8,512]{1,0:T(8,128)S(1)}, u32[]{:S(2)}, u32[]{:S(2)}) %collective-permute-start.16) | collective-permute-done | bytes 16416 | tf_op jit(solution)/shard_map/ppermute | solution.py:45
  61.2 3.7 %collective-permute-start.17 = (f32[136,512]{1,0:T(8,128)S(1)}, f32[136,512]{1,0:T(8,128)S(1)}, u32[]{:S(2)}, u32[]{:S(2)}) collective-permute-start(f32[136,512]{1,0:T(8,128)S(1)} %shard_map.98.refs_0_), channel_id=1, source_target_pairs={{0,24},{2,26},{4,28},{6,30},{8,16},{10,18},{12,20},{14,22},{16,8},... | collective-permute-start | bytes 835592 | tf_op jit(solution)/shard_map/ppermute | solution.py:45
  64.9 4.8 %collective-permute-done.17.refs_1_ = f32[136,512]{1,0:T(8,128)S(1)} collective-permute-done((f32[136,512]{1,0:T(8,128)S(1)}, f32[136,512]{1,0:T(8,128)S(1)}, u32[]{:S(2)}, u32[]{:S(2)}) %collective-permute-start.17) | collective-permute-done | bytes 278560 | tf_op jit(solution)/shard_map/ppermute | solution.py:45
  69.7 6.0 %collective-permute-start.18 = (f32[136,512]{1,0:T(8,128)S(1)}, f32[136,512]{1,0:T(8,128)S(1)}, u32[]{:S(2)}, u32[]{:S(2)}) collective-permute-start(f32[136,512]{1,0:T(8,128)S(1)} %shard_map.99.refs_0_), channel_id=1, source_target_pairs={{0,8},{2,10},{4,12},{6,14},{8,0},{10,2},{12,4},{14,6},{16,24},{18,... | collective-permute-start | bytes 835592 | tf_op jit(solution)/shard_map/ppermute | solution.py:45
  75.8 7.7 %collective-permute-done.19.refs_1_ = f32[32,512]{1,0:T(8,128)S(1)} collective-permute-done((f32[32,512]{1,0:T(8,128)S(1)}, f32[32,512]{1,0:T(8,128)S(1)}, u32[]{:S(2)}, u32[]{:S(2)}) %collective-permute-start.19) | collective-permute-done | bytes 65568 | tf_op jit(solution)/shard_map/ppermute | solution.py:45
  85.3 5.1 %collective-permute-done.20.refs_1_ = f32[64,512]{1,0:T(8,128)S(1)} collective-permute-done((f32[64,512]{1,0:T(8,128)S(1)}, f32[64,512]{1,0:T(8,128)S(1)}, u32[]{:S(2)}, u32[]{:S(2)}) %collective-permute-start.20) | collective-permute-done | bytes 131104 | tf_op jit(solution)/shard_map/ppermute | solution.py:45
  98.9 7.1 %collective-permute-done.24.refs_0_ = f32[128,512]{1,0:T(8,128)S(1)} collective-permute-done((f32[128,512]{1,0:T(8,128)S(1)}, f32[128,512]{1,0:T(8,128)S(1)}, u32[]{:S(2)}, u32[]{:S(2)}) %collective-permute-start.24) | collective-permute-done | bytes 262176 | tf_op jit(solution)/shard_map/ppermute | solution.py:45
  106.8 5.3 %shard_map.104 = (bf16[3,2,256,512]{3,2,1,0:T(8,128)(2,1)S(1)}, bf16[3,2,256,512]{3,2,1,0:T(8,128)(2,1)S(1)}, f32[256,512]{1,0:T(8,128)S(1)}, f32[256,512]{1,0:T(8,128)S(1)}, f32[256,512]{1,0:T(8,128)S(1)}) custom-call(f32[256,512]{1,0:T(8,128)S(1)} %get-tuple-element.99.refs_0_.refs_6_, f32[256,512]{1,0:T(8,128)S(1)} %collective-permute-done.23.refs_1_, ...), custom_call_target="tpu_custom_call" | custom-call | flops 3623878656 | bytes 13635584 | tf_op jit(solution)/shard_map/pallas_call | solution.py:85
  112.1 2.7 %shard_map.105 = (bf16[3,2,256,512]{3,2,1,0:T(8,128)(2,1)S(1)}, f32[256,512]{1,0:T(8,128)S(1)}, f32[256,512]{1,0:T(8,128)S(1)}) custom-call(f32[128,512]{1,0:T(8,128)S(1)} %collective-permute-done.24.refs_0_, f32[128,512]{1,0:T(8,128)S(1)} %collective-permute-done.25.refs_1_, f32[256,512]{1,0:T(8,128)S(1)} %get-tuple-element.103.refs_2_, ...), custom_call_target="tpu_custom_call" | custom-call | flops 2415919104 | bytes 7868416 | tf_op jit(solution)/shard_map/pallas_call | solution.py:85
  115.3 3.0 %shard_map.106 = (bf16[3,2,256,512]{3,2,1,0:T(8,128)(2,1)S(1)}, f32[256,512]{1,0:T(8,128)S(1)}, f32[8,512]{1,0:T(8,128)S(1)}) custom-call(f32[128,512]{1,0:T(8,128)S(1)} %collective-permute-done.24.refs_0_, f32[128,512]{1,0:T(8,128)S(1)} %collective-permute-done.25.refs_1_, f32[128,512]{1,0:T(8,128)S(1)} %collective-permute-done.26.refs_2_, ...), custom_call_target="tpu_custom_call" | custom-call | flops 2415919104 | bytes 8392704 | tf_op jit(solution)/shard_map/pallas_call | solution.py:85
  118.3 2.9 %shard_map.107 = (f32[256,512]{1,0:T(8,128)S(1)}, f32[8,512]{1,0:T(8,128)S(1)}, f32[256,512]{1,0:T(8,128)S(1)}) custom-call(bf16[3,2,256,512]{3,2,1,0:T(8,128)(2,1)S(1)} %get-tuple-element.100.refs_0_, bf16[3,2,256,512]{3,2,1,0:T(8,128)(2,1)S(1)} %get-tuple-element.105.refs_1_, bf16[3,2,256,512]{3,2,1,0:T(8,128)(2,1)S(1)} %get-tuple-element.106.refs_2_, ...), custom_call_target="tpu_custom_call" | custom-call | flops 2415919104 | bytes 13144064 | tf_op jit(solution)/shard_map/pallas_call | solution.py:85
  124.2 5.9 %collective-permute-done.30.refs_2_ = f32[128,512]{1,0:T(8,128)S(1)} collective-permute-done((f32[128,512]{1,0:T(8,128)S(1)}, f32[128,512]{1,0:T(8,128)S(1)}, u32[]{:S(2)}, u32[]{:S(2)}) %collective-permute-start.30) | collective-permute-done | bytes 262176 | tf_op jit(solution)/shard_map/ppermute | solution.py:45
  134.4 2.7 %collective-permute-done.35.refs_5_ = f32[8,512]{1,0:T(8,128)S(1)} collective-permute-done((f32[8,512]{1,0:T(8,128)S(1)}, f32[8,512]{1,0:T(8,128)S(1)}, u32[]{:S(2)}, u32[]{:S(2)}) %collective-permute-start.35) | collective-permute-done | bytes 16416 | tf_op jit(solution)/shard_map/ppermute | solution.py:45
  139.0 5.3 %collective-permute-done.36.refs_1_ = f32[72,512]{1,0:T(8,128)S(1)} collective-permute-done((f32[72,512]{1,0:T(8,128)S(1)}, f32[72,512]{1,0:T(8,128)S(1)}, u32[]{:S(2)}, u32[]{:S(2)}) %collective-permute-start.36) | collective-permute-done | bytes 147488 | tf_op jit(solution)/shard_map/ppermute | solution.py:45
  146.0 2.9 %collective-permute-done.37.refs_1_ = f32[40,512]{1,0:T(8,128)S(1)} collective-permute-done((f32[40,512]{1,0:T(8,128)S(1)}, f32[40,512]{1,0:T(8,128)S(1)}, u32[]{:S(2)}, u32[]{:S(2)}) %collective-permute-start.37) | collective-permute-done | bytes 81952 | tf_op jit(solution)/shard_map/ppermute | solution.py:45
  (91 shorter events, 45.1 us)
Async XLA Ops:
  6.8 7.2 %collective-permute-start.1 = (f32[64,512]{1,0:T(8,128)S(1)}, f32[64,512]{1,0:T(8,128)S(1)}, u32[]{:S(2)}, u32[]{:S(2)}) collective-permute-start(f32[64,512]{1,0:T(8,128)S(1)} %shard_map.86.refs_0_), channel_id=1, source_target_pairs={{0,24},{2,26},{4,28},{6,30},{8,16},{10,18},{12,20},{14,22},{16,8},... | collective-permute-start | bytes 393224 | tf_op jit(solution)/shard_map/ppermute | solution.py:45
  20.8 10.0 %collective-permute-start.4 = (f32[256,512]{1,0:T(8,128)S(1)}, f32[256,512]{1,0:T(8,128)S(1)}, u32[]{:S(2)}, u32[]{:S(2)}) collective-permute-start(f32[256,512]{1,0:T(8,128)S(1)} %get-tuple-element.68.refs_0_.refs_6_), channel_id=1, source_target_pairs={{1,0},{0,1},{3,2},{2,3},{5,4},{4,5},{7,6},{6,7},{9,8},{8,9},{11,10... | collective-permute-start | bytes 1572872 | tf_op jit(solution)/shard_map/ppermute | solution.py:50
  20.9 8.7 %collective-permute-start.5 = (f32[128,512]{1,0:T(8,128)S(1)}, f32[128,512]{1,0:T(8,128)S(1)}, u32[]{:S(2)}, u32[]{:S(2)}) collective-permute-start(f32[128,512]{1,0:T(8,128)S(1)} %get-tuple-element.74), channel_id=1, source_target_pairs={{0,4},{2,6},{4,0},{6,2},{8,12},{10,14},{12,8},{14,10},{16,20},{18,... | collective-permute-start | bytes 786440 | tf_op jit(solution)/shard_map/ppermute | solution.py:45
  22.5 8.4 %collective-permute-start.6 = (f32[128,512]{1,0:T(8,128)S(1)}, f32[128,512]{1,0:T(8,128)S(1)}, u32[]{:S(2)}, u32[]{:S(2)}) collective-permute-start(f32[128,512]{1,0:T(8,128)S(1)} %get-tuple-element.75), channel_id=1, source_target_pairs={{0,2},{2,0},{4,6},{6,4},{8,10},{10,8},{12,14},{14,12},{16,18},{18,... | collective-permute-start | bytes 786440 | tf_op jit(solution)/shard_map/ppermute | solution.py:45
  29.6 9.6 %collective-permute-start.7 = (f32[128,512]{1,0:T(8,128)S(1)}, f32[128,512]{1,0:T(8,128)S(1)}, u32[]{:S(2)}, u32[]{:S(2)}) collective-permute-start(f32[128,512]{1,0:T(8,128)S(1)} %collective-permute-done.5.refs_0_), channel_id=1, source_target_pairs={{1,0},{0,1},{3,2},{2,3},{5,4},{4,5},{7,6},{6,7},{9,8},{8,9},{11,10... | collective-permute-start | bytes 786440 | tf_op jit(solution)/shard_map/ppermute | solution.py:50
  30.9 8.4 %collective-permute-start.8 = (f32[128,512]{1,0:T(8,128)S(1)}, f32[128,512]{1,0:T(8,128)S(1)}, u32[]{:S(2)}, u32[]{:S(2)}) collective-permute-start(f32[128,512]{1,0:T(8,128)S(1)} %collective-permute-done.6.refs_1_), channel_id=1, source_target_pairs={{1,0},{0,1},{3,2},{2,3},{5,4},{4,5},{7,6},{6,7},{9,8},{8,9},{11,10... | collective-permute-start | bytes 786440 | tf_op jit(solution)/shard_map/ppermute | solution.py:50
  38.6 6.6 %collective-permute-start.10 = (f32[256,512]{1,0:T(8,128)S(1)}, f32[256,512]{1,0:T(8,128)S(1)}, u32[]{:S(2)}, u32[]{:S(2)}) collective-permute-start(f32[256,512]{1,0:T(8,128)S(1)} %get-tuple-element.88), channel_id=1, source_target_pairs={{1,0},{0,1},{3,2},{2,3},{5,4},{4,5},{7,6},{6,7},{9,8},{8,9},{11,10... | collective-permute-start | bytes 1572872 | tf_op jit(solution)/shard_map/ppermute | solution.py:50
  45.3 8.8 %collective-permute-start.11 = (f32[128,512]{1,0:T(8,128)S(1)}, f32[128,512]{1,0:T(8,128)S(1)}, u32[]{:S(2)}, u32[]{:S(2)}) collective-permute-start(f32[128,512]{1,0:T(8,128)S(1)} %get-tuple-element.89), channel_id=1, source_target_pairs={{0,4},{2,6},{4,0},{6,2},{8,12},{10,14},{12,8},{14,10},{16,20},{18,... | collective-permute-start | bytes 786440 | tf_op jit(solution)/shard_map/ppermute | solution.py:45
  46.1 8.2 %collective-permute-start.12 = (f32[128,512]{1,0:T(8,128)S(1)}, f32[128,512]{1,0:T(8,128)S(1)}, u32[]{:S(2)}, u32[]{:S(2)}) collective-permute-start(f32[128,512]{1,0:T(8,128)S(1)} %get-tuple-element.90), channel_id=1, source_target_pairs={{0,2},{2,0},{4,6},{6,4},{8,10},{10,8},{12,14},{14,12},{16,18},{18,... | collective-permute-start | bytes 786440 | tf_op jit(solution)/shard_map/ppermute | solution.py:45
  54.4 6.7 %collective-permute-start.14 = (f32[72,512]{1,0:T(8,128)S(1)}, f32[72,512]{1,0:T(8,128)S(1)}, u32[]{:S(2)}, u32[]{:S(2)}) collective-permute-start(f32[72,512]{1,0:T(8,128)S(1)} %get-tuple-element.93), channel_id=1, source_target_pairs={{0,2},{2,0},{4,6},{6,4},{8,10},{10,8},{12,14},{14,12},{16,18},{18,... | collective-permute-start | bytes 442376 | tf_op jit(solution)/shard_map/ppermute | solution.py:45
  54.8 6.3 %collective-permute-start.15 = (f32[72,512]{1,0:T(8,128)S(1)}, f32[72,512]{1,0:T(8,128)S(1)}, u32[]{:S(2)}, u32[]{:S(2)}) collective-permute-start(f32[72,512]{1,0:T(8,128)S(1)} %get-tuple-element.95), channel_id=1, source_target_pairs={{0,4},{2,6},{4,0},{6,2},{8,12},{10,14},{12,8},{14,10},{16,20},{18,... | collective-permute-start | bytes 442376 | tf_op jit(solution)/shard_map/ppermute | solution.py:45
  61.2 8.5 %collective-permute-start.17 = (f32[136,512]{1,0:T(8,128)S(1)}, f32[136,512]{1,0:T(8,128)S(1)}, u32[]{:S(2)}, u32[]{:S(2)}) collective-permute-start(f32[136,512]{1,0:T(8,128)S(1)} %shard_map.98.refs_0_), channel_id=1, source_target_pairs={{0,24},{2,26},{4,28},{6,30},{8,16},{10,18},{12,20},{14,22},{16,8},... | collective-permute-start | bytes 835592 | tf_op jit(solution)/shard_map/ppermute | solution.py:45
  69.7 20.8 %collective-permute-start.18 = (f32[136,512]{1,0:T(8,128)S(1)}, f32[136,512]{1,0:T(8,128)S(1)}, u32[]{:S(2)}, u32[]{:S(2)}) collective-permute-start(f32[136,512]{1,0:T(8,128)S(1)} %shard_map.99.refs_0_), channel_id=1, source_target_pairs={{0,8},{2,10},{4,12},{6,14},{8,0},{10,2},{12,4},{14,6},{16,24},{18,... | collective-permute-start | bytes 835592 | tf_op jit(solution)/shard_map/ppermute | solution.py:45
  75.7 7.8 %collective-permute-start.19 = (f32[32,512]{1,0:T(8,128)S(1)}, f32[32,512]{1,0:T(8,128)S(1)}, u32[]{:S(2)}, u32[]{:S(2)}) collective-permute-start(f32[32,512]{1,0:T(8,128)S(1)} %bitcast.6), channel_id=1, source_target_pairs={{0,8},{2,10},{4,12},{6,14},{8,0},{10,2},{12,4},{14,6},{16,24},{18,... | collective-permute-start | bytes 196616 | tf_op jit(solution)/shard_map/ppermute | solution.py:45
  83.5 6.9 %collective-permute-start.20 = (f32[64,512]{1,0:T(8,128)S(1)}, f32[64,512]{1,0:T(8,128)S(1)}, u32[]{:S(2)}, u32[]{:S(2)}) collective-permute-start(f32[64,512]{1,0:T(8,128)S(1)} %shard_map.100.refs_0_), channel_id=1, source_target_pairs={{0,24},{2,26},{4,28},{6,30},{8,16},{10,18},{12,20},{14,22},{16,8},... | collective-permute-start | bytes 393224 | tf_op jit(solution)/shard_map/ppermute | solution.py:45
  97.2 9.6 %collective-permute-start.23 = (f32[256,512]{1,0:T(8,128)S(1)}, f32[256,512]{1,0:T(8,128)S(1)}, u32[]{:S(2)}, u32[]{:S(2)}) collective-permute-start(f32[256,512]{1,0:T(8,128)S(1)} %get-tuple-element.99.refs_0_.refs_6_), channel_id=1, source_target_pairs={{1,0},{0,1},{3,2},{2,3},{5,4},{4,5},{7,6},{6,7},{9,8},{8,9},{11,10... | collective-permute-start | bytes 1572872 | tf_op jit(solution)/shard_map/ppermute | solution.py:50
  97.3 8.7 %collective-permute-start.24 = (f32[128,512]{1,0:T(8,128)S(1)}, f32[128,512]{1,0:T(8,128)S(1)}, u32[]{:S(2)}, u32[]{:S(2)}) collective-permute-start(f32[128,512]{1,0:T(8,128)S(1)} %get-tuple-element.101), channel_id=1, source_target_pairs={{0,4},{2,6},{4,0},{6,2},{8,12},{10,14},{12,8},{14,10},{16,20},{18,... | collective-permute-start | bytes 786440 | tf_op jit(solution)/shard_map/ppermute | solution.py:45
  98.4 8.4 %collective-permute-start.25 = (f32[128,512]{1,0:T(8,128)S(1)}, f32[128,512]{1,0:T(8,128)S(1)}, u32[]{:S(2)}, u32[]{:S(2)}) collective-permute-start(f32[128,512]{1,0:T(8,128)S(1)} %get-tuple-element.102), channel_id=1, source_target_pairs={{0,2},{2,0},{4,6},{6,4},{8,10},{10,8},{12,14},{14,12},{16,18},{18,... | collective-permute-start | bytes 786440 | tf_op jit(solution)/shard_map/ppermute | solution.py:45
  106.0 9.3 %collective-permute-start.26 = (f32[128,512]{1,0:T(8,128)S(1)}, f32[128,512]{1,0:T(8,128)S(1)}, u32[]{:S(2)}, u32[]{:S(2)}) collective-permute-start(f32[128,512]{1,0:T(8,128)S(1)} %collective-permute-done.24.refs_0_), channel_id=1, source_target_pairs={{1,0},{0,1},{3,2},{2,3},{5,4},{4,5},{7,6},{6,7},{9,8},{8,9},{11,10... | collective-permute-start | bytes 786440 | tf_op jit(solution)/shard_map/ppermute | solution.py:50
  106.8 8.5 %collective-permute-start.27 = (f32[128,512]{1,0:T(8,128)S(1)}, f32[128,512]{1,0:T(8,128)S(1)}, u32[]{:S(2)}, u32[]{:S(2)}) collective-permute-start(f32[128,512]{1,0:T(8,128)S(1)} %collective-permute-done.25.refs_1_), channel_id=1, source_target_pairs={{1,0},{0,1},{3,2},{2,3},{5,4},{4,5},{7,6},{6,7},{9,8},{8,9},{11,10... | collective-permute-start | bytes 786440 | tf_op jit(solution)/shard_map/ppermute | solution.py:50
  114.7 6.5 %collective-permute-start.29 = (f32[256,512]{1,0:T(8,128)S(1)}, f32[256,512]{1,0:T(8,128)S(1)}, u32[]{:S(2)}, u32[]{:S(2)}) collective-permute-start(f32[256,512]{1,0:T(8,128)S(1)} %get-tuple-element.115), channel_id=1, source_target_pairs={{1,0},{0,1},{3,2},{2,3},{5,4},{4,5},{7,6},{6,7},{9,8},{8,9},{11,10... | collective-permute-start | bytes 1572872 | tf_op jit(solution)/shard_map/ppermute | solution.py:50
  121.3 8.8 %collective-permute-start.30 = (f32[128,512]{1,0:T(8,128)S(1)}, f32[128,512]{1,0:T(8,128)S(1)}, u32[]{:S(2)}, u32[]{:S(2)}) collective-permute-start(f32[128,512]{1,0:T(8,128)S(1)} %get-tuple-element.116), channel_id=1, source_target_pairs={{0,4},{2,6},{4,0},{6,2},{8,12},{10,14},{12,8},{14,10},{16,20},{18,... | collective-permute-start | bytes 786440 | tf_op jit(solution)/shard_map/ppermute | solution.py:45
  122.4 8.4 %collective-permute-start.31 = (f32[128,512]{1,0:T(8,128)S(1)}, f32[128,512]{1,0:T(8,128)S(1)}, u32[]{:S(2)}, u32[]{:S(2)}) collective-permute-start(f32[128,512]{1,0:T(8,128)S(1)} %get-tuple-element.117), channel_id=1, source_target_pairs={{0,2},{2,0},{4,6},{6,4},{8,10},{10,8},{12,14},{14,12},{16,18},{18,... | collective-permute-start | bytes 786440 | tf_op jit(solution)/shard_map/ppermute | solution.py:45
  137.2 7.1 %collective-permute-start.36 = (f32[72,512]{1,0:T(8,128)S(1)}, f32[72,512]{1,0:T(8,128)S(1)}, u32[]{:S(2)}, u32[]{:S(2)}) collective-permute-start(f32[72,512]{1,0:T(8,128)S(1)} %shard_map.111), channel_id=1, source_target_pairs={{0,24},{2,26},{4,28},{6,30},{8,16},{10,18},{12,20},{14,22},{16,8},... | collective-permute-start | bytes 442376 | tf_op jit(solution)/shard_map/ppermute | solution.py:45
  (18 other events, 126.1 us)

commit v6 on v5

--- a/solution.py
+++ b/solution.py
@@ -204,7 +204,7 @@
     return block
 
 
-def sigma_apply(column_a, column_b, ops, table, edge):
+def sigma_apply(column_a, column_b, ops, table, edge, halves):
     left, left_t, right, right_t = ops
     pairs, m = left.shape[0], left.shape[2]
     sectors = lax.axis_size("sector")
@@ -368,6 +368,16 @@
     )
     got_a, got_b, corner = swap(go_a, X), swap(go_b, Y), swap(edge, X | Y)
 
+    def second_sums(inputs, outs, scratch):
+        (a_stay, a_got), (b_stay, b_got), (edge_ref, corner_ref) = inputs
+        outs[0][:eighth, :] = a_stay[...] + a_got[:eighth, :]
+        outs[0][eighth:, :] = edge_ref[...] + a_got[eighth:, :] + b_got[eighth:, :] + corner_ref[...]
+        outs[1][...] = b_stay[...] + b_got[:eighth, :]
+
+    if halves:
+        shapes = [array(eighth + EDGE, m), array(eighth, m)]
+        return kernel_call(second_sums, shapes, [stay_a, got_a], [stay_b, got_b], [edge, corner])
+
     def second_sum(inputs, outs, scratch):
         (a_stay, a_got), (b_stay, b_got), (edge_ref, corner_ref) = inputs
         outs[0][:eighth, :] = a_stay[...] + a_got[:eighth, :]
@@ -379,10 +389,8 @@
 
 def turned(value, slots, mask, rows):
     size = len(slots) * rows
-    parts = [
-        value[part * size + slots.index(slot ^ mask) * rows :][:rows] for part in (0, 1) for slot in slots
-    ]
-    return jnp.concatenate(parts + [value[2 * size :]], axis=0)
+    parts = [value[slots.index(slot ^ mask) * rows :][:rows] for slot in slots]
+    return jnp.concatenate(parts + ([value[size:]] if value.shape[0] > size else []), axis=0)
 
 
 def per_device(wavefunction, preconditioner, left_ops, right_ops, charges, coupling):
@@ -408,19 +416,24 @@
         outs[1][...] = inputs[0][0][tall:, :]
 
     vector_a, vector_b = kernel_call(part, [array(tall, m)] * 2, [column])
-    image = sigma_apply(vector_a, vector_b, ops, table, edge)
-    for mask in deep[:0:-1]:
+    image_a, image_b = sigma_apply(vector_a, vector_b, ops, table, edge, True)
+    for masks in zip(deep[:0:-1], deep[:-1]):
 
         def add_columns(inputs, outs, scratch):
-            own, got = inputs[0]
-            outs[0][...] = own[...] + turned(got[...], slots, mask, rows)
-
-        (image,) = kernel_call(add_columns, [array(*image.shape)], [image, swap(image, mask)])
+            for (own, got), out, mask in zip(inputs, outs, masks):
+                out[...] = own[...] + turned(got[...], slots, mask, rows)
+
+        image_a, image_b = kernel_call(
+            add_columns, [array(*image_a.shape), array(*image_b.shape)],
+            [image_a, swap(image_a, masks[0])], [image_b, swap(image_b, masks[1])],
+        )
 
     def correct(inputs, outs, scratch):
-        own, got, w_ref, p_ref = inputs[0]
+        a_ref, a_got, b_ref, b_got, w_ref, p_ref = inputs[0]
         correction_a, correction_b, image_own, sums_out, edge_out = outs
-        total = own[...] + turned(got[...], slots, deep[0], rows)
+        total_a = a_ref[...] + turned(a_got[...], slots, deep[0], rows)
+        total_b = b_ref[...] + turned(b_got[...], slots, deep[-1], rows)
+        total = jnp.concatenate([total_a[:tall], total_b, total_a[tall:]], axis=0)
         sums = total[2 * tall :]
         theta = sums[0:1, :] / sums[1:2, :]
         c = (total[: 2 * tall] - theta * w_ref[...]) / p_ref[...]
@@ -439,10 +452,10 @@
 
     ca, cb, image_own, sums, edge = kernel_call(
         correct, [array(tall, m), array(tall, m), array(2 * rows, m), array(EDGE, m), array(EDGE, m)],
-        [image, swap(image, deep[0]), column, divisor],
+        [image_a, swap(image_a, deep[0]), image_b, swap(image_b, deep[-1]), column, divisor],
     )
     own_c = (ca, cb)
-    second = sigma_apply(ca, cb, ops, table, edge)
+    second = sigma_apply(ca, cb, ops, table, edge, False)
 
     for mask in deep[::-1]:
         size = (second.shape[0] - EDGE) // 4

time: 150 us -> 141 us (0.940)
  waiting for transfers between devices: 69.6 us -> 59.6 us
    ppermute x26 -> x28, waiting for transfers between devices: 67.2 us -> 57.2 us  [swap(): lax.ppermute(block, 'pair', [(i, i ^ mask) for i in range(lax.axis_size('...]
    ppermute x26 -> x28, starting transfers between devices: 41.9 us -> 42.7 us  [swap(): lax.ppermute(block, 'pair', [(i, i ^ mask) for i in range(lax.axis_size('...]
  transfers between devices with their start and end apart: 38 -> 40, of which waited for: 23 -> 23; matrix products, arithmetic and copies ran while one was open for 0% -> 0% of each run, Pallas kernels for 22% -> 24%
where the time goes in v6:
time: 141 us
  waiting for transfers between devices  59.6 us (42%)
  starting transfers between devices  44.2 us (31%)
  Pallas kernels  34.9 us (25%)
    ppermute x28, waiting for transfers between devices, swap(): lax.ppermute(block, 'pair', [(i, i ^ mask) for i in range(lax.axis_size('...  57.2 us
    ppermute x28, starting transfers between devices, swap(): lax.ppermute(block, 'pair', [(i, i ^ mask) for i in range(lax.axis_size('...  42.7 us
    pallas_call x29, Pallas kernels, kernel_call(): pl.pallas_call(kernel, in_specs=[pl.BlockSpec(memory_space=pltpu.VMEM)] *...  29 us
    pallas_call x1, Pallas kernels, prepare(): pl.pallas_call(kernel, grid_spec=pltpu.PrefetchScalarGridSpec(num_scalar_...  5.33 us
  transfers between devices with their start and end apart: 40, of which 23 were waited for; matrix products, arithmetic and copies ran while one was open for 0% of the time, Pallas kernels for 24%

profile of v6, /device:TPU:0, one launch (start us, length us, event | category | flops | bytes accessed | tf_op | source)
XLA Modules:
  0.0 140.6 jit_solution(1272318322759488195)
XLA Ops:
  1.5 3.1 %collective-permute-start = (f32[32,512]{1,0:T(8,128)S(1)}, f32[32,512]{1,0:T(8,128)S(1)}, u32[]{:S(2)}, u32[]{:S(2)}) collective-permute-start(f32[32,512]{1,0:T(8,128)S(1)} %shard_map.85.refs_0_.block_ref.refs_1_), channel_id=1, source_target_pairs={{0,8},{2,10},{4,12},{6,14},{8,0},{10,2},{12,4},{14,6},{16,24},{18,... | collective-permute-start | bytes 196616 | tf_op jit(solution)/shard_map/ppermute | solution.py:45
  6.8 4.1 %collective-permute-start.1 = (f32[64,512]{1,0:T(8,128)S(1)}, f32[64,512]{1,0:T(8,128)S(1)}, u32[]{:S(2)}, u32[]{:S(2)}) collective-permute-start(f32[64,512]{1,0:T(8,128)S(1)} %shard_map.86.refs_0_), channel_id=1, source_target_pairs={{0,24},{2,26},{4,28},{6,30},{8,16},{10,18},{12,20},{14,22},{16,8},... | collective-permute-start | bytes 393224 | tf_op jit(solution)/shard_map/ppermute | solution.py:45
  10.9 3.1 %collective-permute-done.1.refs_1_ = f32[64,512]{1,0:T(8,128)S(1)} collective-permute-done((f32[64,512]{1,0:T(8,128)S(1)}, f32[64,512]{1,0:T(8,128)S(1)}, u32[]{:S(2)}, u32[]{:S(2)}) %collective-permute-start.1) | collective-permute-done | bytes 131104 | tf_op jit(solution)/shard_map/ppermute | solution.py:45
  23.6 5.3 %shard_map.90 = (bf16[3,2,512,512]{3,2,1,0:T(8,128)(2,1)S(1)}, bf16[3,2,512,512]{3,2,1,0:T(8,128)(2,1)S(1)}, bf16[3,2,512,512]{3,2,1,0:T(8,128)(2,1)S(1)}, bf16[...) custom-call(s32[1]{0:T(128)} %bitcast.1.me_ref, f32[3,1,512,512]{3,2,1,0:T(8,128)} %left_ref.1, f32[3,1,512,512]{3,2,1,0:T(8,128)} %right_ref.1, ...), custom_call_target="tpu_custom_call" | custom-call | flops 1179648000 | bytes 18874368 | tf_op jit(solution)/shard_map/pallas_call | solution.py:176
  30.9 5.1 %shard_map.92 = (bf16[3,2,256,512]{3,2,1,0:T(8,128)(2,1)S(1)}, bf16[3,2,256,512]{3,2,1,0:T(8,128)(2,1)S(1)}, f32[256,512]{1,0:T(8,128)S(1)}, f32[256,512]{1,0:T(8,128)S(1)}, f32[256,512]{1,0:T(8,128)S(1)}) custom-call(f32[256,512]{1,0:T(8,128)S(1)} %get-tuple-element.72.refs_0_.refs_6_, f32[256,512]{1,0:T(8,128)S(1)} %collective-permute-done.4.refs_1_, ...), custom_call_target="tpu_custom_call" | custom-call | flops 3623878656 | bytes 13635584 | tf_op jit(solution)/shard_map/pallas_call | solution.py:85
  36.0 2.7 %shard_map.93 = (bf16[3,2,256,512]{3,2,1,0:T(8,128)(2,1)S(1)}, f32[256,512]{1,0:T(8,128)S(1)}, f32[256,512]{1,0:T(8,128)S(1)}) custom-call(f32[128,512]{1,0:T(8,128)S(1)} %collective-permute-done.5.refs_0_, f32[128,512]{1,0:T(8,128)S(1)} %collective-permute-done.6.refs_1_, f32[256,512]{1,0:T(8,128)S(1)} %get-tuple-element.80.refs_2_, ...), custom_call_target="tpu_custom_call" | custom-call | flops 2415919104 | bytes 7868416 | tf_op jit(solution)/shard_map/pallas_call | solution.py:85
  39.2 3.0 %shard_map.94 = (bf16[3,2,256,512]{3,2,1,0:T(8,128)(2,1)S(1)}, f32[256,512]{1,0:T(8,128)S(1)}, f32[8,512]{1,0:T(8,128)S(1)}) custom-call(f32[128,512]{1,0:T(8,128)S(1)} %collective-permute-done.5.refs_0_, f32[128,512]{1,0:T(8,128)S(1)} %collective-permute-done.6.refs_1_, f32[128,512]{1,0:T(8,128)S(1)} %collective-permute-done.7.refs_2_, ...), custom_call_target="tpu_custom_call" | custom-call | flops 2415919104 | bytes 8392704 | tf_op jit(solution)/shard_map/pallas_call | solution.py:85
  42.3 2.9 %shard_map.95 = (f32[256,512]{1,0:T(8,128)S(1)}, f32[8,512]{1,0:T(8,128)S(1)}, f32[256,512]{1,0:T(8,128)S(1)}) custom-call(bf16[3,2,256,512]{3,2,1,0:T(8,128)(2,1)S(1)} %get-tuple-element.77.refs_0_, bf16[3,2,256,512]{3,2,1,0:T(8,128)(2,1)S(1)} %get-tuple-element.82.refs_1_, bf16[3,2,256,512]{3,2,1,0:T(8,128)(2,1)S(1)} %get-tuple-element.83.refs_2_, ...), custom_call_target="tpu_custom_call" | custom-call | flops 2415919104 | bytes 13144064 | tf_op jit(solution)/shard_map/pallas_call | solution.py:85
  47.8 6.2 %collective-permute-done.11.refs_2_ = f32[128,512]{1,0:T(8,128)S(1)} collective-permute-done((f32[128,512]{1,0:T(8,128)S(1)}, f32[128,512]{1,0:T(8,128)S(1)}, u32[]{:S(2)}, u32[]{:S(2)}) %collective-permute-start.11) | collective-permute-done | bytes 262176 | tf_op jit(solution)/shard_map/ppermute | solution.py:45
  57.9 3.2 %collective-permute-done.16.refs_5_ = f32[8,512]{1,0:T(8,128)S(1)} collective-permute-done((f32[8,512]{1,0:T(8,128)S(1)}, f32[8,512]{1,0:T(8,128)S(1)}, u32[]{:S(2)}, u32[]{:S(2)}) %collective-permute-start.16) | collective-permute-done | bytes 16416 | tf_op jit(solution)/shard_map/ppermute | solution.py:45
  61.2 3.7 %collective-permute-start.17 = (f32[72,512]{1,0:T(8,128)S(1)}, f32[72,512]{1,0:T(8,128)S(1)}, u32[]{:S(2)}, u32[]{:S(2)}) collective-permute-start(f32[72,512]{1,0:T(8,128)S(1)} %get-tuple-element.101.refs_0_), channel_id=1, source_target_pairs={{0,24},{2,26},{4,28},{6,30},{8,16},{10,18},{12,20},{14,22},{16,8},... | collective-permute-start | bytes 442376 | tf_op jit(solution)/shard_map/ppermute | solution.py:45
  66.9 4.4 %collective-permute-done.18.refs_3_ = f32[64,512]{1,0:T(8,128)S(1)} collective-permute-done((f32[64,512]{1,0:T(8,128)S(1)}, f32[64,512]{1,0:T(8,128)S(1)}, u32[]{:S(2)}, u32[]{:S(2)}) %collective-permute-start.18) | collective-permute-done | bytes 131104 | tf_op jit(solution)/shard_map/ppermute | solution.py:45
  73.3 3.6 %collective-permute-start.20 = (f32[64,512]{1,0:T(8,128)S(1)}, f32[64,512]{1,0:T(8,128)S(1)}, u32[]{:S(2)}, u32[]{:S(2)}) collective-permute-start(f32[64,512]{1,0:T(8,128)S(1)} %get-tuple-element.104.refs_2_), channel_id=1, source_target_pairs={{0,24},{2,26},{4,28},{6,30},{8,16},{10,18},{12,20},{14,22},{16,8},... | collective-permute-start | bytes 393224 | tf_op jit(solution)/shard_map/ppermute | solution.py:45
  76.9 3.0 %collective-permute-done.22.refs_1_ = f32[64,512]{1,0:T(8,128)S(1)} collective-permute-done((f32[64,512]{1,0:T(8,128)S(1)}, f32[64,512]{1,0:T(8,128)S(1)}, u32[]{:S(2)}, u32[]{:S(2)}) %collective-permute-start.22) | collective-permute-done | bytes 131104 | tf_op jit(solution)/shard_map/ppermute | solution.py:45
  83.8 2.7 %collective-permute-done.23.refs_1_ = f32[64,512]{1,0:T(8,128)S(1)} collective-permute-done((f32[64,512]{1,0:T(8,128)S(1)}, f32[64,512]{1,0:T(8,128)S(1)}, u32[]{:S(2)}, u32[]{:S(2)}) %collective-permute-start.23) | collective-permute-done | bytes 131104 | tf_op jit(solution)/shard_map/ppermute | solution.py:45
  89.5 7.3 %collective-permute-done.26.refs_0_ = f32[128,512]{1,0:T(8,128)S(1)} collective-permute-done((f32[128,512]{1,0:T(8,128)S(1)}, f32[128,512]{1,0:T(8,128)S(1)}, u32[]{:S(2)}, u32[]{:S(2)}) %collective-permute-start.26) | collective-permute-done | bytes 262176 | tf_op jit(solution)/shard_map/ppermute | solution.py:45
  97.4 5.3 %shard_map.104 = (bf16[3,2,256,512]{3,2,1,0:T(8,128)(2,1)S(1)}, bf16[3,2,256,512]{3,2,1,0:T(8,128)(2,1)S(1)}, f32[256,512]{1,0:T(8,128)S(1)}, f32[256,512]{1,0:T(8,128)S(1)}, f32[256,512]{1,0:T(8,128)S(1)}) custom-call(f32[256,512]{1,0:T(8,128)S(1)} %get-tuple-element.107.refs_0_.refs_6_, f32[256,512]{1,0:T(8,128)S(1)} %collective-permute-done.25.refs_1_, ...), custom_call_target="tpu_custom_call" | custom-call | flops 3623878656 | bytes 13635584 | tf_op jit(solution)/shard_map/pallas_call | solution.py:85
  102.7 2.7 %shard_map.105 = (bf16[3,2,256,512]{3,2,1,0:T(8,128)(2,1)S(1)}, f32[256,512]{1,0:T(8,128)S(1)}, f32[256,512]{1,0:T(8,128)S(1)}) custom-call(f32[128,512]{1,0:T(8,128)S(1)} %collective-permute-done.26.refs_0_, f32[128,512]{1,0:T(8,128)S(1)} %collective-permute-done.27.refs_1_, f32[256,512]{1,0:T(8,128)S(1)} %get-tuple-element.111.refs_2_, ...), custom_call_target="tpu_custom_call" | custom-call | flops 2415919104 | bytes 7868416 | tf_op jit(solution)/shard_map/pallas_call | solution.py:85
  105.9 3.0 %shard_map.106 = (bf16[3,2,256,512]{3,2,1,0:T(8,128)(2,1)S(1)}, f32[256,512]{1,0:T(8,128)S(1)}, f32[8,512]{1,0:T(8,128)S(1)}) custom-call(f32[128,512]{1,0:T(8,128)S(1)} %collective-permute-done.26.refs_0_, f32[128,512]{1,0:T(8,128)S(1)} %collective-permute-done.27.refs_1_, f32[128,512]{1,0:T(8,128)S(1)} %collective-permute-done.28.refs_2_, ...), custom_call_target="tpu_custom_call" | custom-call | flops 2415919104 | bytes 8392704 | tf_op jit(solution)/shard_map/pallas_call | solution.py:85
  108.9 2.9 %shard_map.107 = (f32[256,512]{1,0:T(8,128)S(1)}, f32[8,512]{1,0:T(8,128)S(1)}, f32[256,512]{1,0:T(8,128)S(1)}) custom-call(bf16[3,2,256,512]{3,2,1,0:T(8,128)(2,1)S(1)} %get-tuple-element.108.refs_0_, bf16[3,2,256,512]{3,2,1,0:T(8,128)(2,1)S(1)} %get-tuple-element.113.refs_1_, bf16[3,2,256,512]{3,2,1,0:T(8,128)(2,1)S(1)} %get-tuple-element.114.refs_2_, ...), custom_call_target="tpu_custom_call" | custom-call | flops 2415919104 | bytes 13144064 | tf_op jit(solution)/shard_map/pallas_call | solution.py:85
  115.1 5.7 %collective-permute-done.32.refs_2_ = f32[128,512]{1,0:T(8,128)S(1)} collective-permute-done((f32[128,512]{1,0:T(8,128)S(1)}, f32[128,512]{1,0:T(8,128)S(1)}, u32[]{:S(2)}, u32[]{:S(2)}) %collective-permute-start.32) | collective-permute-done | bytes 262176 | tf_op jit(solution)/shard_map/ppermute | solution.py:45
  125.3 2.5 %collective-permute-done.37.refs_5_ = f32[8,512]{1,0:T(8,128)S(1)} collective-permute-done((f32[8,512]{1,0:T(8,128)S(1)}, f32[8,512]{1,0:T(8,128)S(1)}, u32[]{:S(2)}, u32[]{:S(2)}) %collective-permute-start.37) | collective-permute-done | bytes 16416 | tf_op jit(solution)/shard_map/ppermute | solution.py:45
  127.8 2.5 %collective-permute-start.38 = (f32[72,512]{1,0:T(8,128)S(1)}, f32[72,512]{1,0:T(8,128)S(1)}, u32[]{:S(2)}, u32[]{:S(2)}) collective-permute-start(f32[72,512]{1,0:T(8,128)S(1)} %shard_map.111), channel_id=1, source_target_pairs={{0,24},{2,26},{4,28},{6,30},{8,16},{10,18},{12,20},{14,22},{16,8},... | collective-permute-start | bytes 442376 | tf_op jit(solution)/shard_map/ppermute | solution.py:45
  130.3 4.6 %collective-permute-done.38.refs_1_ = f32[72,512]{1,0:T(8,128)S(1)} collective-permute-done((f32[72,512]{1,0:T(8,128)S(1)}, f32[72,512]{1,0:T(8,128)S(1)}, u32[]{:S(2)}, u32[]{:S(2)}) %collective-permute-start.38) | collective-permute-done | bytes 147488 | tf_op jit(solution)/shard_map/ppermute | solution.py:45
  (95 shorter events, 47.1 us)
Async XLA Ops:
  6.8 7.2 %collective-permute-start.1 = (f32[64,512]{1,0:T(8,128)S(1)}, f32[64,512]{1,0:T(8,128)S(1)}, u32[]{:S(2)}, u32[]{:S(2)}) collective-permute-start(f32[64,512]{1,0:T(8,128)S(1)} %shard_map.86.refs_0_), channel_id=1, source_target_pairs={{0,24},{2,26},{4,28},{6,30},{8,16},{10,18},{12,20},{14,22},{16,8},... | collective-permute-start | bytes 393224 | tf_op jit(solution)/shard_map/ppermute | solution.py:45
  20.8 10.0 %collective-permute-start.4 = (f32[256,512]{1,0:T(8,128)S(1)}, f32[256,512]{1,0:T(8,128)S(1)}, u32[]{:S(2)}, u32[]{:S(2)}) collective-permute-start(f32[256,512]{1,0:T(8,128)S(1)} %get-tuple-element.72.refs_0_.refs_6_), channel_id=1, source_target_pairs={{1,0},{0,1},{3,2},{2,3},{5,4},{4,5},{7,6},{6,7},{9,8},{8,9},{11,10... | collective-permute-start | bytes 1572872 | tf_op jit(solution)/shard_map/ppermute | solution.py:50
  20.9 8.7 %collective-permute-start.5 = (f32[128,512]{1,0:T(8,128)S(1)}, f32[128,512]{1,0:T(8,128)S(1)}, u32[]{:S(2)}, u32[]{:S(2)}) collective-permute-start(f32[128,512]{1,0:T(8,128)S(1)} %get-tuple-element.78), channel_id=1, source_target_pairs={{0,4},{2,6},{4,0},{6,2},{8,12},{10,14},{12,8},{14,10},{16,20},{18,... | collective-permute-start | bytes 786440 | tf_op jit(solution)/shard_map/ppermute | solution.py:45
  22.5 8.4 %collective-permute-start.6 = (f32[128,512]{1,0:T(8,128)S(1)}, f32[128,512]{1,0:T(8,128)S(1)}, u32[]{:S(2)}, u32[]{:S(2)}) collective-permute-start(f32[128,512]{1,0:T(8,128)S(1)} %get-tuple-element.79), channel_id=1, source_target_pairs={{0,2},{2,0},{4,6},{6,4},{8,10},{10,8},{12,14},{14,12},{16,18},{18,... | collective-permute-start | bytes 786440 | tf_op jit(solution)/shard_map/ppermute | solution.py:45
  29.6 9.6 %collective-permute-start.7 = (f32[128,512]{1,0:T(8,128)S(1)}, f32[128,512]{1,0:T(8,128)S(1)}, u32[]{:S(2)}, u32[]{:S(2)}) collective-permute-start(f32[128,512]{1,0:T(8,128)S(1)} %collective-permute-done.5.refs_0_), channel_id=1, source_target_pairs={{1,0},{0,1},{3,2},{2,3},{5,4},{4,5},{7,6},{6,7},{9,8},{8,9},{11,10... | collective-permute-start | bytes 786440 | tf_op jit(solution)/shard_map/ppermute | solution.py:50
  30.9 8.4 %collective-permute-start.8 = (f32[128,512]{1,0:T(8,128)S(1)}, f32[128,512]{1,0:T(8,128)S(1)}, u32[]{:S(2)}, u32[]{:S(2)}) collective-permute-start(f32[128,512]{1,0:T(8,128)S(1)} %collective-permute-done.6.refs_1_), channel_id=1, source_target_pairs={{1,0},{0,1},{3,2},{2,3},{5,4},{4,5},{7,6},{6,7},{9,8},{8,9},{11,10... | collective-permute-start | bytes 786440 | tf_op jit(solution)/shard_map/ppermute | solution.py:50
  38.6 6.6 %collective-permute-start.10 = (f32[256,512]{1,0:T(8,128)S(1)}, f32[256,512]{1,0:T(8,128)S(1)}, u32[]{:S(2)}, u32[]{:S(2)}) collective-permute-start(f32[256,512]{1,0:T(8,128)S(1)} %get-tuple-element.92), channel_id=1, source_target_pairs={{1,0},{0,1},{3,2},{2,3},{5,4},{4,5},{7,6},{6,7},{9,8},{8,9},{11,10... | collective-permute-start | bytes 1572872 | tf_op jit(solution)/shard_map/ppermute | solution.py:50
  45.3 8.8 %collective-permute-start.11 = (f32[128,512]{1,0:T(8,128)S(1)}, f32[128,512]{1,0:T(8,128)S(1)}, u32[]{:S(2)}, u32[]{:S(2)}) collective-permute-start(f32[128,512]{1,0:T(8,128)S(1)} %get-tuple-element.93), channel_id=1, source_target_pairs={{0,4},{2,6},{4,0},{6,2},{8,12},{10,14},{12,8},{14,10},{16,20},{18,... | collective-permute-start | bytes 786440 | tf_op jit(solution)/shard_map/ppermute | solution.py:45
  46.1 8.2 %collective-permute-start.12 = (f32[128,512]{1,0:T(8,128)S(1)}, f32[128,512]{1,0:T(8,128)S(1)}, u32[]{:S(2)}, u32[]{:S(2)}) collective-permute-start(f32[128,512]{1,0:T(8,128)S(1)} %get-tuple-element.94), channel_id=1, source_target_pairs={{0,2},{2,0},{4,6},{6,4},{8,10},{10,8},{12,14},{14,12},{16,18},{18,... | collective-permute-start | bytes 786440 | tf_op jit(solution)/shard_map/ppermute | solution.py:45
  54.4 6.7 %collective-permute-start.14 = (f32[72,512]{1,0:T(8,128)S(1)}, f32[72,512]{1,0:T(8,128)S(1)}, u32[]{:S(2)}, u32[]{:S(2)}) collective-permute-start(f32[72,512]{1,0:T(8,128)S(1)} %get-tuple-element.97), channel_id=1, source_target_pairs={{0,2},{2,0},{4,6},{6,4},{8,10},{10,8},{12,14},{14,12},{16,18},{18,... | collective-permute-start | bytes 442376 | tf_op jit(solution)/shard_map/ppermute | solution.py:45
  61.2 10.1 %collective-permute-start.17 = (f32[72,512]{1,0:T(8,128)S(1)}, f32[72,512]{1,0:T(8,128)S(1)}, u32[]{:S(2)}, u32[]{:S(2)}) collective-permute-start(f32[72,512]{1,0:T(8,128)S(1)} %get-tuple-element.101.refs_0_), channel_id=1, source_target_pairs={{0,24},{2,26},{4,28},{6,30},{8,16},{10,18},{12,20},{14,22},{16,8},... | collective-permute-start | bytes 442376 | tf_op jit(solution)/shard_map/ppermute | solution.py:45
  64.9 8.1 %collective-permute-start.21 = (f32[32,512]{1,0:T(8,128)S(1)}, f32[32,512]{1,0:T(8,128)S(1)}, u32[]{:S(2)}, u32[]{:S(2)}) collective-permute-start(f32[32,512]{1,0:T(8,128)S(1)} %bitcast.6), channel_id=1, source_target_pairs={{0,8},{2,10},{4,12},{6,14},{8,0},{10,2},{12,4},{14,6},{16,24},{18,... | collective-permute-start | bytes 196616 | tf_op jit(solution)/shard_map/ppermute | solution.py:45
  71.3 10.1 %collective-permute-start.19 = (f32[72,512]{1,0:T(8,128)S(1)}, f32[72,512]{1,0:T(8,128)S(1)}, u32[]{:S(2)}, u32[]{:S(2)}) collective-permute-start(f32[72,512]{1,0:T(8,128)S(1)} %get-tuple-element.103.refs_0_), channel_id=1, source_target_pairs={{0,8},{2,10},{4,12},{6,14},{8,0},{10,2},{12,4},{14,6},{16,24},{18,... | collective-permute-start | bytes 442376 | tf_op jit(solution)/shard_map/ppermute | solution.py:45
  73.0 6.9 %collective-permute-start.22 = (f32[64,512]{1,0:T(8,128)S(1)}, f32[64,512]{1,0:T(8,128)S(1)}, u32[]{:S(2)}, u32[]{:S(2)}) collective-permute-start(f32[64,512]{1,0:T(8,128)S(1)} %shard_map.100.refs_0_), channel_id=1, source_target_pairs={{0,24},{2,26},{4,28},{6,30},{8,16},{10,18},{12,20},{14,22},{16,8},... | collective-permute-start | bytes 393224 | tf_op jit(solution)/shard_map/ppermute | solution.py:45
  73.3 8.1 %collective-permute-start.20 = (f32[64,512]{1,0:T(8,128)S(1)}, f32[64,512]{1,0:T(8,128)S(1)}, u32[]{:S(2)}, u32[]{:S(2)}) collective-permute-start(f32[64,512]{1,0:T(8,128)S(1)} %get-tuple-element.104.refs_2_), channel_id=1, source_target_pairs={{0,24},{2,26},{4,28},{6,30},{8,16},{10,18},{12,20},{14,22},{16,8},... | collective-permute-start | bytes 393224 | tf_op jit(solution)/shard_map/ppermute | solution.py:45
  88.0 9.3 %collective-permute-start.25 = (f32[256,512]{1,0:T(8,128)S(1)}, f32[256,512]{1,0:T(8,128)S(1)}, u32[]{:S(2)}, u32[]{:S(2)}) collective-permute-start(f32[256,512]{1,0:T(8,128)S(1)} %get-tuple-element.107.refs_0_.refs_6_), channel_id=1, source_target_pairs={{1,0},{0,1},{3,2},{2,3},{5,4},{4,5},{7,6},{6,7},{9,8},{8,9},{11,10... | collective-permute-start | bytes 1572872 | tf_op jit(solution)/shard_map/ppermute | solution.py:50
  88.1 8.7 %collective-permute-start.26 = (f32[128,512]{1,0:T(8,128)S(1)}, f32[128,512]{1,0:T(8,128)S(1)}, u32[]{:S(2)}, u32[]{:S(2)}) collective-permute-start(f32[128,512]{1,0:T(8,128)S(1)} %get-tuple-element.109), channel_id=1, source_target_pairs={{0,4},{2,6},{4,0},{6,2},{8,12},{10,14},{12,8},{14,10},{16,20},{18,... | collective-permute-start | bytes 786440 | tf_op jit(solution)/shard_map/ppermute | solution.py:45
  89.0 8.4 %collective-permute-start.27 = (f32[128,512]{1,0:T(8,128)S(1)}, f32[128,512]{1,0:T(8,128)S(1)}, u32[]{:S(2)}, u32[]{:S(2)}) collective-permute-start(f32[128,512]{1,0:T(8,128)S(1)} %get-tuple-element.110), channel_id=1, source_target_pairs={{0,2},{2,0},{4,6},{6,4},{8,10},{10,8},{12,14},{14,12},{16,18},{18,... | collective-permute-start | bytes 786440 | tf_op jit(solution)/shard_map/ppermute | solution.py:45
  96.8 9.1 %collective-permute-start.28 = (f32[128,512]{1,0:T(8,128)S(1)}, f32[128,512]{1,0:T(8,128)S(1)}, u32[]{:S(2)}, u32[]{:S(2)}) collective-permute-start(f32[128,512]{1,0:T(8,128)S(1)} %collective-permute-done.26.refs_0_), channel_id=1, source_target_pairs={{1,0},{0,1},{3,2},{2,3},{5,4},{4,5},{7,6},{6,7},{9,8},{8,9},{11,10... | collective-permute-start | bytes 786440 | tf_op jit(solution)/shard_map/ppermute | solution.py:50
  97.4 8.5 %collective-permute-start.29 = (f32[128,512]{1,0:T(8,128)S(1)}, f32[128,512]{1,0:T(8,128)S(1)}, u32[]{:S(2)}, u32[]{:S(2)}) collective-permute-start(f32[128,512]{1,0:T(8,128)S(1)} %collective-permute-done.27.refs_1_), channel_id=1, source_target_pairs={{1,0},{0,1},{3,2},{2,3},{5,4},{4,5},{7,6},{6,7},{9,8},{8,9},{11,10... | collective-permute-start | bytes 786440 | tf_op jit(solution)/shard_map/ppermute | solution.py:50
  105.4 6.6 %collective-permute-start.31 = (f32[256,512]{1,0:T(8,128)S(1)}, f32[256,512]{1,0:T(8,128)S(1)}, u32[]{:S(2)}, u32[]{:S(2)}) collective-permute-start(f32[256,512]{1,0:T(8,128)S(1)} %get-tuple-element.123), channel_id=1, source_target_pairs={{1,0},{0,1},{3,2},{2,3},{5,4},{4,5},{7,6},{6,7},{9,8},{8,9},{11,10... | collective-permute-start | bytes 1572872 | tf_op jit(solution)/shard_map/ppermute | solution.py:50
  112.0 8.8 %collective-permute-start.32 = (f32[128,512]{1,0:T(8,128)S(1)}, f32[128,512]{1,0:T(8,128)S(1)}, u32[]{:S(2)}, u32[]{:S(2)}) collective-permute-start(f32[128,512]{1,0:T(8,128)S(1)} %get-tuple-element.124), channel_id=1, source_target_pairs={{0,4},{2,6},{4,0},{6,2},{8,12},{10,14},{12,8},{14,10},{16,20},{18,... | collective-permute-start | bytes 786440 | tf_op jit(solution)/shard_map/ppermute | solution.py:45
  113.2 8.4 %collective-permute-start.33 = (f32[128,512]{1,0:T(8,128)S(1)}, f32[128,512]{1,0:T(8,128)S(1)}, u32[]{:S(2)}, u32[]{:S(2)}) collective-permute-start(f32[128,512]{1,0:T(8,128)S(1)} %get-tuple-element.125), channel_id=1, source_target_pairs={{0,2},{2,0},{4,6},{6,4},{8,10},{10,8},{12,14},{14,12},{16,18},{18,... | collective-permute-start | bytes 786440 | tf_op jit(solution)/shard_map/ppermute | solution.py:45
  127.8 7.1 %collective-permute-start.38 = (f32[72,512]{1,0:T(8,128)S(1)}, f32[72,512]{1,0:T(8,128)S(1)}, u32[]{:S(2)}, u32[]{:S(2)}) collective-permute-start(f32[72,512]{1,0:T(8,128)S(1)} %shard_map.111), channel_id=1, source_target_pairs={{0,24},{2,26},{4,28},{6,30},{8,16},{10,18},{12,20},{14,22},{16,8},... | collective-permute-start | bytes 442376 | tf_op jit(solution)/shard_map/ppermute | solution.py:45
  (20 other events, 137.0 us)

commit v7 on v6

--- a/solution.py
+++ b/solution.py
@@ -188,9 +188,9 @@
     )(me, left_ops, right_ops, block)
 
 
-def double(block, masks):
-    for mask in masks:
-        more = swap(block, mask)
+def double(block, masks, first=None):
+    for step, mask in enumerate(masks):
+        more = swap(first if step == 0 and first is not None else block, mask)
         rows, m = block.shape[0] // 2, block.shape[1]
 
         def meet_column(inputs, outs, scratch):
@@ -405,10 +405,11 @@
     def load(inputs, outs, scratch):
         outs[0][...] = inputs[0][0][...]
 
+    source = vector
     (vector,) = kernel_call(load, [array(2 * rows, m)], [vector])
     table = tabulate(charges, coupling)
     *ops, edge = prepare(me, left_ops, right_ops, vector, count)
-    column = double(vector, deep)
+    column = double(vector, deep, source)
     divisor = double(divisor, deep)
 
     def part(inputs, outs, scratch):

time: 141 us -> 140 us (level)
  no operation moved by 1% of the time
where the time goes in v7:
time: 140 us
  waiting for transfers between devices  59 us (42%)
  starting transfers between devices  44.4 us (32%)
  Pallas kernels  34.9 us (25%)
    ppermute x28, waiting for transfers between devices, swap(): lax.ppermute(block, 'pair', [(i, i ^ mask) for i in range(lax.axis_size('...  56.6 us
    ppermute x28, starting transfers between devices, swap(): lax.ppermute(block, 'pair', [(i, i ^ mask) for i in range(lax.axis_size('...  42.9 us
    pallas_call x29, Pallas kernels, kernel_call(): pl.pallas_call(kernel, in_specs=[pl.BlockSpec(memory_space=pltpu.VMEM)] *...  29 us
    pallas_call x1, Pallas kernels, prepare(): pl.pallas_call(kernel, grid_spec=pltpu.PrefetchScalarGridSpec(num_scalar_...  5.33 us
  transfers between devices with their start and end apart: 40, of which 23 were waited for; matrix products, arithmetic and copies ran while one was open for 0% of the time, Pallas kernels for 24%

profile of v7, /device:TPU:0, one launch (start us, length us, event | category | flops | bytes accessed | tf_op | source)
XLA Modules:
  0.0 140.2 jit_solution(1099950402362262320)
XLA Ops:
  0.7 3.1 %collective-permute-start = (f32[32,512]{1,0:T(8,128)}, f32[32,512]{1,0:T(8,128)S(1)}, u32[]{:S(2)}, u32[]{:S(2)}) collective-permute-start(f32[32,512]{1,0:T(8,128)} %bitcast.5), channel_id=1, source_target_pairs={{0,8},{2,10},{4,12},{6,14},{8,0},{10,2},{12,4},{14,6},{16,24},{18,... | collective-permute-start | bytes 196616 | tf_op jit(solution)/shard_map/ppermute | solution.py:45
  6.2 4.1 %collective-permute-start.1 = (f32[64,512]{1,0:T(8,128)S(1)}, f32[64,512]{1,0:T(8,128)S(1)}, u32[]{:S(2)}, u32[]{:S(2)}) collective-permute-start(f32[64,512]{1,0:T(8,128)S(1)} %shard_map.86.refs_0_), channel_id=1, source_target_pairs={{0,24},{2,26},{4,28},{6,30},{8,16},{10,18},{12,20},{14,22},{16,8},... | collective-permute-start | bytes 393224 | tf_op jit(solution)/shard_map/ppermute | solution.py:45
  10.3 3.1 %collective-permute-done.1.refs_1_ = f32[64,512]{1,0:T(8,128)S(1)} collective-permute-done((f32[64,512]{1,0:T(8,128)S(1)}, f32[64,512]{1,0:T(8,128)S(1)}, u32[]{:S(2)}, u32[]{:S(2)}) %collective-permute-start.1) | collective-permute-done | bytes 131104 | tf_op jit(solution)/shard_map/ppermute | solution.py:45
  23.0 5.3 %shard_map.90 = (bf16[3,2,512,512]{3,2,1,0:T(8,128)(2,1)S(1)}, bf16[3,2,512,512]{3,2,1,0:T(8,128)(2,1)S(1)}, bf16[3,2,512,512]{3,2,1,0:T(8,128)(2,1)S(1)}, bf16[...) custom-call(s32[1]{0:T(128)} %bitcast.1.me_ref, f32[3,1,512,512]{3,2,1,0:T(8,128)} %left_ref.1, f32[3,1,512,512]{3,2,1,0:T(8,128)} %right_ref.1, ...), custom_call_target="tpu_custom_call" | custom-call | flops 1179648000 | bytes 18874368 | tf_op jit(solution)/shard_map/pallas_call | solution.py:176
  30.3 5.1 %shard_map.92 = (bf16[3,2,256,512]{3,2,1,0:T(8,128)(2,1)S(1)}, bf16[3,2,256,512]{3,2,1,0:T(8,128)(2,1)S(1)}, f32[256,512]{1,0:T(8,128)S(1)}, f32[256,512]{1,0:T(8,128)S(1)}, f32[256,512]{1,0:T(8,128)S(1)}) custom-call(f32[256,512]{1,0:T(8,128)S(1)} %get-tuple-element.72.refs_0_.refs_6_, f32[256,512]{1,0:T(8,128)S(1)} %collective-permute-done.4.refs_1_, ...), custom_call_target="tpu_custom_call" | custom-call | flops 3623878656 | bytes 13635584 | tf_op jit(solution)/shard_map/pallas_call | solution.py:85
  35.4 2.7 %shard_map.93 = (bf16[3,2,256,512]{3,2,1,0:T(8,128)(2,1)S(1)}, f32[256,512]{1,0:T(8,128)S(1)}, f32[256,512]{1,0:T(8,128)S(1)}) custom-call(f32[128,512]{1,0:T(8,128)S(1)} %collective-permute-done.5.refs_0_, f32[128,512]{1,0:T(8,128)S(1)} %collective-permute-done.6.refs_1_, f32[256,512]{1,0:T(8,128)S(1)} %get-tuple-element.80.refs_2_, ...), custom_call_target="tpu_custom_call" | custom-call | flops 2415919104 | bytes 7868416 | tf_op jit(solution)/shard_map/pallas_call | solution.py:85
  38.7 3.0 %shard_map.94 = (bf16[3,2,256,512]{3,2,1,0:T(8,128)(2,1)S(1)}, f32[256,512]{1,0:T(8,128)S(1)}, f32[8,512]{1,0:T(8,128)S(1)}) custom-call(f32[128,512]{1,0:T(8,128)S(1)} %collective-permute-done.5.refs_0_, f32[128,512]{1,0:T(8,128)S(1)} %collective-permute-done.6.refs_1_, f32[128,512]{1,0:T(8,128)S(1)} %collective-permute-done.7.refs_2_, ...), custom_call_target="tpu_custom_call" | custom-call | flops 2415919104 | bytes 8392704 | tf_op jit(solution)/shard_map/pallas_call | solution.py:85
  41.7 2.9 %shard_map.95 = (f32[256,512]{1,0:T(8,128)S(1)}, f32[8,512]{1,0:T(8,128)S(1)}, f32[256,512]{1,0:T(8,128)S(1)}) custom-call(bf16[3,2,256,512]{3,2,1,0:T(8,128)(2,1)S(1)} %get-tuple-element.77.refs_0_, bf16[3,2,256,512]{3,2,1,0:T(8,128)(2,1)S(1)} %get-tuple-element.82.refs_1_, bf16[3,2,256,512]{3,2,1,0:T(8,128)(2,1)S(1)} %get-tuple-element.83.refs_2_, ...), custom_call_target="tpu_custom_call" | custom-call | flops 2415919104 | bytes 13144064 | tf_op jit(solution)/shard_map/pallas_call | solution.py:85
  47.3 6.2 %collective-permute-done.11.refs_2_ = f32[128,512]{1,0:T(8,128)S(1)} collective-permute-done((f32[128,512]{1,0:T(8,128)S(1)}, f32[128,512]{1,0:T(8,128)S(1)}, u32[]{:S(2)}, u32[]{:S(2)}) %collective-permute-start.11) | collective-permute-done | bytes 262176 | tf_op jit(solution)/shard_map/ppermute | solution.py:45
  57.3 3.2 %collective-permute-done.16.refs_5_ = f32[8,512]{1,0:T(8,128)S(1)} collective-permute-done((f32[8,512]{1,0:T(8,128)S(1)}, f32[8,512]{1,0:T(8,128)S(1)}, u32[]{:S(2)}, u32[]{:S(2)}) %collective-permute-start.16) | collective-permute-done | bytes 16416 | tf_op jit(solution)/shard_map/ppermute | solution.py:45
  60.6 3.7 %collective-permute-start.17 = (f32[72,512]{1,0:T(8,128)S(1)}, f32[72,512]{1,0:T(8,128)S(1)}, u32[]{:S(2)}, u32[]{:S(2)}) collective-permute-start(f32[72,512]{1,0:T(8,128)S(1)} %get-tuple-element.101.refs_0_), channel_id=1, source_target_pairs={{0,24},{2,26},{4,28},{6,30},{8,16},{10,18},{12,20},{14,22},{16,8},... | collective-permute-start | bytes 442376 | tf_op jit(solution)/shard_map/ppermute | solution.py:45
  66.3 4.4 %collective-permute-done.18.refs_3_ = f32[64,512]{1,0:T(8,128)S(1)} collective-permute-done((f32[64,512]{1,0:T(8,128)S(1)}, f32[64,512]{1,0:T(8,128)S(1)}, u32[]{:S(2)}, u32[]{:S(2)}) %collective-permute-start.18) | collective-permute-done | bytes 131104 | tf_op jit(solution)/shard_map/ppermute | solution.py:45
  72.7 3.6 %collective-permute-start.20 = (f32[64,512]{1,0:T(8,128)S(1)}, f32[64,512]{1,0:T(8,128)S(1)}, u32[]{:S(2)}, u32[]{:S(2)}) collective-permute-start(f32[64,512]{1,0:T(8,128)S(1)} %get-tuple-element.104.refs_2_), channel_id=1, source_target_pairs={{0,24},{2,26},{4,28},{6,30},{8,16},{10,18},{12,20},{14,22},{16,8},... | collective-permute-start | bytes 393224 | tf_op jit(solution)/shard_map/ppermute | solution.py:45
  76.3 3.0 %collective-permute-done.22.refs_1_ = f32[64,512]{1,0:T(8,128)S(1)} collective-permute-done((f32[64,512]{1,0:T(8,128)S(1)}, f32[64,512]{1,0:T(8,128)S(1)}, u32[]{:S(2)}, u32[]{:S(2)}) %collective-permute-start.22) | collective-permute-done | bytes 131104 | tf_op jit(solution)/shard_map/ppermute | solution.py:45
  83.2 2.8 %collective-permute-done.23.refs_1_ = f32[64,512]{1,0:T(8,128)S(1)} collective-permute-done((f32[64,512]{1,0:T(8,128)S(1)}, f32[64,512]{1,0:T(8,128)S(1)}, u32[]{:S(2)}, u32[]{:S(2)}) %collective-permute-start.23) | collective-permute-done | bytes 131104 | tf_op jit(solution)/shard_map/ppermute | solution.py:45
  88.9 7.3 %collective-permute-done.26.refs_0_ = f32[128,512]{1,0:T(8,128)S(1)} collective-permute-done((f32[128,512]{1,0:T(8,128)S(1)}, f32[128,512]{1,0:T(8,128)S(1)}, u32[]{:S(2)}, u32[]{:S(2)}) %collective-permute-start.26) | collective-permute-done | bytes 262176 | tf_op jit(solution)/shard_map/ppermute | solution.py:45
  96.8 5.3 %shard_map.104 = (bf16[3,2,256,512]{3,2,1,0:T(8,128)(2,1)S(1)}, bf16[3,2,256,512]{3,2,1,0:T(8,128)(2,1)S(1)}, f32[256,512]{1,0:T(8,128)S(1)}, f32[256,512]{1,0:T(8,128)S(1)}, f32[256,512]{1,0:T(8,128)S(1)}) custom-call(f32[256,512]{1,0:T(8,128)S(1)} %get-tuple-element.107.refs_0_.refs_6_, f32[256,512]{1,0:T(8,128)S(1)} %collective-permute-done.25.refs_1_, ...), custom_call_target="tpu_custom_call" | custom-call | flops 3623878656 | bytes 13635584 | tf_op jit(solution)/shard_map/pallas_call | solution.py:85
  102.1 2.7 %shard_map.105 = (bf16[3,2,256,512]{3,2,1,0:T(8,128)(2,1)S(1)}, f32[256,512]{1,0:T(8,128)S(1)}, f32[256,512]{1,0:T(8,128)S(1)}) custom-call(f32[128,512]{1,0:T(8,128)S(1)} %collective-permute-done.26.refs_0_, f32[128,512]{1,0:T(8,128)S(1)} %collective-permute-done.27.refs_1_, f32[256,512]{1,0:T(8,128)S(1)} %get-tuple-element.111.refs_2_, ...), custom_call_target="tpu_custom_call" | custom-call | flops 2415919104 | bytes 7868416 | tf_op jit(solution)/shard_map/pallas_call | solution.py:85
  105.3 3.0 %shard_map.106 = (bf16[3,2,256,512]{3,2,1,0:T(8,128)(2,1)S(1)}, f32[256,512]{1,0:T(8,128)S(1)}, f32[8,512]{1,0:T(8,128)S(1)}) custom-call(f32[128,512]{1,0:T(8,128)S(1)} %collective-permute-done.26.refs_0_, f32[128,512]{1,0:T(8,128)S(1)} %collective-permute-done.27.refs_1_, f32[128,512]{1,0:T(8,128)S(1)} %collective-permute-done.28.refs_2_, ...), custom_call_target="tpu_custom_call" | custom-call | flops 2415919104 | bytes 8392704 | tf_op jit(solution)/shard_map/pallas_call | solution.py:85
  108.3 2.9 %shard_map.107 = (f32[256,512]{1,0:T(8,128)S(1)}, f32[8,512]{1,0:T(8,128)S(1)}, f32[256,512]{1,0:T(8,128)S(1)}) custom-call(bf16[3,2,256,512]{3,2,1,0:T(8,128)(2,1)S(1)} %get-tuple-element.108.refs_0_, bf16[3,2,256,512]{3,2,1,0:T(8,128)(2,1)S(1)} %get-tuple-element.113.refs_1_, bf16[3,2,256,512]{3,2,1,0:T(8,128)(2,1)S(1)} %get-tuple-element.114.refs_2_, ...), custom_call_target="tpu_custom_call" | custom-call | flops 2415919104 | bytes 13144064 | tf_op jit(solution)/shard_map/pallas_call | solution.py:85
  114.5 5.6 %collective-permute-done.32.refs_2_ = f32[128,512]{1,0:T(8,128)S(1)} collective-permute-done((f32[128,512]{1,0:T(8,128)S(1)}, f32[128,512]{1,0:T(8,128)S(1)}, u32[]{:S(2)}, u32[]{:S(2)}) %collective-permute-start.32) | collective-permute-done | bytes 262176 | tf_op jit(solution)/shard_map/ppermute | solution.py:45
  127.3 2.5 %collective-permute-start.38 = (f32[72,512]{1,0:T(8,128)S(1)}, f32[72,512]{1,0:T(8,128)S(1)}, u32[]{:S(2)}, u32[]{:S(2)}) collective-permute-start(f32[72,512]{1,0:T(8,128)S(1)} %shard_map.111), channel_id=1, source_target_pairs={{0,24},{2,26},{4,28},{6,30},{8,16},{10,18},{12,20},{14,22},{16,8},... | collective-permute-start | bytes 442376 | tf_op jit(solution)/shard_map/ppermute | solution.py:45
  129.7 4.6 %collective-permute-done.38.refs_1_ = f32[72,512]{1,0:T(8,128)S(1)} collective-permute-done((f32[72,512]{1,0:T(8,128)S(1)}, f32[72,512]{1,0:T(8,128)S(1)}, u32[]{:S(2)}, u32[]{:S(2)}) %collective-permute-start.38) | collective-permute-done | bytes 147488 | tf_op jit(solution)/shard_map/ppermute | solution.py:45
  134.4 2.5 %collective-permute-start.39 = (f32[40,512]{1,0:T(8,128)S(1)}, f32[40,512]{1,0:T(8,128)S(1)}, u32[]{:S(2)}, u32[]{:S(2)}) collective-permute-start(f32[40,512]{1,0:T(8,128)S(1)} %shard_map.113), channel_id=1, source_target_pairs={{0,8},{2,10},{4,12},{6,14},{8,0},{10,2},{12,4},{14,6},{16,24},{18,... | collective-permute-start | bytes 245768 | tf_op jit(solution)/shard_map/ppermute | solution.py:45
  (95 shorter events, 46.6 us)
Async XLA Ops:
  6.2 7.2 %collective-permute-start.1 = (f32[64,512]{1,0:T(8,128)S(1)}, f32[64,512]{1,0:T(8,128)S(1)}, u32[]{:S(2)}, u32[]{:S(2)}) collective-permute-start(f32[64,512]{1,0:T(8,128)S(1)} %shard_map.86.refs_0_), channel_id=1, source_target_pairs={{0,24},{2,26},{4,28},{6,30},{8,16},{10,18},{12,20},{14,22},{16,8},... | collective-permute-start | bytes 393224 | tf_op jit(solution)/shard_map/ppermute | solution.py:45
  20.3 10.0 %collective-permute-start.4 = (f32[256,512]{1,0:T(8,128)S(1)}, f32[256,512]{1,0:T(8,128)S(1)}, u32[]{:S(2)}, u32[]{:S(2)}) collective-permute-start(f32[256,512]{1,0:T(8,128)S(1)} %get-tuple-element.72.refs_0_.refs_6_), channel_id=1, source_target_pairs={{1,0},{0,1},{3,2},{2,3},{5,4},{4,5},{7,6},{6,7},{9,8},{8,9},{11,10... | collective-permute-start | bytes 1572872 | tf_op jit(solution)/shard_map/ppermute | solution.py:50
  20.3 8.7 %collective-permute-start.5 = (f32[128,512]{1,0:T(8,128)S(1)}, f32[128,512]{1,0:T(8,128)S(1)}, u32[]{:S(2)}, u32[]{:S(2)}) collective-permute-start(f32[128,512]{1,0:T(8,128)S(1)} %get-tuple-element.78), channel_id=1, source_target_pairs={{0,4},{2,6},{4,0},{6,2},{8,12},{10,14},{12,8},{14,10},{16,20},{18,... | collective-permute-start | bytes 786440 | tf_op jit(solution)/shard_map/ppermute | solution.py:45
  21.9 8.4 %collective-permute-start.6 = (f32[128,512]{1,0:T(8,128)S(1)}, f32[128,512]{1,0:T(8,128)S(1)}, u32[]{:S(2)}, u32[]{:S(2)}) collective-permute-start(f32[128,512]{1,0:T(8,128)S(1)} %get-tuple-element.79), channel_id=1, source_target_pairs={{0,2},{2,0},{4,6},{6,4},{8,10},{10,8},{12,14},{14,12},{16,18},{18,... | collective-permute-start | bytes 786440 | tf_op jit(solution)/shard_map/ppermute | solution.py:45
  29.0 9.6 %collective-permute-start.7 = (f32[128,512]{1,0:T(8,128)S(1)}, f32[128,512]{1,0:T(8,128)S(1)}, u32[]{:S(2)}, u32[]{:S(2)}) collective-permute-start(f32[128,512]{1,0:T(8,128)S(1)} %collective-permute-done.5.refs_0_), channel_id=1, source_target_pairs={{1,0},{0,1},{3,2},{2,3},{5,4},{4,5},{7,6},{6,7},{9,8},{8,9},{11,10... | collective-permute-start | bytes 786440 | tf_op jit(solution)/shard_map/ppermute | solution.py:50
  30.3 8.4 %collective-permute-start.8 = (f32[128,512]{1,0:T(8,128)S(1)}, f32[128,512]{1,0:T(8,128)S(1)}, u32[]{:S(2)}, u32[]{:S(2)}) collective-permute-start(f32[128,512]{1,0:T(8,128)S(1)} %collective-permute-done.6.refs_1_), channel_id=1, source_target_pairs={{1,0},{0,1},{3,2},{2,3},{5,4},{4,5},{7,6},{6,7},{9,8},{8,9},{11,10... | collective-permute-start | bytes 786440 | tf_op jit(solution)/shard_map/ppermute | solution.py:50
  38.0 6.6 %collective-permute-start.10 = (f32[256,512]{1,0:T(8,128)S(1)}, f32[256,512]{1,0:T(8,128)S(1)}, u32[]{:S(2)}, u32[]{:S(2)}) collective-permute-start(f32[256,512]{1,0:T(8,128)S(1)} %get-tuple-element.92), channel_id=1, source_target_pairs={{1,0},{0,1},{3,2},{2,3},{5,4},{4,5},{7,6},{6,7},{9,8},{8,9},{11,10... | collective-permute-start | bytes 1572872 | tf_op jit(solution)/shard_map/ppermute | solution.py:50
  44.8 8.8 %collective-permute-start.11 = (f32[128,512]{1,0:T(8,128)S(1)}, f32[128,512]{1,0:T(8,128)S(1)}, u32[]{:S(2)}, u32[]{:S(2)}) collective-permute-start(f32[128,512]{1,0:T(8,128)S(1)} %get-tuple-element.93), channel_id=1, source_target_pairs={{0,4},{2,6},{4,0},{6,2},{8,12},{10,14},{12,8},{14,10},{16,20},{18,... | collective-permute-start | bytes 786440 | tf_op jit(solution)/shard_map/ppermute | solution.py:45
  45.6 8.1 %collective-permute-start.12 = (f32[128,512]{1,0:T(8,128)S(1)}, f32[128,512]{1,0:T(8,128)S(1)}, u32[]{:S(2)}, u32[]{:S(2)}) collective-permute-start(f32[128,512]{1,0:T(8,128)S(1)} %get-tuple-element.94), channel_id=1, source_target_pairs={{0,2},{2,0},{4,6},{6,4},{8,10},{10,8},{12,14},{14,12},{16,18},{18,... | collective-permute-start | bytes 786440 | tf_op jit(solution)/shard_map/ppermute | solution.py:45
  53.8 6.8 %collective-permute-start.14 = (f32[72,512]{1,0:T(8,128)S(1)}, f32[72,512]{1,0:T(8,128)S(1)}, u32[]{:S(2)}, u32[]{:S(2)}) collective-permute-start(f32[72,512]{1,0:T(8,128)S(1)} %get-tuple-element.97), channel_id=1, source_target_pairs={{0,2},{2,0},{4,6},{6,4},{8,10},{10,8},{12,14},{14,12},{16,18},{18,... | collective-permute-start | bytes 442376 | tf_op jit(solution)/shard_map/ppermute | solution.py:45
  60.6 10.1 %collective-permute-start.17 = (f32[72,512]{1,0:T(8,128)S(1)}, f32[72,512]{1,0:T(8,128)S(1)}, u32[]{:S(2)}, u32[]{:S(2)}) collective-permute-start(f32[72,512]{1,0:T(8,128)S(1)} %get-tuple-element.101.refs_0_), channel_id=1, source_target_pairs={{0,24},{2,26},{4,28},{6,30},{8,16},{10,18},{12,20},{14,22},{16,8},... | collective-permute-start | bytes 442376 | tf_op jit(solution)/shard_map/ppermute | solution.py:45
  64.4 8.1 %collective-permute-start.21 = (f32[32,512]{1,0:T(8,128)S(1)}, f32[32,512]{1,0:T(8,128)S(1)}, u32[]{:S(2)}, u32[]{:S(2)}) collective-permute-start(f32[32,512]{1,0:T(8,128)S(1)} %bitcast.7), channel_id=1, source_target_pairs={{0,8},{2,10},{4,12},{6,14},{8,0},{10,2},{12,4},{14,6},{16,24},{18,... | collective-permute-start | bytes 196616 | tf_op jit(solution)/shard_map/ppermute | solution.py:45
  70.7 10.1 %collective-permute-start.19 = (f32[72,512]{1,0:T(8,128)S(1)}, f32[72,512]{1,0:T(8,128)S(1)}, u32[]{:S(2)}, u32[]{:S(2)}) collective-permute-start(f32[72,512]{1,0:T(8,128)S(1)} %get-tuple-element.103.refs_0_), channel_id=1, source_target_pairs={{0,8},{2,10},{4,12},{6,14},{8,0},{10,2},{12,4},{14,6},{16,24},{18,... | collective-permute-start | bytes 442376 | tf_op jit(solution)/shard_map/ppermute | solution.py:45
  72.5 6.9 %collective-permute-start.22 = (f32[64,512]{1,0:T(8,128)S(1)}, f32[64,512]{1,0:T(8,128)S(1)}, u32[]{:S(2)}, u32[]{:S(2)}) collective-permute-start(f32[64,512]{1,0:T(8,128)S(1)} %shard_map.100.refs_0_), channel_id=1, source_target_pairs={{0,24},{2,26},{4,28},{6,30},{8,16},{10,18},{12,20},{14,22},{16,8},... | collective-permute-start | bytes 393224 | tf_op jit(solution)/shard_map/ppermute | solution.py:45
  72.7 8.1 %collective-permute-start.20 = (f32[64,512]{1,0:T(8,128)S(1)}, f32[64,512]{1,0:T(8,128)S(1)}, u32[]{:S(2)}, u32[]{:S(2)}) collective-permute-start(f32[64,512]{1,0:T(8,128)S(1)} %get-tuple-element.104.refs_2_), channel_id=1, source_target_pairs={{0,24},{2,26},{4,28},{6,30},{8,16},{10,18},{12,20},{14,22},{16,8},... | collective-permute-start | bytes 393224 | tf_op jit(solution)/shard_map/ppermute | solution.py:45
  87.5 9.3 %collective-permute-start.25 = (f32[256,512]{1,0:T(8,128)S(1)}, f32[256,512]{1,0:T(8,128)S(1)}, u32[]{:S(2)}, u32[]{:S(2)}) collective-permute-start(f32[256,512]{1,0:T(8,128)S(1)} %get-tuple-element.107.refs_0_.refs_6_), channel_id=1, source_target_pairs={{1,0},{0,1},{3,2},{2,3},{5,4},{4,5},{7,6},{6,7},{9,8},{8,9},{11,10... | collective-permute-start | bytes 1572872 | tf_op jit(solution)/shard_map/ppermute | solution.py:50
  87.6 8.7 %collective-permute-start.26 = (f32[128,512]{1,0:T(8,128)S(1)}, f32[128,512]{1,0:T(8,128)S(1)}, u32[]{:S(2)}, u32[]{:S(2)}) collective-permute-start(f32[128,512]{1,0:T(8,128)S(1)} %get-tuple-element.109), channel_id=1, source_target_pairs={{0,4},{2,6},{4,0},{6,2},{8,12},{10,14},{12,8},{14,10},{16,20},{18,... | collective-permute-start | bytes 786440 | tf_op jit(solution)/shard_map/ppermute | solution.py:45
  88.4 8.4 %collective-permute-start.27 = (f32[128,512]{1,0:T(8,128)S(1)}, f32[128,512]{1,0:T(8,128)S(1)}, u32[]{:S(2)}, u32[]{:S(2)}) collective-permute-start(f32[128,512]{1,0:T(8,128)S(1)} %get-tuple-element.110), channel_id=1, source_target_pairs={{0,2},{2,0},{4,6},{6,4},{8,10},{10,8},{12,14},{14,12},{16,18},{18,... | collective-permute-start | bytes 786440 | tf_op jit(solution)/shard_map/ppermute | solution.py:45
  96.3 9.0 %collective-permute-start.28 = (f32[128,512]{1,0:T(8,128)S(1)}, f32[128,512]{1,0:T(8,128)S(1)}, u32[]{:S(2)}, u32[]{:S(2)}) collective-permute-start(f32[128,512]{1,0:T(8,128)S(1)} %collective-permute-done.26.refs_0_), channel_id=1, source_target_pairs={{1,0},{0,1},{3,2},{2,3},{5,4},{4,5},{7,6},{6,7},{9,8},{8,9},{11,10... | collective-permute-start | bytes 786440 | tf_op jit(solution)/shard_map/ppermute | solution.py:50
  96.8 8.5 %collective-permute-start.29 = (f32[128,512]{1,0:T(8,128)S(1)}, f32[128,512]{1,0:T(8,128)S(1)}, u32[]{:S(2)}, u32[]{:S(2)}) collective-permute-start(f32[128,512]{1,0:T(8,128)S(1)} %collective-permute-done.27.refs_1_), channel_id=1, source_target_pairs={{1,0},{0,1},{3,2},{2,3},{5,4},{4,5},{7,6},{6,7},{9,8},{8,9},{11,10... | collective-permute-start | bytes 786440 | tf_op jit(solution)/shard_map/ppermute | solution.py:50
  104.8 6.5 %collective-permute-start.31 = (f32[256,512]{1,0:T(8,128)S(1)}, f32[256,512]{1,0:T(8,128)S(1)}, u32[]{:S(2)}, u32[]{:S(2)}) collective-permute-start(f32[256,512]{1,0:T(8,128)S(1)} %get-tuple-element.123), channel_id=1, source_target_pairs={{1,0},{0,1},{3,2},{2,3},{5,4},{4,5},{7,6},{6,7},{9,8},{8,9},{11,10... | collective-permute-start | bytes 1572872 | tf_op jit(solution)/shard_map/ppermute | solution.py:50
  111.4 8.7 %collective-permute-start.32 = (f32[128,512]{1,0:T(8,128)S(1)}, f32[128,512]{1,0:T(8,128)S(1)}, u32[]{:S(2)}, u32[]{:S(2)}) collective-permute-start(f32[128,512]{1,0:T(8,128)S(1)} %get-tuple-element.124), channel_id=1, source_target_pairs={{0,4},{2,6},{4,0},{6,2},{8,12},{10,14},{12,8},{14,10},{16,20},{18,... | collective-permute-start | bytes 786440 | tf_op jit(solution)/shard_map/ppermute | solution.py:45
  112.7 8.4 %collective-permute-start.33 = (f32[128,512]{1,0:T(8,128)S(1)}, f32[128,512]{1,0:T(8,128)S(1)}, u32[]{:S(2)}, u32[]{:S(2)}) collective-permute-start(f32[128,512]{1,0:T(8,128)S(1)} %get-tuple-element.125), channel_id=1, source_target_pairs={{0,2},{2,0},{4,6},{6,4},{8,10},{10,8},{12,14},{14,12},{16,18},{18,... | collective-permute-start | bytes 786440 | tf_op jit(solution)/shard_map/ppermute | solution.py:45
  127.3 7.1 %collective-permute-start.38 = (f32[72,512]{1,0:T(8,128)S(1)}, f32[72,512]{1,0:T(8,128)S(1)}, u32[]{:S(2)}, u32[]{:S(2)}) collective-permute-start(f32[72,512]{1,0:T(8,128)S(1)} %shard_map.111), channel_id=1, source_target_pairs={{0,24},{2,26},{4,28},{6,30},{8,16},{10,18},{12,20},{14,22},{16,8},... | collective-permute-start | bytes 442376 | tf_op jit(solution)/shard_map/ppermute | solution.py:45
  (20 other events, 136.4 us)
